TPU v7x, 8 devices: a whole 2x2x1 slice. The times are simulated.
8 devices in a mesh: tp: 4 (over z, y, x), dp: 2 (over core).
Axes of the slice: x: 2, y: 2, z: 1, core: 2. Of those that a mesh axis runs over, the one named last changes fastest.
Arguments:
- x: bfloat16 [6144, 5120], P(('dp', 'tp'))
- w_gate: bfloat16 [5120, 13824], P('dp', 'tp')
- w_up: bfloat16 [5120, 13824], P('dp', 'tp')
- w_down: bfloat16 [13824, 5120], P('tp', 'dp')
- dy: bfloat16 [6144, 5120], P(('dp', 'tp'))
Outputs:
- output 1: bfloat16 [6144, 5120], P(('dp', 'tp'))
- output 2: bfloat16 [6144, 5120], P(('dp', 'tp'))
- output 3: float32 [5120, 13824], P('dp', 'tp')
- output 4: float32 [5120, 13824], P('dp', 'tp')
- output 5: float32 [13824, 5120], P('tp', 'dp')
All inputs are finite; a program needn't handle non-finite values.
Results may differ from a plain program's by a relative error of at most 0.00119.
Values are sent between devices in bfloat16 or wider.
A program may use at most 1 GiB of HBM per device.

v0:
```python
import jax
import jax.numpy as jnp
from jax import lax
from jax.sharding import PartitionSpec as P


def solution(mesh):
    nx = mesh.shape["dp"]
    ny = mesh.shape["tp"]
    rows = P(("dp", "tp"), None)
    wsp = P("dp", "tp")
    dsp = P("tp", "dp")
    f32 = jnp.float32
    bf = jnp.bfloat16

    def to_columns(v):
        tl = v.shape[0]
        dl = v.shape[1] // nx
        vr = v.reshape(tl, nx, dl).transpose(1, 0, 2)
        return lax.all_to_all(vr, "dp", 0, 0, tiled=True)

    def from_columns(v):
        tl = v.shape[1]
        dl = v.shape[2]
        vr = lax.all_to_all(v, "dp", 0, 0, tiled=True)
        return vr.transpose(1, 0, 2).reshape(tl, nx * dl)

    def all_tokens(va):
        vg = lax.all_gather(va, "tp", axis=0, tiled=False)
        tl = vg.shape[2]
        dl = vg.shape[3]
        return vg.transpose(1, 0, 2, 3).reshape(nx * ny * tl, dl)

    def combine_tp(q, res):
        dl = q.shape[1]
        tl = q.shape[0] // (nx * ny)
        qs = lax.psum_scatter(q.reshape(nx, ny, tl, dl), "tp", scatter_dimension=1, tiled=True)
        out = res.astype(f32) + qs.reshape(nx, tl, dl)
        return from_columns(out.astype(bf))

    def local(x, w_gate, w_up, w_down, dy):
        fl = w_gate.shape[1]
        w = jnp.concatenate([w_gate, w_up], axis=1)
        xa = to_columns(x)
        xt = all_tokens(xa)
        p = lax.psum_scatter(jnp.dot(xt, w, preferred_element_type=f32), "dp", scatter_dimension=0, tiled=True)
        a = p[:, :fl]
        b = p[:, fl:]
        sig = jax.nn.sigmoid(a)
        sa = a * sig
        h = (sa * b).astype(bf)
        hg = lax.all_gather(h, "dp", axis=0, tiled=True)
        y = combine_tp(jnp.dot(hg, w_down, preferred_element_type=f32), xa)
        dya = to_columns(dy)
        dyt = all_tokens(dya)
        g = lax.psum_scatter(jnp.dot(dyt, w_down.T, preferred_element_type=f32), "dp", scatter_dimension=0, tiled=True)
        da = (g * b * sig * (1.0 + a * (1.0 - sig))).astype(bf)
        db = (g * sa).astype(bf)
        dab = lax.all_gather(jnp.concatenate([da, db], axis=1), "dp", axis=0, tiled=True)
        dx = combine_tp(jnp.dot(dab, w.T, preferred_element_type=f32), dya)
        dw = jnp.dot(xt.T, dab, preferred_element_type=f32)
        dw_down = jnp.dot(hg.T, dyt, preferred_element_type=f32)
        return y, dx, dw[:, :fl], dw[:, fl:], dw_down

    return jax.shard_map(local, mesh=mesh, in_specs=(rows, wsp, wsp, dsp, rows), out_specs=(rows, rows, wsp, wsp, dsp), check_vma=False)
```

profile of v0, /device:TPU:0, one launch (start us, length us, event | category | flops | bytes accessed | tf_op | source)
XLA Modules:
  0.0 2429.9 jit_solution(10681376166706106406)
XLA Ops:
  7.2 10.6 copy.48
  17.8 18.1 all_to_all.20
  35.9 10.6 copy.49
  46.6 11.2 copy.44
  57.8 18.2 all_to_all.21
  76.0 10.6 copy.45
  86.7 236.6 %all-gather.13.cloned.1.call-done = bf16[8,768,2560]{2,1,0:T(8,128)(2,1)} async-done(((bf16[2,768,2560]{2,1,0:T(8,128)(2,1)}), bf16[8,768,2560]{2,1,0:T(8,128)(2,1)}) %all-gather.13.cloned.1.call-update) | async-done | bytes 31457296 | tf_op jit(solution)/shard_map/all_gather | solution.py:29
  323.3 25.4 %copy.50 = bf16[2,4,768,2560]{3,2,1,0:T(8,128)(2,1)} copy(bf16[2,4,768,2560]{3,2,0,1:T(8,128)(2,1)} %bitcast.54) | data formatting | bytes 62914560 | tf_op jit(solution)/shard_map/transpose | solution.py:32
  348.7 121.7 %fusion.5 = f32[6144,3456]{0,1:T(8,128)} fusion(bf16[6144,2560]{1,0:T(8,128)(2,1)} %bitcast.49, bf16[3456,2560]{1,0:T(8,128)(2,1)} %param.8), kind=kOutput, calls=%fused_computation.16 | convolution fusion | flops 108716359680 | bytes 134086656 | tf_op jit(solution)/shard_map/dot_general | solution.py:56
  470.4 9.3 reduce-scatter.9.cloned.1.call-start
  479.7 17.0 constant_dynamic-update-slice_fusion.1
  504.9 94.9 %all-gather.11.cloned.1.call-done = bf16[8,768,2560]{2,1,0:T(8,128)(2,1)} async-done(((bf16[2,768,2560]{2,1,0:T(8,128)(2,1)}), bf16[8,768,2560]{2,1,0:T(8,128)(2,1)}) %all-gather.11.cloned.1.call-update) | async-done | bytes 31457296 | tf_op jit(solution)/shard_map/all_gather | solution.py:29
  599.8 27.7 %copy.46 = bf16[2,4,768,2560]{3,2,1,0:T(8,128)(2,1)} copy(bf16[2,4,768,2560]{3,2,0,1:T(8,128)(2,1)} %bitcast.53) | data formatting | bytes 62914560 | tf_op jit(solution)/shard_map/transpose | solution.py:32
  627.5 238.9 %convolution_bitcast_fusion = f32[6144,6912]{0,1:T(8,128)} fusion(bf16[2560,6912]{1,0:T(8,128)(2,1)} %constant_dynamic-update-slice_fusion, bf16[6144,2560]{1,0:T(8,128)(2,1)} %bitcast.51), kind=kOutput, calls=%fused_computation | convolution fusion | flops 217432719360 | bytes 236716032 | tf_op jit(solution)/shard_map/dot_general | solution.py:46
  866.5 165.2 %reduce-scatter.9.cloned.1.call-done = f32[3072,6912]{0,1:T(8,128)} async-done(((f32[6144,6912]{0,1:T(8,128)}), f32[3072,6912]{0,1:T(8,128)}) %reduce-scatter.9.cloned.1.call-update) | async-done | bytes 84934672 | tf_op jit(solution)/shard_map/reduce_scatter | solution.py:46
  1031.7 62.9 %multiply_convert_fusion.1 = (bf16[3072,3456]{0,1:T(8,128)(2,1)}, bf16[3072,3456]{0,1:T(8,128)(2,1)}, bf16[3072,3456]{0,1:T(8,128)(2,1)}) fusion(f32[3072,3456]{0,1:T(8,128)} %reduce-scatter.11.cloned.1.call-done, f32[3072,6912]{0,1:T(8,128)} %reduce-scatter.9.cloned.1.call-done), kind=kLoop, calls=%fused_computation.4 | loop fusion | flops 159252480 | bytes 191102976 | tf_op jit(solution)/shard_map/convert_element_type | solution.py:57
  1094.6 38.9 %pad_maximum_fusion = bf16[3072,6912]{0,1:T(8,128)(2,1)} fusion(bf16[3072,3456]{0,1:T(8,128)(2,1)} %get-tuple-element.31, bf16[3072,3456]{0,1:T(8,128)(2,1)} %get-tuple-element.30), kind=kLoop, calls=%fused_computation.2 | loop fusion | flops 84934656 | bytes 84934656 | tf_op jit(solution)/shard_map/concatenate | solution.py:59
  1133.8 24.4 %all-gather.7.cloned.1.call-done = bf16[6144,3456]{0,1:T(8,128)(2,1)} async-done(((bf16[3072,3456]{0,1:T(8,128)(2,1)}), bf16[6144,3456]{0,1:T(8,128)(2,1)}) %all-gather.7.cloned.1.call-update) | async-done | bytes 42467344 | tf_op jit(solution)/shard_map/all_gather | solution.py:52
  1158.2 129.1 %fusion.4 = f32[6144,2560]{1,0:T(8,128)} fusion(bf16[6144,3456]{0,1:T(8,128)(2,1)} %all-gather.7.cloned.1.call-done, bf16[3456,2560]{1,0:T(8,128)(2,1)} %param.8), kind=kOutput, calls=%fused_computation.15 | convolution fusion | flops 108716359680 | bytes 123076608 | tf_op jit(solution)/shard_map/dot_general | solution.py:53
  1287.3 61.0 %copy.47 = f32[2,4,768,2560]{2,3,0,1:T(8,128)} copy(f32[2,4,768,2560]{3,2,1,0:T(8,128)} %bitcast.48) | data formatting | bytes 125829120 | tf_op jit(solution)/shard_map/reshape | solution.py:37
  1348.8 235.3 %fusion.6 = f32[6144,2560]{1,0:T(8,128)} fusion(bf16[6144,6912]{0,1:T(8,128)(2,1)} %all-gather.9.cloned.1.call-done, bf16[2560,6912]{1,0:T(8,128)(2,1)} %constant_dynamic-update-slice_fusion), kind=kOutput, calls=%fused_computation.17 | convolution fusion | flops 217432719360 | bytes 183238656 | tf_op jit(solution)/shard_map/dot_general | solution.py:60
  1584.1 62.2 %copy.52 = f32[2,4,768,2560]{2,3,0,1:T(8,128)} copy(f32[2,4,768,2560]{3,2,1,0:T(8,128)} %bitcast.47) | data formatting | bytes 125829120 | tf_op jit(solution)/shard_map/reshape | solution.py:37
  1646.4 121.5 %fusion.7 = f32[3456,2560]{1,0:T(8,128)} fusion(bf16[6144,3456]{0,1:T(8,128)(2,1)} %all-gather.7.cloned.1.call-done, bf16[6144,2560]{1,0:T(8,128)(2,1)} %bitcast.50), kind=kOutput, calls=%fused_computation.18 | convolution fusion | flops 108716359680 | bytes 109314048 | tf_op jit(solution)/shard_map/dot_general | solution.py:62
  1767.9 236.4 %convolution_bitcast_fusion.1 = f32[2560,6912]{0,1:T(8,128)} fusion(bf16[6144,6912]{0,1:T(8,128)(2,1)} %all-gather.9.cloned.1.call-done, bf16[6144,2560]{1,0:T(8,128)(2,1)} %bitcast.52), kind=kOutput, calls=%fused_computation.1 | convolution fusion | flops 217432719360 | bytes 187170816 | tf_op jit(solution)/shard_map/dot_general | solution.py:61
  2004.3 50.1 %fusion.3 = (f32[2560,3456]{0,1:T(8,128)}, f32[2560,3456]{0,1:T(8,128)}) fusion(f32[2560,6912]{0,1:T(8,128)} %convolution_bitcast_fusion.1), kind=kLoop, calls=%fused_computation.14 | loop fusion | bytes 141557760 | tf_op jit(solution)/shard_map/slice | solution.py:63
  2054.4 34.5 %copy.55 = f32[2560,3456]{1,0:T(8,128)} copy(f32[2560,3456]{0,1:T(8,128)} %get-tuple-element.34) | data formatting | bytes 70778880
  2088.9 34.1 %copy.56 = f32[2560,3456]{1,0:T(8,128)} copy(f32[2560,3456]{0,1:T(8,128)} %get-tuple-element.33) | data formatting | bytes 70778880
  2132.0 11.4 all_to_all.22
  2143.4 10.8 copy.53
  2154.2 238.3 %reduce-scatter.15.cloned.1.call-done = f32[2,1,768,2560]{2,3,0,1:T(8,128)} async-done(((f32[2,4,768,2560]{2,3,0,1:T(8,128)}), f32[2,1,768,2560]{2,3,0,1:T(8,128)}) %reduce-scatter.15.cloned.1.call-update) | async-done | bytes 15728656
  2401.0 11.3 all_to_all.23
  2412.2 10.6 copy.54
  (23 shorter events, 26.7 us)
Async XLA Ops:
  7.2 316.2 %all-gather.13.cloned.1.call-start = ((), (), s32[]{:S(2)}) async-start(), calls=%async_computation.13 | async-start | bytes 39321600 | tf_op jit(solution)/shard_map/all_gather | solution.py:29
  46.6 553.2 %all-gather.11.cloned.1.call-start = ((), (), s32[]{:S(2)}) async-start(), calls=%async_computation.12 | async-start | bytes 39321600 | tf_op jit(solution)/shard_map/all_gather | solution.py:29
  86.7 779.8 %reduce-scatter.11.cloned.1.call-start = ((), (), s32[]{:S(2)}) async-start(), calls=%async_computation.10 | async-start | bytes 127401984 | tf_op jit(solution)/shard_map/reduce_scatter | solution.py:56
  470.4 561.3 %reduce-scatter.9.cloned.1.call-start = ((), (), s32[]{:S(2)}) async-start(), calls=%async_computation.8 | async-start | bytes 254803968 | tf_op jit(solution)/shard_map/reduce_scatter | solution.py:46
  479.7 17.9 copy-start
  866.4 291.8 %all-gather.7.cloned.1.call-start = ((), (), s32[]{:S(2)}) async-start(), calls=%async_computation.9 | async-start | bytes 63700992 | tf_op jit(solution)/shard_map/all_gather | solution.py:52
  1094.6 254.3 %all-gather.9.cloned.1.call-start = ((), (), s32[]{:S(2)}) async-start(), calls=%async_computation.11 | async-start | bytes 127401984 | tf_op jit(solution)/shard_map/all_gather | solution.py:59
  1133.5 989.5 %reduce-scatter.13.cloned.1.call-start = ((), (), s32[]{:S(2)}) async-start(), calls=%async_computation.14 | async-start | bytes 78643200
  1348.4 1044.1 %reduce-scatter.15.cloned.1.call-start = ((), (), s32[]{:S(2)}) async-start(), calls=%async_computation.15 | async-start | bytes 78643200
Sparse Core Ops, SparseCore 0:
  46.7 276.5 all-gather.12
  325.7 274.0 all-gather.10
  602.1 85.0 reduce-scatter.10
  866.5 165.1 reduce-scatter.8
  1094.7 63.4 all-gather.6
  1159.6 118.5 all-gather.8
  1348.5 520.9 reduce-scatter.12
  1872.5 519.9 reduce-scatter.14
where the time goes:
time: 2440 us; the launch traced here: 2430 us
  matrix products  1080 us (44%)
  waiting for transfers between devices  760 us (31%)
  local copies, waits for them, and re-layouts  385 us (16%)
  other arithmetic  119 us (5%)
  blocking collectives  59 us (2%)
    all_gather x2, waiting for transfers between devices, all_tokens(): vg = lax.all_gather(va, 'tp', axis=0, tiled=False)  331 us
    dot_general x1, matrix products, local(): jnp.dot(xt, w, preferred_element_type=f32)  239 us
    unnamed x10, waiting for transfers between devices  238 us
    dot_general x1, matrix products, local(): dw = jnp.dot(xt.T, dab, preferred_element_type=f32)  236 us
    dot_general x1, matrix products, local(): dx = combine_tp(jnp.dot(dab, w.T, preferred_element_type=f32), dya)  235 us
    reduce_scatter x1, waiting for transfers between devices, local(): lax.psum_scatter(jnp.dot(xt, w, preferred_element_type=f32), 'dp', scatte...  165 us
    unnamed x9, local copies, waits for them, and re-layouts  130 us
    dot_general x1, matrix products, local(): y = combine_tp(jnp.dot(hg, w_down, preferred_element_type=f32), xa)  129 us
  transfers between devices with their start and end apart: 8, of which 5 were waited for; matrix products, arithmetic and copies ran while one was open for 61% of the time, Pallas kernels for 0%

commit v1 on v0

v1 whole, which is shorter than its diff:
```python
import jax
import jax.numpy as jnp
from jax import lax
from jax.experimental import pallas as pl
from jax.experimental.pallas import tpu as pltpu
from jax.sharding import PartitionSpec as P


f32 = jnp.float32
bf = jnp.bfloat16
NT = (((1,), (1,)), ((), ()))
TN = (((0,), (0,)), ((), ()))
VMEM = 62 * 1024 * 1024
ONE = pl.Buffered(1)
ANY = pl.BlockSpec(memory_space=pl.ANY)


def mm(u, v):
    return jnp.dot(u, v, preferred_element_type=f32)


def dg(u, v, dims):
    return lax.dot_general(u, v, dims, preferred_element_type=f32)


def sds(shape, dtype):
    return jax.ShapeDtypeStruct(shape, dtype)


def spec(shape, index, once=False):
    if once:
        return pl.BlockSpec(shape, index, pipeline_mode=ONE)
    return pl.BlockSpec(shape, index)


def row_loop(rows, step, fn):
    def trip(m, carry):
        fn(pl.ds(pl.multiple_of(m * step, step), step))
        return carry

    lax.fori_loop(0, rows // step, trip, 0)


def call(body, core, grid, ins, outs, args, flops, scratch=(), aliases=None):
    moved = sum(a.size * a.dtype.itemsize for a in args)
    return pl.pallas_call(
        body,
        grid_spec=pltpu.PrefetchScalarGridSpec(
            num_scalar_prefetch=1, grid=grid, in_specs=list(ins), out_specs=[o[0] for o in outs], scratch_shapes=list(scratch)
        ),
        out_shape=[sds(o[1], o[2]) for o in outs],
        input_output_aliases=aliases or {},
        compiler_params=pltpu.CompilerParams(dimension_semantics=("arbitrary",) * len(grid), vmem_limit_bytes=VMEM),
        cost_estimate=pl.CostEstimate(flops=int(flops), bytes_accessed=int(moved), transcendentals=0),
    )(core, *args)


def silu_h(a, b):
    return (a * jax.nn.sigmoid(a) * b).astype(bf)


def k_fwd0(core, x, wg, wgo, wu, wuo, tn=512):
    r, d = x.shape
    hd, f = wg.shape
    steps = pl.cdiv(f, tn)
    last = f - (steps - 1) * tn

    def body(i_ref, x_ref, wg_ref, wgo_ref, wu_ref, wuo_ref, a_ref, b_ref, h_ref, hall_ref, xall_ref, wgc_ref, wuc_ref, sem, wsem):
        n = pl.program_id(0)
        s = pl.multiple_of(i_ref[0] * hd, 128)
        o = pl.multiple_of((1 - i_ref[0]) * hd, 128)
        keep_x = pltpu.make_async_copy(x_ref, xall_ref.at[pl.ds(0, r), :], sem)

        def copies(width):
            c = pl.ds(pl.multiple_of(n * tn, 128), width)
            moves = ((wg_ref, wgc_ref, s), (wgo_ref, wgc_ref, o), (wu_ref, wuc_ref, s), (wuo_ref, wuc_ref, o))
            return [
                pltpu.make_async_copy(u.at[:, pl.ds(0, width)], v.at[pl.ds(q, hd), c], wsem.at[k])
                for k, (u, v, q) in enumerate(moves)
            ]

        @pl.when(n == 0)
        def _():
            keep_x.start()

        @pl.when(n < steps - 1)
        def _():
            for c in copies(tn):
                c.start()

        @pl.when(n == steps - 1)
        def _():
            for c in copies(last):
                c.start()

        def rows(m):
            xs = x_ref[m, pl.ds(s, hd)]
            xo = x_ref[m, pl.ds(o, hd)]
            a = mm(xs, wg_ref[...]) + mm(xo, wgo_ref[...])
            b = mm(xs, wu_ref[...]) + mm(xo, wuo_ref[...])
            a_ref[m, :] = a
            b_ref[m, :] = b
            h = silu_h(a, b)
            h_ref[m, :] = h
            hall_ref[m, :] = h

        row_loop(r, 256, rows)

        @pl.when(n < steps - 1)
        def _():
            for c in copies(tn):
                c.wait()

        @pl.when(n == steps - 1)
        def _():
            for c in copies(last):
                c.wait()
            keep_x.wait()

    w = spec((hd, tn), lambda n, i: (0, n))
    o = spec((r, tn), lambda n, i: (0, n))
    return call(
        body, core, (steps,),
        [spec((r, d), lambda n, i: (0, 0), True), w, w, w, w],
        [(o, (r, f), f32), (o, (r, f), f32), (o, (r, f), bf), (o, (4 * r, f), bf), (ANY, (4 * r, d), bf),
         (ANY, (d, f), bf), (ANY, (d, f), bf)],
        (x, wg, wgo, wu, wuo), 4 * r * d * f,
        scratch=[pltpu.SemaphoreType.DMA, pltpu.SemaphoreType.DMA((4,))],
    )


def k_fwd(core, slot, x, wg, wu, hall, xall, tn=512):
    r, d = x.shape
    f = wg.shape[1]
    steps = pl.cdiv(f, tn)

    def body(i_ref, x_ref, wg_ref, wu_ref, hin_ref, xin_ref, a_ref, b_ref, h_ref, hall_ref, xall_ref, sem):
        n = pl.program_id(0)
        keep_x = pltpu.make_async_copy(x_ref, xall_ref.at[pl.ds(slot * r, r), :], sem)

        @pl.when(n == 0)
        def _():
            keep_x.start()

        def rows(m):
            a = mm(x_ref[m, :], wg_ref[...])
            b = mm(x_ref[m, :], wu_ref[...])
            a_ref[m, :] = a
            b_ref[m, :] = b
            h = silu_h(a, b)
            h_ref[m, :] = h
            hall_ref[m, :] = h

        row_loop(r, 256, rows)

        @pl.when(n == steps - 1)
        def _():
            keep_x.wait()

    w = spec((d, tn), lambda n, i: (0, n))
    o = spec((r, tn), lambda n, i: (0, n))
    return call(
        body, core, (steps,),
        [spec((r, d), lambda n, i: (0, 0), True), w, w, ANY, ANY],
        [(o, (r, f), f32), (o, (r, f), f32), (o, (r, f), bf),
         (spec((r, tn), lambda n, i: (slot, n)), (4 * r, f), bf), (ANY, (4 * r, d), bf)],
        (x, wg, wu, hall, xall), 4 * r * d * f,
        scratch=[pltpu.SemaphoreType.DMA], aliases={4: 3, 5: 4},
    )


def k_y0(core, h, wd, wdo, tn=512):
    r, f = h.shape
    hd = wd.shape[1]
    nt = hd // tn

    def body(i_ref, h_ref, w_ref, wo_ref, o_ref, wc_ref, sem):
        n = pl.program_id(0)
        own = (n < nt) == (i_ref[0] == 0)

        def part(w):
            keep = pltpu.make_async_copy(w, wc_ref.at[:, pl.ds(pl.multiple_of(n * tn, 128), tn)], sem)
            keep.start()

            def rows(m):
                o_ref[m, :] = mm(h_ref[m, :], w[...])

            row_loop(r, 256, rows)
            keep.wait()

        @pl.when(own)
        def _():
            part(w_ref)

        @pl.when(jnp.logical_not(own))
        def _():
            part(wo_ref)

    return call(
        body, core, (2 * nt,),
        [spec((r, f), lambda n, i: (0, 0), True),
         spec((f, tn), lambda n, i: (0, jnp.clip(n - i[0] * nt, 0, nt - 1))),
         spec((f, tn), lambda n, i: (0, jnp.clip(n - (1 - i[0]) * nt, 0, nt - 1)))],
        [(spec((r, tn), lambda n, i: (0, n)), (r, 2 * hd), f32), (ANY, (f, 2 * hd), bf)],
        (h, wd, wdo), 4 * r * hd * f,
        scratch=[pltpu.SemaphoreType.DMA],
    )


def k_y(core, h, wd, add=None, tn=512):
    r, f = h.shape
    d = wd.shape[1]

    def body(i_ref, h_ref, w_ref, *rest):
        def rows(m):
            v = mm(h_ref[m, :], w_ref[...])
            rest[-1][m, :] = v if add is None else v + rest[0][m, :]

        row_loop(r, 256, rows)

    o = spec((r, tn), lambda n, i: (0, n))
    more = () if add is None else (add,)
    return call(
        body, core, (d // tn,),
        [spec((r, f), lambda n, i: (0, 0), True), spec((f, tn), lambda n, i: (0, n))] + [o] * len(more),
        [(o, (r, d), f32)], (h, wd) + more, 2 * r * d * f,
    )[0]


def k_g(core, slot, dy, wd, a, b, keep, tn=512):
    r, d = dy.shape
    f = wd.shape[0]
    steps = pl.cdiv(f, tn)
    n_in = 5 + len(keep)

    def body(*refs):
        _, dy_ref, w_ref, a_ref, b_ref = refs[:5]
        da_ref, db_ref, daall_ref, dball_ref, dyall_ref, sem = refs[n_in:]
        n = pl.program_id(0)
        keep_dy = pltpu.make_async_copy(dy_ref, dyall_ref.at[pl.ds(slot * r, r), :], sem)

        @pl.when(n == 0)
        def _():
            keep_dy.start()

        def rows(m):
            g = dg(dy_ref[m, :], w_ref[...], NT)
            a = a_ref[m, :]
            b = b_ref[m, :]
            sig = jax.nn.sigmoid(a)
            da = (g * b * sig * (1.0 + a * (1.0 - sig))).astype(bf)
            db = (g * (a * sig)).astype(bf)
            da_ref[m, :] = da
            db_ref[m, :] = db
            daall_ref[m, :] = da
            dball_ref[m, :] = db

        row_loop(r, 256, rows)

        @pl.when(n == steps - 1)
        def _():
            keep_dy.wait()

    o = spec((r, tn), lambda n, i: (0, n))
    oall = spec((r, tn), lambda n, i: (slot, n))
    return call(
        body, core, (steps,),
        [spec((r, d), lambda n, i: (0, 0), True), spec((tn, d), lambda n, i: (n, 0)), o, o] + [ANY] * len(keep),
        [(o, (r, f), bf), (o, (r, f), bf), (oall, (4 * r, f), bf), (oall, (4 * r, f), bf), (ANY, (4 * r, d), bf)],
        (dy, wd, a, b) + tuple(keep), 2 * r * d * f,
        scratch=[pltpu.SemaphoreType.DMA], aliases={5: 2, 6: 3, 7: 4} if keep else None,
    )


def k_dx(core, da, db, wg, wu, add=None, pieces=1, tn=512):
    r, f = da.shape
    d = wg.shape[0]
    rp = r // pieces
    more = () if add is None else (add,)

    def body(i_ref, da_ref, db_ref, wg_ref, wu_ref, *rest):
        outs = rest[len(more):]

        def rows(m, o_ref, mo):
            v = dg(da_ref[m, :], wg_ref[...], NT) + dg(db_ref[m, :], wu_ref[...], NT)
            o_ref[mo, :] = v if add is None else v + rest[0][m, :].astype(f32)

        if pieces == 1:
            row_loop(r, 256, lambda m: rows(m, outs[0], m))
        else:
            for p in range(pieces):
                rows(slice(p * rp, (p + 1) * rp), outs[p], slice(0, rp))

    w = spec((tn, f), lambda n, i: (n, 0))
    hs = spec((r, f), lambda n, i: (0, 0), True)
    return call(
        body, core, (d // tn,),
        [hs, hs, w, w] + [spec((r, tn), lambda n, i: (0, n))] * len(more),
        [(spec((rp, tn), lambda n, i: (0, n)), (rp, d), f32)] * pieces,
        (da, db, wg, wu) + more, 4 * r * d * f,
    )


def k_dw(core, x, xo, d, do, tm=1280, tn=512):
    t, f = d.shape
    hd = x.shape[1] // 2
    nt = hd // tm

    def body(i_ref, x_ref, xo_ref, d_ref, do_ref, o_ref):
        def cols(m):
            o_ref[m, :] = dg(x_ref[:, m], d_ref[...], TN) + dg(xo_ref[:, m], do_ref[...], TN)

        row_loop(tm, 256, cols)

    xs = spec((t, tm), lambda n, m, i: (0, m + i[0] * nt))
    ds = spec((t, tn), lambda n, m, i: (0, n))
    return call(
        body, core, (pl.cdiv(f, tn), nt), [xs, xs, ds, ds],
        [(spec((tm, tn), lambda n, m, i: (m, n)), (hd, f), f32)], (x, xo, d, do), 4 * t * hd * f,
    )[0]


def k_dwd(core, h, ho, dy, dyo, tm=1152, tn=512):
    t, f = h.shape
    hd = dy.shape[1] // 2
    nt = hd // tn

    def body(i_ref, h_ref, ho_ref, d_ref, do_ref, o_ref):
        def cols(m):
            o_ref[m, :] = dg(h_ref[:, m], d_ref[...], TN) + dg(ho_ref[:, m], do_ref[...], TN)

        row_loop(tm, 384, cols)

    hs = spec((t, tm), lambda n, m, i: (0, m))
    ds = spec((t, tn), lambda n, m, i: (0, n + i[0] * nt))
    return call(
        body, core, (nt, f // tm), [hs, hs, ds, ds],
        [(spec((tm, tn), lambda n, m, i: (m, n)), (f, hd), f32)], (h, ho, dy, dyo), 4 * t * hd * f,
    )[0]


def k_add(core, u, v, tr=96):
    r, d = u.shape

    def body(i_ref, u_ref, v_ref, o_ref):
        o_ref[...] = u_ref[...] + v_ref[...]

    o = spec((tr, d), lambda n, i: (n, 0))
    return call(body, core, (r // tr,), [o, o], [(o, (r, d), f32)], (u, v), r * d)[0]


def k_fin(core, p, u, v, keep, tr=64):
    r, d = u.shape
    n0 = p * v.shape[0] // tr

    def body(i_ref, u_ref, v_ref, *rest):
        rest[-1][...] = (u_ref[...] + v_ref[...]).astype(bf)

    o = spec((tr, d), lambda n, i: (n0 + n, 0))
    return call(
        body, core, (v.shape[0] // tr,), [o, spec((tr, d), lambda n, i: (n, 0))] + [ANY] * len(keep),
        [(o, (r, d), bf)], (u, v) + tuple(keep), r * d, aliases={3: 0} if keep else None,
    )[0]


def solution(mesh):
    ny = mesh.shape["tp"]
    rows = P(("dp", "tp"), None)
    wsp = P("dp", "tp")
    dsp = P("tp", "dp")
    axes = ("tp", "dp")

    def pairs(first):
        out = []
        for j in range(ny):
            for c in range(2):
                bit = 1 if (c == 0) == first else 2
                out.append((j * 2 + c, (j ^ bit) * 2 + c))
        return out

    p1, p2 = pairs(True), pairs(False)

    def to1(v):
        return lax.ppermute(v, axes, p1)

    def to2(v):
        return lax.ppermute(v, axes, p2)

    def swap(v):
        return lax.ppermute(v, "dp", [(0, 1), (1, 0)])

    def layer(x, wg, wu, wd, dy):
        i = lax.axis_index("dp").astype(jnp.int32).reshape(1)
        x1, x2 = to1(x), to2(x)
        dy2 = to2(dy)
        wgo, wuo, wdo = swap(wg), swap(wu), swap(wd)
        xd = to1(x2)
        dy1 = to1(dy)
        dyd = to1(dy2)

        a0, b0, h0, hall, xall, wgc, wuc = k_fwd0(i, x, wg, wgo, wu, wuo)
        y0, wdc = k_y0(i, h0, wd, wdo)
        a1, b1, h1, hall, xall = k_fwd(i, 1, x1, wgc, wuc, hall, xall)
        a2, b2, h2, hall, xall = k_fwd(i, 2, x2, wgc, wuc, hall, xall)
        a3, b3, h3, hall, xall = k_fwd(i, 3, xd, wgc, wuc, hall, xall)
        y1 = k_y(i, h1, wdc)
        y3 = k_y(i, h3, wdc)
        ra = to1(y3)
        r1 = to1(y1)
        y2 = k_y(i, h2, wdc, ra)
        r2 = to2(y2)

        def bwd(slot, v, a, b, keep):
            return k_g(i, slot, v, wdc, a, b, keep)

        da0, db0, *alls = bwd(0, dy, a0, b0, ())
        da1, db1, *alls = bwd(1, dy1, a1, b1, alls)
        da2, db2, *alls = bwd(2, dy2, a2, b2, alls)
        da3, db3, *alls = bwd(3, dyd, a3, b3, alls)
        daall, dball, dyall = alls
        z0 = k_dx(i, da0, db0, wgc, wuc, add=dy)[0]
        z1 = k_dx(i, da1, db1, wgc, wuc)[0]
        z3 = k_dx(i, da3, db3, wgc, wuc)[0]
        sa = to1(z3)
        s1 = to1(z1)
        z2 = k_dx(i, da2, db2, wgc, wuc, add=sa, pieces=4)
        s2 = [to2(z2[p]) for p in range(4)]

        xallo, hallo = swap(xall), swap(hall)
        dyallo, daallo, dballo = swap(dyall), swap(daall), swap(dball)
        dwd = k_dwd(i, hall, hallo, dyall, dyallo)
        dwg = k_dw(i, xall, xallo, daall, daallo)
        dwu = k_dw(i, xall, xallo, dball, dballo)

        y = (x.astype(f32) + y0 + r1 + r2).astype(bf)
        pre = k_add(i, z0, s1)
        dx = ()
        for p in range(4):
            dx = (k_fin(i, p, pre, s2[p], dx),)
        return y, dx[0], dwg, dwu, dwd

    return jax.shard_map(layer, mesh=mesh, in_specs=(rows, wsp, wsp, dsp, rows), out_specs=(rows, rows, wsp, wsp, dsp), check_vma=False)
```

time: 2440 us -> 2040 us (0.84)
  Pallas kernels: 0 us -> 1360 us
  matrix products: 1080 us -> 0 us
  local copies, waits for them, and re-layouts: 385 us -> 0 us
  waiting for transfers between devices: 760 us -> 634 us
  other arithmetic: 119 us -> 21.6 us
  blocking collectives: 59 us -> 0 us
    pallas_call x0 -> x24, Pallas kernels: none -> 1360 us  [call(): pl.pallas_call(body, grid_spec=pltpu.PrefetchScalarGridSpec(num_scalar_pr...]
    dot_general x6 -> x0, matrix products: 1080 us -> none  [the longest x1 239 us: local(): jnp.dot(xt, w, preferred_element_type=f32)]
    ppermute x0 -> x23, waiting for transfers between devices: none -> 634 us  [the longest x8 376 us: to1(): return lax.ppermute(v, axes, p1)]
    all_gather x4 -> x0, waiting for transfers between devices: 356 us -> none  [the longest x2 331 us: all_tokens(): vg = lax.all_gather(va, 'tp', axis=0, tiled=False)]
    unnamed x10 -> x0, waiting for transfers between devices: 238 us -> none
    reduce_scatter x2 -> x0, waiting for transfers between devices: 165 us -> none  [the longest x1 165 us: local(): lax.psum_scatter(jnp.dot(xt, w, preferred_element_type=f32), 'dp', scatte...]
    unnamed x9 -> x0, local copies, waits for them, and re-layouts: 130 us -> none
    reshape x2 -> x0, local copies, waits for them, and re-layouts: 123 us -> none  [combine_tp(): q.reshape(nx, ny, tl, dl)]
  transfers between devices with their start and end apart: 8 -> 23, of which waited for: 5 -> 6; matrix products, arithmetic and copies ran while one was open for 61% -> 0% of each run, Pallas kernels for 0% -> 61%
where the time goes in v1:
time: 2040 us
  Pallas kernels  1360 us (67%)
  waiting for transfers between devices  634 us (31%)
  other arithmetic  21.6 us (1%)
  starting transfers between devices  20.8 us (1%)
    pallas_call x24, Pallas kernels, call(): pl.pallas_call(body, grid_spec=pltpu.PrefetchScalarGridSpec(num_scalar_pr...  1360 us
    ppermute x8, waiting for transfers between devices, to1(): return lax.ppermute(v, axes, p1)  376 us
    ppermute x7, waiting for transfers between devices, to2(): return lax.ppermute(v, axes, p2)  258 us
  transfers between devices with their start and end apart: 23, of which 6 were waited for; matrix products, arithmetic and copies ran while one was open for 0% of the time, Pallas kernels for 61%

profile of v1, /device:TPU:0, one launch (start us, length us, event | category | flops | bytes accessed | tf_op | source)
XLA Modules:
  0.0 2036.0 jit_solution(4709152570111417810)
XLA Ops:
  1.5 3.0 collective-permute-start.5
  6.5 167.6 %collective-permute-done.5.x_ref = bf16[768,5120]{1,0:T(8,128)(2,1)} collective-permute-done((bf16[768,5120]{1,0:T(8,128)(2,1)}, bf16[768,5120]{1,0:T(8,128)(2,1)}, u32[]{:S(2)}, u32[]{:S(2)}) %collective-permute-start.5) | collective-permute-done | bytes 7864352 | tf_op jit(solution)/shard_map/ppermute | solution.py:387
  174.1 85.1 %collective-permute-done.11.refs_1_ = bf16[768,5120]{1,0:T(8,128)(2,1)} collective-permute-done((bf16[768,5120]{1,0:T(8,128)(2,1)}, bf16[768,5120]{1,0:T(8,128)(2,1)}, u32[]{:S(2)}, u32[]{:S(2)}) %collective-permute-start.11) | collective-permute-done | bytes 7864352 | tf_op jit(solution)/shard_map/ppermute | solution.py:387
  263.2 70.4 %shard_map.92 = (f32[768,3456]{1,0:T(8,128)}, f32[768,3456]{1,0:T(8,128)}, bf16[768,3456]{1,0:T(8,128)(2,1)}, bf16[3072,3456]{1,0:T(8,128)(2,1)}, bf16[3072,5120...) custom-call(s32[1]{0:T(128)} %bitcast.i_ref.refs_0_, bf16[768,5120]{1,0:T(8,128)(2,1)} %x_ref.1, ...), custom_call_target="tpu_custom_call" | custom-call | flops 54358179840 | bytes 78643200 | tf_op jit(solution)/shard_map/pallas_call | solution.py:46
  333.6 68.9 %shard_map.94 = (f32[768,3456]{1,0:T(8,128)}, f32[768,3456]{1,0:T(8,128)}, bf16[768,3456]{1,0:T(8,128)(2,1)}, bf16[3072,3456]{1,0:T(8,128)(2,1)}, bf16[3072,5120]{1,0:T(8,128)(2,1)}) custom-call(s32[1]{0:T(128)} %bitcast.i_ref.refs_0_, bf16[768,5120]{1,0:T(8,128)(2,1)} %collective-permute-done.3.x_ref, ...), custom_call_target="tpu_custom_call", output_to_operand_aliasing={{3}: (4, {}), {4}: (5, {})} | custom-call | flops 54358179840 | bytes 131334144 | tf_op jit(solution)/shard_map/pallas_call | solution.py:46
  402.5 69.0 %shard_map.96 = (f32[768,3456]{1,0:T(8,128)}, f32[768,3456]{1,0:T(8,128)}, bf16[768,3456]{1,0:T(8,128)(2,1)}, bf16[3072,3456]{1,0:T(8,128)(2,1)}, bf16[3072,5120]{1,0:T(8,128)(2,1)}) custom-call(s32[1]{0:T(128)} %bitcast.i_ref.refs_0_, bf16[768,5120]{1,0:T(8,128)(2,1)} %collective-permute-done.5.x_ref, ...), custom_call_target="tpu_custom_call", output_to_operand_aliasing={{3}: (4, {}), {4}: (5, {})} | custom-call | flops 54358179840 | bytes 131334144 | tf_op jit(solution)/shard_map/pallas_call | solution.py:46
  471.5 41.8 %shard_map.93 = (f32[768,5120]{1,0:T(8,128)}, bf16[3456,5120]{1,0:T(8,128)(2,1)}) custom-call(s32[1]{0:T(128)} %bitcast.i_ref.refs_0_, bf16[768,3456]{1,0:T(8,128)(2,1)} %get-tuple-element.53.h_ref, bf16[3456,2560]{1,0:T(8,128)(2,1)} %w_ref.1, bf16[3456,2560]{1,0:T(8,128)(2,1)} %collective-permute-done.2.wo_ref), custom_call_target="tpu_custom_call" | custom-call | flops 27179089920 | bytes 40697856 | tf_op jit(solution)/shard_map/pallas_call | solution.py:46
  513.4 42.4 %shard_map.100 = (bf16[768,3456]{1,0:T(8,128)(2,1)}, bf16[768,3456]{1,0:T(8,128)(2,1)}, bf16[3072,3456]{1,0:T(8,128)(2,1)}, bf16[3072,3456]{1,0:T(8,128)(2,1)}, bf16[3072,5120]{1,0:T(8,128)(2,1)}) custom-call(s32[1]{0:T(128)} %bitcast.i_ref.refs_0_, bf16[768,5120]{1,0:T(8,128)(2,1)} %rest_0_.1, bf16[3456,5120]{1,0:T(8,128)(2,1)} %get-tuple-element.60.w_ref.refs_2_, ...), custom_call_target="tpu_custom_call" | custom-call | flops 27179089920 | bytes 64487424 | tf_op jit(solution)/shard_map/pallas_call | solution.py:46
  555.8 42.5 %shard_map.102 = (bf16[768,3456]{1,0:T(8,128)(2,1)}, bf16[768,3456]{1,0:T(8,128)(2,1)}, bf16[3072,3456]{1,0:T(8,128)(2,1)}, bf16[3072,3456]{1,0:T(8,128)(2,1)}, bf16[3072,5120]{1,0:T(8,128)(2,1)}) custom-call(s32[1]{0:T(128)} %bitcast.i_ref.refs_0_, ...), custom_call_target="tpu_custom_call", output_to_operand_aliasing={{2}: (5, {}), {3}: (6, {}), {4}: (7, {})} | custom-call | flops 27179089920 | bytes 138412032 | tf_op jit(solution)/shard_map/pallas_call | solution.py:46
  598.3 42.4 %shard_map.105 = (bf16[768,3456]{1,0:T(8,128)(2,1)}, bf16[768,3456]{1,0:T(8,128)(2,1)}, bf16[3072,3456]{1,0:T(8,128)(2,1)}, bf16[3072,3456]{1,0:T(8,128)(2,1)}, bf16[3072,5120]{1,0:T(8,128)(2,1)}) custom-call(s32[1]{0:T(128)} %bitcast.i_ref.refs_0_, ...), custom_call_target="tpu_custom_call", output_to_operand_aliasing={{2}: (5, {}), {3}: (6, {}), {4}: (7, {})} | custom-call | flops 27179089920 | bytes 138412032 | tf_op jit(solution)/shard_map/pallas_call | solution.py:46
  640.7 69.1 %shard_map.97 = (f32[768,3456]{1,0:T(8,128)}, f32[768,3456]{1,0:T(8,128)}, bf16[768,3456]{1,0:T(8,128)(2,1)}, bf16[3072,3456]{1,0:T(8,128)(2,1)}, bf16[3072,5120]{1,0:T(8,128)(2,1)}) custom-call(s32[1]{0:T(128)} %bitcast.i_ref.refs_0_, bf16[768,5120]{1,0:T(8,128)(2,1)} %collective-permute-done.6.x_ref, ...), custom_call_target="tpu_custom_call", output_to_operand_aliasing={{3}: (4, {}), {4}: (5, {})} | custom-call | flops 54358179840 | bytes 131334144 | tf_op jit(solution)/shard_map/pallas_call | solution.py:46
  709.9 42.4 %shard_map.106 = (bf16[768,3456]{1,0:T(8,128)(2,1)}, bf16[768,3456]{1,0:T(8,128)(2,1)}, bf16[3072,3456]{1,0:T(8,128)(2,1)}, bf16[3072,3456]{1,0:T(8,128)(2,1)}, bf16[3072,5120]{1,0:T(8,128)(2,1)}) custom-call(s32[1]{0:T(128)} %bitcast.i_ref.refs_0_, ...), custom_call_target="tpu_custom_call", output_to_operand_aliasing={{2}: (5, {}), {3}: (6, {}), {4}: (7, {})} | custom-call | flops 27179089920 | bytes 138412032 | tf_op jit(solution)/shard_map/pallas_call | solution.py:46
  752.2 70.2 %shard_map.107 = f32[768,5120]{1,0:T(8,128)} custom-call(s32[1]{0:T(128)} %bitcast.i_ref.refs_0_, bf16[768,3456]{1,0:T(8,128)(2,1)} %get-tuple-element.90.da_ref, bf16[768,3456]{1,0:T(8,128)(2,1)} %get-tuple-element.91.db_ref, bf16[5120,3456]{1,0:T(8,128)(2,1)} %get-tuple-element.55.wg_ref, bf16[5120,3456]{1,0:T(8,128)(2,1)} %get-tuple-element.56.wu_ref), custom_call_target="tpu_custom_call" | custom-call | flops 54358179840 | bytes 81395712 | tf_op jit(solution)/shard_map/pallas_call | solution.py:46
  822.5 70.2 %shard_map.103 = f32[768,5120]{1,0:T(8,128)} custom-call(s32[1]{0:T(128)} %bitcast.i_ref.refs_0_, bf16[768,3456]{1,0:T(8,128)(2,1)} %get-tuple-element.76.da_ref, bf16[768,3456]{1,0:T(8,128)(2,1)} %get-tuple-element.77.db_ref, bf16[5120,3456]{1,0:T(8,128)(2,1)} %get-tuple-element.55.wg_ref, bf16[5120,3456]{1,0:T(8,128)(2,1)} %get-tuple-element.56.wu_ref), custom_call_target="tpu_custom_call" | custom-call | flops 54358179840 | bytes 81395712 | tf_op jit(solution)/shard_map/pallas_call | solution.py:46
  894.6 38.2 %shard_map.98 = f32[768,5120]{1,0:T(8,128)} custom-call(s32[1]{0:T(128)} %bitcast.i_ref.refs_0_, bf16[768,3456]{1,0:T(8,128)(2,1)} %get-tuple-element.66.h_ref, bf16[3456,5120]{1,0:T(8,128)(2,1)} %get-tuple-element.60.w_ref.refs_2_), custom_call_target="tpu_custom_call" | custom-call | flops 27179089920 | bytes 40697856 | tf_op jit(solution)/shard_map/pallas_call | solution.py:46
  933.1 61.7 %collective-permute-done.13.rest_0_ = f32[768,5120]{1,0:T(8,128)} collective-permute-done((f32[768,5120]{1,0:T(8,128)}, f32[768,5120]{1,0:T(8,128)}, u32[]{:S(2)}, u32[]{:S(2)}) %collective-permute-start.13) | collective-permute-done | bytes 15728672 | tf_op jit(solution)/shard_map/ppermute | solution.py:384
  994.9 102.9 %shard_map.108 = (f32[192,5120]{1,0:T(8,128)}, f32[192,5120]{1,0:T(8,128)}, f32[192,5120]{1,0:T(8,128)}, f32[192,5120]{1,0:T(8,128)}) custom-call(s32[1]{0:T(128)} %bitcast.i_ref.refs_0_, bf16[768,3456]{1,0:T(8,128)(2,1)} %get-tuple-element.83.da_ref, bf16[768,3456]{1,0:T(8,128)(2,1)} %get-tuple-element.84.db_ref, ...), custom_call_target="tpu_custom_call" | custom-call | flops 54358179840 | bytes 97124352 | tf_op jit(solution)/shard_map/pallas_call | solution.py:46
  1099.3 106.2 %collective-permute-done.10.v_ref = f32[768,5120]{1,0:T(8,128)} collective-permute-done((f32[768,5120]{1,0:T(8,128)}, f32[768,5120]{1,0:T(8,128)}, u32[]{:S(2)}, u32[]{:S(2)}) %collective-permute-start.10) | collective-permute-done | bytes 15728672 | tf_op jit(solution)/shard_map/ppermute | solution.py:384
  1207.8 208.4 %collective-permute-done.7.rest_0_ = f32[768,5120]{1,0:T(8,128)} collective-permute-done((f32[768,5120]{1,0:T(8,128)}, f32[768,5120]{1,0:T(8,128)}, u32[]{:S(2)}, u32[]{:S(2)}) %collective-permute-start.7) | collective-permute-done | bytes 15728672 | tf_op jit(solution)/shard_map/ppermute | solution.py:384
  1419.0 38.2 %shard_map.95 = f32[768,5120]{1,0:T(8,128)} custom-call(s32[1]{0:T(128)} %bitcast.i_ref.refs_0_, bf16[768,3456]{1,0:T(8,128)(2,1)} %get-tuple-element.59.h_ref, bf16[3456,5120]{1,0:T(8,128)(2,1)} %get-tuple-element.60.w_ref.refs_2_), custom_call_target="tpu_custom_call" | custom-call | flops 27179089920 | bytes 40697856 | tf_op jit(solution)/shard_map/pallas_call | solution.py:46
  1457.2 5.2 collective-permute-done.15.v_ref
  1464.5 72.5 %shard_map.101.u_ref = f32[768,5120]{1,0:T(8,128)} custom-call(s32[1]{0:T(128)} %bitcast.i_ref.refs_0_, bf16[768,3456]{1,0:T(8,128)(2,1)} %get-tuple-element.69.da_ref, bf16[768,3456]{1,0:T(8,128)(2,1)} %get-tuple-element.70.db_ref, bf16[5120,3456]{1,0:T(8,128)(2,1)} %get-tuple-element.55.wg_ref, bf16[5120,3456]{1,0:T(8,128)(2,1)} %get-tuple-element.56.wu_ref, ...), custom_call_target="tpu_custom_call" | custom-call | flops 54358179840 | bytes 89260032 | tf_op jit(solution)/shard_map/pallas_call | solution.py:46
  1537.0 38.9 %shard_map.99 = f32[768,5120]{1,0:T(8,128)} custom-call(s32[1]{0:T(128)} %bitcast.i_ref.refs_0_, bf16[768,3456]{1,0:T(8,128)(2,1)} %get-tuple-element.63.h_ref, bf16[3456,5120]{1,0:T(8,128)(2,1)} %get-tuple-element.60.w_ref.refs_2_, f32[768,5120]{1,0:T(8,128)} %collective-permute-done.7.rest_0_), custom_call_target="tpu_custom_call" | custom-call | flops 27179089920 | bytes 56426496 | tf_op jit(solution)/shard_map/pallas_call | solution.py:46
  1575.9 16.4 shard_map.104.u_ref
  1592.3 5.1 shard_map.109.rest_0_
  1597.4 5.1 shard_map.110.rest_0_
  1602.5 5.1 shard_map.111.rest_0_
  1607.7 5.1 shard_map.112
  1612.9 136.9 %shard_map.114 = f32[2560,3456]{1,0:T(8,128)} custom-call(s32[1]{0:T(128)} %bitcast.i_ref.refs_0_, bf16[3072,5120]{1,0:T(8,128)(2,1)} %get-tuple-element.96.x_ref, bf16[3072,5120]{1,0:T(8,128)(2,1)} %collective-permute-done.18.xo_ref, bf16[3072,3456]{1,0:T(8,128)(2,1)} %get-tuple-element.98.d_ref, bf16[3072,3456]{1,0:T(8,128)(2,1)} %collective-permute-done.20.do_ref), custom_call_target="tpu_custom_call" | custom-call | flops 108716359680 | bytes 105381888 | tf_op jit(solution)/shard_map/pallas_call | solution.py:46
  1749.8 136.9 %shard_map.113 = f32[2560,3456]{1,0:T(8,128)} custom-call(s32[1]{0:T(128)} %bitcast.i_ref.refs_0_, bf16[3072,5120]{1,0:T(8,128)(2,1)} %get-tuple-element.96.x_ref, bf16[3072,5120]{1,0:T(8,128)(2,1)} %collective-permute-done.18.xo_ref, bf16[3072,3456]{1,0:T(8,128)(2,1)} %get-tuple-element.97.d_ref, bf16[3072,3456]{1,0:T(8,128)(2,1)} %collective-permute-done.19.do_ref), custom_call_target="tpu_custom_call" | custom-call | flops 108716359680 | bytes 105381888 | tf_op jit(solution)/shard_map/pallas_call | solution.py:46
  1886.7 127.7 %shard_map.115 = f32[3456,2560]{1,0:T(8,128)} custom-call(s32[1]{0:T(128)} %bitcast.i_ref.refs_0_, bf16[3072,3456]{1,0:T(8,128)(2,1)} %get-tuple-element.99.h_ref, bf16[3072,3456]{1,0:T(8,128)(2,1)} %collective-permute-done.21.ho_ref, bf16[3072,5120]{1,0:T(8,128)(2,1)} %get-tuple-element.100.d_ref, bf16[3072,5120]{1,0:T(8,128)(2,1)} %collective-permute-done.22.do_ref), custom_call_target="tpu_custom_call" | custom-call | flops 108716359680 | bytes 105381888 | tf_op jit(solution)/shard_map/pallas_call | solution.py:46
  2014.3 21.6 %add_convert_fusion = bf16[768,5120]{1,0:T(8,128)(2,1)} fusion(f32[768,5120]{1,0:T(8,128)} %collective-permute-done.8, f32[768,5120]{1,0:T(8,128)} %collective-permute-done.4, f32[768,5120]{1,0:T(8,128)} %get-tuple-element.54, bf16[768,5120]{1,0:T(8,128)(2,1)} %x_ref.1), kind=kLoop, calls=%fused_computation | loop fusion | flops 19660800 | bytes 62914560 | tf_op jit(solution)/shard_map/convert_element_type | solution.py:435
  (39 shorter events, 17.9 us)
Async XLA Ops:
  0.6 260.5 %collective-permute-start = (bf16[2560,3456]{1,0:T(8,128)(2,1)}, bf16[2560,3456]{1,0:T(8,128)(2,1)}, u32[]{:S(2)}, u32[]{:S(2)}) collective-permute-start(bf16[2560,3456]{1,0:T(8,128)(2,1)} %wg_ref.1), channel_id=1, source_target_pairs={{0,1},{1,0},{2,3},{3,2},{4,5},{5,4},{6,7},{7,6}} | collective-permute-start | bytes 53084168 | tf_op jit(solution)/shard_map/ppermute | solution.py:390
  1.5 259.7 %collective-permute-start.1 = (bf16[2560,3456]{1,0:T(8,128)(2,1)}, bf16[2560,3456]{1,0:T(8,128)(2,1)}, u32[]{:S(2)}, u32[]{:S(2)}) collective-permute-start(bf16[2560,3456]{1,0:T(8,128)(2,1)} %wu_ref.1), channel_id=1, source_target_pairs={{0,1},{1,0},{2,3},{3,2},{4,5},{5,4},{6,7},{7,6}} | collective-permute-start | bytes 53084168 | tf_op jit(solution)/shard_map/ppermute | solution.py:390
  1.5 172.5 %collective-permute-start.5 = (bf16[768,5120]{1,0:T(8,128)(2,1)}, bf16[768,5120]{1,0:T(8,128)(2,1)}, u32[]{:S(2)}, u32[]{:S(2)}) collective-permute-start(bf16[768,5120]{1,0:T(8,128)(2,1)} %x_ref.1), channel_id=1, source_target_pairs={{0,4},{1,3},{2,6},{3,1},{4,0},{5,7},{6,2},{7,5}} | collective-permute-start | bytes 23592968 | tf_op jit(solution)/shard_map/ppermute | solution.py:387
  4.5 254.7 %collective-permute-start.11 = (bf16[768,5120]{1,0:T(8,128)(2,1)}, bf16[768,5120]{1,0:T(8,128)(2,1)}, u32[]{:S(2)}, u32[]{:S(2)}) collective-permute-start(bf16[768,5120]{1,0:T(8,128)(2,1)} %rest_0_.1), channel_id=1, source_target_pairs={{0,4},{1,3},{2,6},{3,1},{4,0},{5,7},{6,2},{7,5}} | collective-permute-start | bytes 23592968 | tf_op jit(solution)/shard_map/ppermute | solution.py:387
  4.5 329.1 %collective-permute-start.3 = (bf16[768,5120]{1,0:T(8,128)(2,1)}, bf16[768,5120]{1,0:T(8,128)(2,1)}, u32[]{:S(2)}, u32[]{:S(2)}) collective-permute-start(bf16[768,5120]{1,0:T(8,128)(2,1)} %x_ref.1), channel_id=1, source_target_pairs={{0,2},{1,5},{2,0},{3,7},{4,6},{5,1},{6,4},{7,3}} | collective-permute-start | bytes 23592968 | tf_op jit(solution)/shard_map/ppermute | solution.py:384
  174.1 297.5 %collective-permute-start.2 = (bf16[3456,2560]{1,0:T(8,128)(2,1)}, bf16[3456,2560]{1,0:T(8,128)(2,1)}, u32[]{:S(2)}, u32[]{:S(2)}) collective-permute-start(bf16[3456,2560]{1,0:T(8,128)(2,1)} %w_ref.1), channel_id=1, source_target_pairs={{0,1},{1,0},{2,3},{3,2},{4,5},{5,4},{6,7},{7,6}} | collective-permute-start | bytes 53084168 | tf_op jit(solution)/shard_map/ppermute | solution.py:390
  259.2 296.7 %collective-permute-start.9 = (bf16[768,5120]{1,0:T(8,128)(2,1)}, bf16[768,5120]{1,0:T(8,128)(2,1)}, u32[]{:S(2)}, u32[]{:S(2)}) collective-permute-start(bf16[768,5120]{1,0:T(8,128)(2,1)} %rest_0_.1), channel_id=1, source_target_pairs={{0,2},{1,5},{2,0},{3,7},{4,6},{5,1},{6,4},{7,3}} | collective-permute-start | bytes 23592968 | tf_op jit(solution)/shard_map/ppermute | solution.py:384
  261.2 379.6 %collective-permute-start.6 = (bf16[768,5120]{1,0:T(8,128)(2,1)}, bf16[768,5120]{1,0:T(8,128)(2,1)}, u32[]{:S(2)}, u32[]{:S(2)}) collective-permute-start(bf16[768,5120]{1,0:T(8,128)(2,1)} %collective-permute-done.5.x_ref), channel_id=1, source_target_pairs={{0,2},{1,5},{2,0},{3,7},{4,6},{5,1},{6,4},{7,3}} | collective-permute-start | bytes 23592968 | tf_op jit(solution)/shard_map/ppermute | solution.py:384
  261.2 448.7 %collective-permute-start.12 = (bf16[768,5120]{1,0:T(8,128)(2,1)}, bf16[768,5120]{1,0:T(8,128)(2,1)}, u32[]{:S(2)}, u32[]{:S(2)}) collective-permute-start(bf16[768,5120]{1,0:T(8,128)(2,1)} %collective-permute-done.11.refs_1_), channel_id=1, source_target_pairs={{0,2},{1,5},{2,0},{3,7},{4,6},{5,1},{6,4},{7,3}} | collective-permute-start | bytes 23592968 | tf_op jit(solution)/shard_map/ppermute | solution.py:384
  822.4 172.4 %collective-permute-start.13 = (f32[768,5120]{1,0:T(8,128)}, f32[768,5120]{1,0:T(8,128)}, u32[]{:S(2)}, u32[]{:S(2)}) collective-permute-start(f32[768,5120]{1,0:T(8,128)} %shard_map.107), channel_id=1, source_target_pairs={{0,2},{1,5},{2,0},{3,7},{4,6},{5,1},{6,4},{7,3}} | collective-permute-start | bytes 47185928 | tf_op jit(solution)/shard_map/ppermute | solution.py:384
  822.5 790.4 %collective-permute-start.18 = (bf16[3072,5120]{1,0:T(8,128)(2,1)}, bf16[3072,5120]{1,0:T(8,128)(2,1)}, u32[]{:S(2)}, u32[]{:S(2)}) collective-permute-start(bf16[3072,5120]{1,0:T(8,128)(2,1)} %get-tuple-element.96.x_ref), channel_id=1, source_target_pairs={{0,1},{1,0},{2,3},{3,2},{4,5},{5,4},{6,7},{7,6}} | collective-permute-start | bytes 94371848 | tf_op jit(solution)/shard_map/ppermute | solution.py:390
  892.7 312.9 %collective-permute-start.10 = (f32[768,5120]{1,0:T(8,128)}, f32[768,5120]{1,0:T(8,128)}, u32[]{:S(2)}, u32[]{:S(2)}) collective-permute-start(f32[768,5120]{1,0:T(8,128)} %shard_map.103), channel_id=1, source_target_pairs={{0,2},{1,5},{2,0},{3,7},{4,6},{5,1},{6,4},{7,3}} | collective-permute-start | bytes 47185928 | tf_op jit(solution)/shard_map/ppermute | solution.py:384
  932.9 483.3 %collective-permute-start.7 = (f32[768,5120]{1,0:T(8,128)}, f32[768,5120]{1,0:T(8,128)}, u32[]{:S(2)}, u32[]{:S(2)}) collective-permute-start(f32[768,5120]{1,0:T(8,128)} %shard_map.98), channel_id=1, source_target_pairs={{0,2},{1,5},{2,0},{3,7},{4,6},{5,1},{6,4},{7,3}} | collective-permute-start | bytes 47185928 | tf_op jit(solution)/shard_map/ppermute | solution.py:384
  932.9 679.9 %collective-permute-start.20 = (bf16[3072,3456]{1,0:T(8,128)(2,1)}, bf16[3072,3456]{1,0:T(8,128)(2,1)}, u32[]{:S(2)}, u32[]{:S(2)}) collective-permute-start(bf16[3072,3456]{1,0:T(8,128)(2,1)} %get-tuple-element.98.d_ref), channel_id=1, source_target_pairs={{0,1},{1,0},{2,3},{3,2},{4,5},{5,4},{6,7},{7,6}} | collective-permute-start | bytes 63701000 | tf_op jit(solution)/shard_map/ppermute | solution.py:390
  1097.8 320.7 %collective-permute-start.17 = (f32[192,5120]{1,0:T(8,128)}, f32[192,5120]{1,0:T(8,128)}, u32[]{:S(2)}, u32[]{:S(2)}) collective-permute-start(f32[192,5120]{1,0:T(8,128)} %get-tuple-element.95), channel_id=1, source_target_pairs={{0,4},{1,3},{2,6},{3,1},{4,0},{5,7},{6,2},{7,5}} | collective-permute-start | bytes 11796488 | tf_op jit(solution)/shard_map/ppermute | solution.py:387
  1205.5 213.0 %collective-permute-start.16 = (f32[192,5120]{1,0:T(8,128)}, f32[192,5120]{1,0:T(8,128)}, u32[]{:S(2)}, u32[]{:S(2)}) collective-permute-start(f32[192,5120]{1,0:T(8,128)} %get-tuple-element.94), channel_id=1, source_target_pairs={{0,4},{1,3},{2,6},{3,1},{4,0},{5,7},{6,2},{7,5}} | collective-permute-start | bytes 11796488 | tf_op jit(solution)/shard_map/ppermute | solution.py:387
  1416.2 46.3 %collective-permute-start.15 = (f32[192,5120]{1,0:T(8,128)}, f32[192,5120]{1,0:T(8,128)}, u32[]{:S(2)}, u32[]{:S(2)}) collective-permute-start(f32[192,5120]{1,0:T(8,128)} %get-tuple-element.93), channel_id=1, source_target_pairs={{0,4},{1,3},{2,6},{3,1},{4,0},{5,7},{6,2},{7,5}} | collective-permute-start | bytes 11796488 | tf_op jit(solution)/shard_map/ppermute | solution.py:387
  1418.5 468.2 %collective-permute-start.22 = (bf16[3072,5120]{1,0:T(8,128)(2,1)}, bf16[3072,5120]{1,0:T(8,128)(2,1)}, u32[]{:S(2)}, u32[]{:S(2)}) collective-permute-start(bf16[3072,5120]{1,0:T(8,128)(2,1)} %get-tuple-element.100.d_ref), channel_id=1, source_target_pairs={{0,1},{1,0},{2,3},{3,2},{4,5},{5,4},{6,7},{7,6}} | collective-permute-start | bytes 94371848 | tf_op jit(solution)/shard_map/ppermute | solution.py:390
  1418.5 331.3 %collective-permute-start.19 = (bf16[3072,3456]{1,0:T(8,128)(2,1)}, bf16[3072,3456]{1,0:T(8,128)(2,1)}, u32[]{:S(2)}, u32[]{:S(2)}) collective-permute-start(bf16[3072,3456]{1,0:T(8,128)(2,1)} %get-tuple-element.97.d_ref), channel_id=1, source_target_pairs={{0,1},{1,0},{2,3},{3,2},{4,5},{5,4},{6,7},{7,6}} | collective-permute-start | bytes 63701000 | tf_op jit(solution)/shard_map/ppermute | solution.py:390
  1462.5 74.5 %collective-permute-start.14 = (f32[192,5120]{1,0:T(8,128)}, f32[192,5120]{1,0:T(8,128)}, u32[]{:S(2)}, u32[]{:S(2)}) collective-permute-start(f32[192,5120]{1,0:T(8,128)} %get-tuple-element.92), channel_id=1, source_target_pairs={{0,4},{1,3},{2,6},{3,1},{4,0},{5,7},{6,2},{7,5}} | collective-permute-start | bytes 11796488 | tf_op jit(solution)/shard_map/ppermute | solution.py:387
  1537.0 349.7 %collective-permute-start.21 = (bf16[3072,3456]{1,0:T(8,128)(2,1)}, bf16[3072,3456]{1,0:T(8,128)(2,1)}, u32[]{:S(2)}, u32[]{:S(2)}) collective-permute-start(bf16[3072,3456]{1,0:T(8,128)(2,1)} %get-tuple-element.99.h_ref), channel_id=1, source_target_pairs={{0,1},{1,0},{2,3},{3,2},{4,5},{5,4},{6,7},{7,6}} | collective-permute-start | bytes 63701000 | tf_op jit(solution)/shard_map/ppermute | solution.py:390
  1612.8 401.5 %collective-permute-start.4 = (f32[768,5120]{1,0:T(8,128)}, f32[768,5120]{1,0:T(8,128)}, u32[]{:S(2)}, u32[]{:S(2)}) collective-permute-start(f32[768,5120]{1,0:T(8,128)} %shard_map.95), channel_id=1, source_target_pairs={{0,2},{1,5},{2,0},{3,7},{4,6},{5,1},{6,4},{7,3}} | collective-permute-start | bytes 47185928 | tf_op jit(solution)/shard_map/ppermute | solution.py:384
  1612.8 401.5 %collective-permute-start.8 = (f32[768,5120]{1,0:T(8,128)}, f32[768,5120]{1,0:T(8,128)}, u32[]{:S(2)}, u32[]{:S(2)}) collective-permute-start(f32[768,5120]{1,0:T(8,128)} %shard_map.99), channel_id=1, source_target_pairs={{0,4},{1,3},{2,6},{3,1},{4,0},{5,7},{6,2},{7,5}} | collective-permute-start | bytes 47185928 | tf_op jit(solution)/shard_map/ppermute | solution.py:387

commit v2 on v1

--- a/solution.py
+++ b/solution.py
@@ -169,73 +169,124 @@
     )
 
 
-def k_y0(core, h, wd, wdo, tn=512):
+def k_y2(core, h, wd, hr, ws, res=None, tn=512):
     r, f = h.shape
-    hd = wd.shape[1]
-    nt = hd // tn
-
-    def body(i_ref, h_ref, w_ref, wo_ref, o_ref, wc_ref, sem):
+    d = wd.shape[1]
+    ka = ws[0].shape[0]
+    nt = d // 2 // tn
+
+    def body(i_ref, h_ref, w_ref, hr_ref, *rest):
         n = pl.program_id(0)
         own = (n < nt) == (i_ref[0] == 0)
-
-        def part(w):
-            keep = pltpu.make_async_copy(w, wc_ref.at[:, pl.ds(pl.multiple_of(n * tn, 128), tn)], sem)
-            keep.start()
-
+        o_ref = rest[-1]
+
+        def part(ua, ub):
             def rows(m):
-                o_ref[m, :] = mm(h_ref[m, :], w[...])
+                v = mm(h_ref[m, :], w_ref[...]) + (mm(hr_ref[m, :ka], ua[...]) + mm(hr_ref[m, ka:], ub[...]))
+                if res is not None:
+                    v = (rest[4][m, :].astype(f32) + v + rest[5][m, :]).astype(bf)
+                o_ref[m, :] = v
 
             row_loop(r, 256, rows)
-            keep.wait()
 
         @pl.when(own)
         def _():
-            part(w_ref)
+            part(rest[0], rest[1])
 
         @pl.when(jnp.logical_not(own))
         def _():
-            part(wo_ref)
-
+            part(rest[2], rest[3])
+
+    o = spec((r, tn), lambda n, i: (0, n))
+    hs = spec((r, f), lambda n, i: (0, 0), True)
+
+    def part_spec(k, other):
+        return spec((k, tn), lambda n, i: (0, jnp.clip(n - ((1 - i[0]) if other else i[0]) * nt, 0, nt - 1)))
+
+    more = () if res is None else tuple(res)
     return call(
         body, core, (2 * nt,),
-        [spec((r, f), lambda n, i: (0, 0), True),
-         spec((f, tn), lambda n, i: (0, jnp.clip(n - i[0] * nt, 0, nt - 1))),
-         spec((f, tn), lambda n, i: (0, jnp.clip(n - (1 - i[0]) * nt, 0, nt - 1)))],
-        [(spec((r, tn), lambda n, i: (0, n)), (r, 2 * hd), f32), (ANY, (f, 2 * hd), bf)],
-        (h, wd, wdo), 4 * r * hd * f,
-        scratch=[pltpu.SemaphoreType.DMA],
+        [hs, spec((f, tn), lambda n, i: (0, n)), hs]
+        + [part_spec(ka, False), part_spec(f - ka, False), part_spec(ka, True), part_spec(f - ka, True)] + [o] * len(more),
+        [(o, (r, d), f32 if res is None else bf)], (h, wd, hr) + tuple(ws) + more, 4 * r * d * f,
+    )[0]
+
+
+def grads(g, a, b):
+    sig = jax.nn.sigmoid(a)
+    return (g * b * sig * (1.0 + a * (1.0 - sig))).astype(bf), (g * (a * sig)).astype(bf)
+
+
+def k_g0(core, dy, wd, wdo, a, b, tn=512):
+    r, d = dy.shape
+    f, hd = wd.shape
+    steps = pl.cdiv(f, tn)
+    last = f - (steps - 1) * tn
+
+    def body(i_ref, dy_ref, w_ref, wo_ref, a_ref, b_ref, daall_ref, dball_ref, dyall_ref, wc_ref, sem, wsem):
+        n = pl.program_id(0)
+        s = pl.multiple_of(i_ref[0] * hd, 128)
+        o = pl.multiple_of((1 - i_ref[0]) * hd, 128)
+        keep_dy = pltpu.make_async_copy(dy_ref, dyall_ref.at[pl.ds(0, r), :], sem)
+
+        def copies(height):
+            c = pl.ds(pl.multiple_of(n * tn, 128), height)
+            return [
+                pltpu.make_async_copy(u.at[pl.ds(0, height), :], wc_ref.at[c, pl.ds(q, hd)], wsem.at[k])
+                for k, (u, q) in enumerate(((w_ref, s), (wo_ref, o)))
+            ]
+
+        @pl.when(n == 0)
+        def _():
+            keep_dy.start()
+
+        @pl.when(n < steps - 1)
+        def _():
+            for c in copies(tn):
+                c.start()
+
+        @pl.when(n == steps - 1)
+        def _():
+            for c in copies(last):
+                c.start()
+
+        def rows(m):
+            g = dg(dy_ref[m, pl.ds(s, hd)], w_ref[...], NT) + dg(dy_ref[m, pl.ds(o, hd)], wo_ref[...], NT)
+            daall_ref[m, :], dball_ref[m, :] = grads(g, a_ref[m, :], b_ref[m, :])
+
+        row_loop(r, 256, rows)
+
+        @pl.when(n < steps - 1)
+        def _():
+            for c in copies(tn):
+                c.wait()
+
+        @pl.when(n == steps - 1)
+        def _():
+            for c in copies(last):
+                c.wait()
+            keep_dy.wait()
+
+    o = spec((r, tn), lambda n, i: (0, n))
+    w = spec((tn, hd), lambda n, i: (n, 0))
+    return call(
+        body, core, (steps,),
+        [spec((r, d), lambda n, i: (0, 0), True), w, w, o, o],
+        [(o, (4 * r, f), bf), (o, (4 * r, f), bf), (ANY, (4 * r, d), bf), (ANY, (f, d), bf)],
+        (dy, wd, wdo, a, b), 2 * r * d * f,
+        scratch=[pltpu.SemaphoreType.DMA, pltpu.SemaphoreType.DMA((2,))],
     )
 
 
-def k_y(core, h, wd, add=None, tn=512):
-    r, f = h.shape
-    d = wd.shape[1]
-
-    def body(i_ref, h_ref, w_ref, *rest):
-        def rows(m):
-            v = mm(h_ref[m, :], w_ref[...])
-            rest[-1][m, :] = v if add is None else v + rest[0][m, :]
-
-        row_loop(r, 256, rows)
-
-    o = spec((r, tn), lambda n, i: (0, n))
-    more = () if add is None else (add,)
-    return call(
-        body, core, (d // tn,),
-        [spec((r, f), lambda n, i: (0, 0), True), spec((f, tn), lambda n, i: (0, n))] + [o] * len(more),
-        [(o, (r, d), f32)], (h, wd) + more, 2 * r * d * f,
-    )[0]
-
-
-def k_g(core, slot, dy, wd, a, b, keep, tn=512):
+def k_g(core, slot, dy, wd, a, b, keep, after=(), tn=512):
     r, d = dy.shape
     f = wd.shape[0]
     steps = pl.cdiv(f, tn)
-    n_in = 5 + len(keep)
+    n_in = 8 + len(after)
 
     def body(*refs):
         _, dy_ref, w_ref, a_ref, b_ref = refs[:5]
-        da_ref, db_ref, daall_ref, dball_ref, dyall_ref, sem = refs[n_in:]
+        daall_ref, dball_ref, dyall_ref, sem = refs[n_in:]
         n = pl.program_id(0)
         keep_dy = pltpu.make_async_copy(dy_ref, dyall_ref.at[pl.ds(slot * r, r), :], sem)
 
@@ -245,15 +296,7 @@
 
         def rows(m):
             g = dg(dy_ref[m, :], w_ref[...], NT)
-            a = a_ref[m, :]
-            b = b_ref[m, :]
-            sig = jax.nn.sigmoid(a)
-            da = (g * b * sig * (1.0 + a * (1.0 - sig))).astype(bf)
-            db = (g * (a * sig)).astype(bf)
-            da_ref[m, :] = da
-            db_ref[m, :] = db
-            daall_ref[m, :] = da
-            dball_ref[m, :] = db
+            daall_ref[m, :], dball_ref[m, :] = grads(g, a_ref[m, :], b_ref[m, :])
 
         row_loop(r, 256, rows)
 
@@ -265,40 +308,33 @@
     oall = spec((r, tn), lambda n, i: (slot, n))
     return call(
         body, core, (steps,),
-        [spec((r, d), lambda n, i: (0, 0), True), spec((tn, d), lambda n, i: (n, 0)), o, o] + [ANY] * len(keep),
-        [(o, (r, f), bf), (o, (r, f), bf), (oall, (4 * r, f), bf), (oall, (4 * r, f), bf), (ANY, (4 * r, d), bf)],
-        (dy, wd, a, b) + tuple(keep), 2 * r * d * f,
-        scratch=[pltpu.SemaphoreType.DMA], aliases={5: 2, 6: 3, 7: 4} if keep else None,
+        [spec((r, d), lambda n, i: (0, 0), True), spec((tn, d), lambda n, i: (n, 0)), o, o] + [ANY] * (3 + len(after)),
+        [(oall, (4 * r, f), bf), (oall, (4 * r, f), bf), (ANY, (4 * r, d), bf)],
+        (dy, wd, a, b) + tuple(keep) + tuple(after), 2 * r * d * f,
+        scratch=[pltpu.SemaphoreType.DMA], aliases={5: 0, 6: 1, 7: 2},
     )
 
 
-def k_dx(core, da, db, wg, wu, add=None, pieces=1, tn=512):
-    r, f = da.shape
+def k_dx(core, slot, daall, dball, wg, wu, add=None, tn=512):
+    f = daall.shape[1]
+    r = daall.shape[0] // 4
     d = wg.shape[0]
-    rp = r // pieces
     more = () if add is None else (add,)
 
     def body(i_ref, da_ref, db_ref, wg_ref, wu_ref, *rest):
-        outs = rest[len(more):]
-
-        def rows(m, o_ref, mo):
+        def rows(m):
             v = dg(da_ref[m, :], wg_ref[...], NT) + dg(db_ref[m, :], wu_ref[...], NT)
-            o_ref[mo, :] = v if add is None else v + rest[0][m, :].astype(f32)
-
-        if pieces == 1:
-            row_loop(r, 256, lambda m: rows(m, outs[0], m))
-        else:
-            for p in range(pieces):
-                rows(slice(p * rp, (p + 1) * rp), outs[p], slice(0, rp))
+            rest[-1][m, :] = v if add is None else v + rest[0][m, :].astype(f32)
+
+        row_loop(r, 256, rows)
 
     w = spec((tn, f), lambda n, i: (n, 0))
-    hs = spec((r, f), lambda n, i: (0, 0), True)
-    return call(
-        body, core, (d // tn,),
-        [hs, hs, w, w] + [spec((r, tn), lambda n, i: (0, n))] * len(more),
-        [(spec((rp, tn), lambda n, i: (0, n)), (rp, d), f32)] * pieces,
-        (da, db, wg, wu) + more, 4 * r * d * f,
-    )
+    hs = spec((r, f), lambda n, i: (slot(i[0]), 0), True)
+    o = spec((r, tn), lambda n, i: (0, n))
+    return call(
+        body, core, (d // tn,), [hs, hs, w, w] + [o] * len(more),
+        [(o, (r, d), f32)], (daall, dball, wg, wu) + more, 4 * r * d * f,
+    )[0]
 
 
 def k_dw(core, x, xo, d, do, tm=1280, tn=512):
@@ -339,14 +375,18 @@
     )[0]
 
 
-def k_add(core, u, v, tr=96):
+def k_add(core, u, v, pieces=1, tn=512):
     r, d = u.shape
-
-    def body(i_ref, u_ref, v_ref, o_ref):
-        o_ref[...] = u_ref[...] + v_ref[...]
-
-    o = spec((tr, d), lambda n, i: (n, 0))
-    return call(body, core, (r // tr,), [o, o], [(o, (r, d), f32)], (u, v), r * d)[0]
+    rp = r // pieces
+
+    def body(i_ref, u_ref, v_ref, *outs):
+        for p, o_ref in enumerate(outs):
+            m = slice(p * rp, (p + 1) * rp)
+            o_ref[...] = u_ref[m, :] + v_ref[m, :]
+
+    s = spec((r, tn), lambda n, i: (0, n))
+    o = spec((rp, tn), lambda n, i: (0, n))
+    return call(body, core, (d // tn,), [s, s], [(o, (rp, d), f32)] * pieces, (u, v), r * d)
 
 
 def k_fin(core, p, u, v, keep, tr=64):
@@ -370,61 +410,48 @@
     dsp = P("tp", "dp")
     axes = ("tp", "dp")
 
-    def pairs(first):
-        out = []
-        for j in range(ny):
-            for c in range(2):
-                bit = 1 if (c == 0) == first else 2
-                out.append((j * 2 + c, (j ^ bit) * 2 + c))
-        return out
-
-    p1, p2 = pairs(True), pairs(False)
-
-    def to1(v):
-        return lax.ppermute(v, axes, p1)
-
-    def to2(v):
-        return lax.ppermute(v, axes, p2)
+    def hop(v, bit0, bit1):
+        pairs = [(j * 2 + c, (j ^ b) * 2 + c) for j in range(ny) for c, b in enumerate((bit0, bit1))]
+        return lax.ppermute(v, axes, pairs)
 
     def swap(v):
         return lax.ppermute(v, "dp", [(0, 1), (1, 0)])
 
     def layer(x, wg, wu, wd, dy):
         i = lax.axis_index("dp").astype(jnp.int32).reshape(1)
-        x1, x2 = to1(x), to2(x)
-        dy2 = to2(dy)
+        ka = 1792
+        qa = 304
+        xX, xY = hop(x, 1, 1), hop(x, 2, 2)
+        dyX, dyY = hop(dy, 1, 1), hop(dy, 2, 2)
         wgo, wuo, wdo = swap(wg), swap(wu), swap(wd)
-        xd = to1(x2)
-        dy1 = to1(dy)
-        dyd = to1(dy2)
+        wXa, wXb = hop(wd[:ka], 1, 1), hop(wd[ka:], 1, 1)
+        xD = hop(xX, 2, 2)
+        dyDa = hop(jnp.where(i[0] == 0, dyY[:qa], dyX[:qa]), 1, 2)
+        dyDb = hop(dyX[qa:], 2, 2)
+        dyD = jnp.concatenate([dyDa, dyDb], axis=0)
+        wX = (wXa, wXb, swap(wXa), swap(wXb))
 
         a0, b0, h0, hall, xall, wgc, wuc = k_fwd0(i, x, wg, wgo, wu, wuo)
-        y0, wdc = k_y0(i, h0, wd, wdo)
-        a1, b1, h1, hall, xall = k_fwd(i, 1, x1, wgc, wuc, hall, xall)
-        a2, b2, h2, hall, xall = k_fwd(i, 2, x2, wgc, wuc, hall, xall)
-        a3, b3, h3, hall, xall = k_fwd(i, 3, xd, wgc, wuc, hall, xall)
-        y1 = k_y(i, h1, wdc)
-        y3 = k_y(i, h3, wdc)
-        ra = to1(y3)
-        r1 = to1(y1)
-        y2 = k_y(i, h2, wdc, ra)
-        r2 = to2(y2)
-
-        def bwd(slot, v, a, b, keep):
-            return k_g(i, slot, v, wdc, a, b, keep)
-
-        da0, db0, *alls = bwd(0, dy, a0, b0, ())
-        da1, db1, *alls = bwd(1, dy1, a1, b1, alls)
-        da2, db2, *alls = bwd(2, dy2, a2, b2, alls)
-        da3, db3, *alls = bwd(3, dyd, a3, b3, alls)
-        daall, dball, dyall = alls
-        z0 = k_dx(i, da0, db0, wgc, wuc, add=dy)[0]
-        z1 = k_dx(i, da1, db1, wgc, wuc)[0]
-        z3 = k_dx(i, da3, db3, wgc, wuc)[0]
-        sa = to1(z3)
-        s1 = to1(z1)
-        z2 = k_dx(i, da2, db2, wgc, wuc, add=sa, pieces=4)
-        s2 = [to2(z2[p]) for p in range(4)]
+        *alls, wdc = k_g0(i, dy, wd, wdo, a0, b0)
+        a1, b1, h1, hall, xall = k_fwd(i, 1, xX, wgc, wuc, hall, xall)
+        a2, b2, h2, hall, xall = k_fwd(i, 2, xY, wgc, wuc, hall, xall)
+        a3, b3, h3, hall, xall = k_fwd(i, 3, xD, wgc, wuc, hall, xall)
+
+        alls = k_g(i, 1, dyX, wdc, a1, b1, alls)
+        alls = k_g(i, 2, dyY, wdc, a2, b2, alls)
+        z1 = k_dx(i, lambda c: 1 + c, alls[0], alls[1], wgc, wuc)
+        s1 = hop(z1, 1, 2)
+        z0 = k_dx(i, lambda c: 0, alls[0], alls[1], wgc, wuc, add=dy)
+        daall, dball, dyall = k_g(i, 3, dyD, wdc, a3, b3, alls, (z0, z1))
+        z3 = k_dx(i, lambda c: 3, daall, dball, wgc, wuc)
+        sa = hop(z3, 1, 2)
+        z2 = k_dx(i, lambda c: 2 - c, daall, dball, wgc, wuc)
+        s2 = k_add(i, z2, sa, pieces=4)
+        s2 = [hop(s2[p], 2, 1) for p in range(4)]
+
+        hDr, hXr = hop(h3, 1, 1), hop(h1, 1, 1)
+        yYr = hop(k_y2(i, h2, wdc, hDr, wX), 2, 2)
+        y = k_y2(i, h0, wdc, hXr, wX, (x, yYr))
 
         xallo, hallo = swap(xall), swap(hall)
         dyallo, daallo, dballo = swap(dyall), swap(daall), swap(dball)
@@ -432,8 +459,7 @@
         dwg = k_dw(i, xall, xallo, daall, daallo)
         dwu = k_dw(i, xall, xallo, dball, dballo)
 
-        y = (x.astype(f32) + y0 + r1 + r2).astype(bf)
-        pre = k_add(i, z0, s1)
+        pre = k_add(i, z0, s1)[0]
         dx = ()
         for p in range(4):
             dx = (k_fin(i, p, pre, s2[p], dx),)

time: 2040 us -> 2930 us (1.44)
  waiting for transfers between devices: 634 us -> 1370 us
  starting transfers between devices: 20.8 us -> 202 us
  Pallas kernels: 1360 us -> 1330 us
    ppermute x15 -> x18, waiting for transfers between devices: 634 us -> 1360 us  [hop(): return lax.ppermute(v, axes, pairs)]
    ppermute x8 -> x10, starting transfers between devices: 1.62 us -> 181 us  [swap(): return lax.ppermute(v, 'dp', [(0, 1), (1, 0)])]
    pallas_call x24 -> x23, Pallas kernels: 1360 us -> 1330 us  [call(): pl.pallas_call(body, grid_spec=pltpu.PrefetchScalarGridSpec(num_scalar_pr...]
  transfers between devices with their start and end apart: 23 -> 28, of which waited for: 6 -> 10; matrix products, arithmetic and copies ran while one was open for 0% -> 1% of each run, Pallas kernels for 61% -> 41%
where the time goes in v2:
time: 2930 us
  waiting for transfers between devices  1370 us (47%)
  Pallas kernels  1330 us (45%)
  starting transfers between devices  202 us (7%)
    ppermute x18, waiting for transfers between devices, hop(): return lax.ppermute(v, axes, pairs)  1360 us
    pallas_call x23, Pallas kernels, call(): pl.pallas_call(body, grid_spec=pltpu.PrefetchScalarGridSpec(num_scalar_pr...  1330 us
    ppermute x10, starting transfers between devices, swap(): return lax.ppermute(v, 'dp', [(0, 1), (1, 0)])  181 us
  transfers between devices with their start and end apart: 28, of which 10 were waited for; matrix products, arithmetic and copies ran while one was open for 1% of the time, Pallas kernels for 41%

profile of v2, /device:TPU:0, one launch (start us, length us, event | category | flops | bytes accessed | tf_op | source)
XLA Modules:
  0.0 2931.8 jit_solution(16227380464500407843)
XLA Ops:
  6.0 167.5 %collective-permute-done.14.refs_1_ = bf16[768,5120]{1,0:T(8,128)(2,1)} collective-permute-done((bf16[768,5120]{1,0:T(8,128)(2,1)}, bf16[768,5120]{1,0:T(8,128)(2,1)}, u32[]{:S(2)}, u32[]{:S(2)}) %collective-permute-start.14) | collective-permute-done | bytes 7864352 | tf_op jit(solution)/shard_map/ppermute | solution.py:415
  184.2 7.5 slice.16
  191.7 28.3 collective-permute-done.16
  221.5 60.2 %collective-permute-done.17 = bf16[464,5120]{1,0:T(8,128)(2,1)} collective-permute-done((bf16[464,5120]{1,0:T(8,128)(2,1)S(1)}, bf16[464,5120]{1,0:T(8,128)(2,1)}, u32[]{:S(2)}, u32[]{:S(2)}) %collective-permute-start.17) | collective-permute-done | bytes 4751392 | tf_op jit(solution)/shard_map/ppermute | solution.py:415
  283.4 7.8 slice.15
  298.2 184.3 %collective-permute-done.3.x_ref = bf16[768,5120]{1,0:T(8,128)(2,1)} collective-permute-done((bf16[768,5120]{1,0:T(8,128)(2,1)}, bf16[768,5120]{1,0:T(8,128)(2,1)}, u32[]{:S(2)}, u32[]{:S(2)}) %collective-permute-start.3) | collective-permute-done | bytes 7864352 | tf_op jit(solution)/shard_map/ppermute | solution.py:415
  486.0 180.3 %collective-permute-start.8 = (bf16[1664,2560]{1,0:T(8,128)(2,1)}, bf16[1664,2560]{1,0:T(8,128)(2,1)}, u32[]{:S(2)}, u32[]{:S(2)}) collective-permute-start(bf16[1664,2560]{1,0:T(8,128)(2,1)} %collective-permute-done.6.rest_1_), channel_id=1, source_target_pairs={{0,1},{1,0},{2,3},{3,2},{4,5},{5,4},{6,7},{7,6}} | collective-permute-start | bytes 25559048 | tf_op jit(solution)/shard_map/ppermute | solution.py:418
  666.3 70.3 %shard_map.92 = (f32[768,3456]{1,0:T(8,128)}, f32[768,3456]{1,0:T(8,128)}, bf16[768,3456]{1,0:T(8,128)(2,1)}, bf16[3072,3456]{1,0:T(8,128)(2,1)}, bf16[3072,5120...) custom-call(s32[1]{0:T(128)} %bitcast.i_ref.refs_0_, bf16[768,5120]{1,0:T(8,128)(2,1)} %rest_4_.1, ...), custom_call_target="tpu_custom_call" | custom-call | flops 54358179840 | bytes 78643200 | tf_op jit(solution)/shard_map/pallas_call | solution.py:46
  736.7 44.3 %shard_map.93 = (bf16[3072,3456]{1,0:T(8,128)(2,1)}, bf16[3072,3456]{1,0:T(8,128)(2,1)}, bf16[3072,5120]{1,0:T(8,128)(2,1)}, bf16[3456,5120]{1,0:T(8,128)(2,1)}) custom-call(s32[1]{0:T(128)} %bitcast.i_ref.refs_0_, bf16[768,5120]{1,0:T(8,128)(2,1)} %rest_0_.1, bf16[3456,2560]{1,0:T(8,128)(2,1)} %w_ref.1, bf16[3456,2560]{1,0:T(8,128)(2,1)} %collective-permute-done.2.wo_ref, ...), custom_call_target="tpu_custom_call" | custom-call | flops 27179089920 | bytes 64487424 | tf_op jit(solution)/shard_map/pallas_call | solution.py:46
  781.0 68.9 %shard_map.94 = (f32[768,3456]{1,0:T(8,128)}, f32[768,3456]{1,0:T(8,128)}, bf16[768,3456]{1,0:T(8,128)(2,1)}, bf16[3072,3456]{1,0:T(8,128)(2,1)}, bf16[3072,5120]{1,0:T(8,128)(2,1)}) custom-call(s32[1]{0:T(128)} %bitcast.i_ref.refs_0_, bf16[768,5120]{1,0:T(8,128)(2,1)} %collective-permute-done.3.x_ref, ...), custom_call_target="tpu_custom_call", output_to_operand_aliasing={{3}: (4, {}), {4}: (5, {})} | custom-call | flops 54358179840 | bytes 131334144 | tf_op jit(solution)/shard_map/pallas_call | solution.py:46
  850.0 68.9 %shard_map.95 = (f32[768,3456]{1,0:T(8,128)}, f32[768,3456]{1,0:T(8,128)}, bf16[768,3456]{1,0:T(8,128)(2,1)}, bf16[3072,3456]{1,0:T(8,128)(2,1)}, bf16[3072,5120]{1,0:T(8,128)(2,1)}) custom-call(s32[1]{0:T(128)} %bitcast.i_ref.refs_0_, bf16[768,5120]{1,0:T(8,128)(2,1)} %collective-permute-done.9.x_ref, ...), custom_call_target="tpu_custom_call", output_to_operand_aliasing={{3}: (4, {}), {4}: (5, {})} | custom-call | flops 54358179840 | bytes 131334144 | tf_op jit(solution)/shard_map/pallas_call | solution.py:46
  918.9 41.8 %shard_map.99 = (bf16[3072,3456]{1,0:T(8,128)(2,1)}, bf16[3072,3456]{1,0:T(8,128)(2,1)}, bf16[3072,5120]{1,0:T(8,128)(2,1)}) custom-call(s32[1]{0:T(128)} %bitcast.i_ref.refs_0_, bf16[768,5120]{1,0:T(8,128)(2,1)} %collective-permute-done.14.refs_1_, ...), custom_call_target="tpu_custom_call", output_to_operand_aliasing={{0}: (5, {}), {1}: (6, {}), {2}: (7, {})} | custom-call | flops 27179089920 | bytes 138412032 | tf_op jit(solution)/shard_map/pallas_call | solution.py:46
  960.7 41.9 %shard_map.100 = (bf16[3072,3456]{1,0:T(8,128)(2,1)}, bf16[3072,3456]{1,0:T(8,128)(2,1)}, bf16[3072,5120]{1,0:T(8,128)(2,1)}) custom-call(s32[1]{0:T(128)} %bitcast.i_ref.refs_0_, bf16[768,5120]{1,0:T(8,128)(2,1)} %collective-permute-done.13.refs_1_, ...), custom_call_target="tpu_custom_call", output_to_operand_aliasing={{0}: (5, {}), {1}: (6, {}), {2}: (7, {})} | custom-call | flops 27179089920 | bytes 138412032 | tf_op jit(solution)/shard_map/pallas_call | solution.py:46
  1002.6 70.2 %shard_map.102.refs_9_ = f32[768,5120]{1,0:T(8,128)} custom-call(s32[1]{0:T(128)} %bitcast.i_ref.refs_0_, bf16[3072,3456]{1,0:T(8,128)(2,1)} %get-tuple-element.69.da_ref.refs_5_, bf16[3072,3456]{1,0:T(8,128)(2,1)} %get-tuple-element.70.db_ref.refs_6_, bf16[5120,3456]{1,0:T(8,128)(2,1)} %get-tuple-element.48.wg_ref, bf16[5120,3456]{1,0:T(8,128)(2,1)} %get-tuple-element.49.wu_ref), custom_call_target="tpu_custom_call" | custom-call | flops 54358179840 | bytes 113246208 | tf_op jit(solution)/shard_map/pallas_call | solution.py:46
  1072.8 72.7 %shard_map.101.u_ref.refs_8_ = f32[768,5120]{1,0:T(8,128)} custom-call(s32[1]{0:T(128)} %bitcast.i_ref.refs_0_, bf16[3072,3456]{1,0:T(8,128)(2,1)} %get-tuple-element.69.da_ref.refs_5_, bf16[3072,3456]{1,0:T(8,128)(2,1)} %get-tuple-element.70.db_ref.refs_6_, bf16[5120,3456]{1,0:T(8,128)(2,1)} %get-tuple-element.48.wg_ref, ...), custom_call_target="tpu_custom_call" | custom-call | flops 54358179840 | bytes 121110528 | tf_op jit(solution)/shard_map/pallas_call | solution.py:46
  1145.6 68.9 %shard_map.96 = (f32[768,3456]{1,0:T(8,128)}, f32[768,3456]{1,0:T(8,128)}, bf16[768,3456]{1,0:T(8,128)(2,1)}, bf16[3072,3456]{1,0:T(8,128)(2,1)}, bf16[3072,5120]{1,0:T(8,128)(2,1)}) custom-call(s32[1]{0:T(128)} %bitcast.i_ref.refs_0_, bf16[768,5120]{1,0:T(8,128)(2,1)} %collective-permute-done.10.x_ref, ...), custom_call_target="tpu_custom_call", output_to_operand_aliasing={{3}: (4, {}), {4}: (5, {})} | custom-call | flops 54358179840 | bytes 131334144 | tf_op jit(solution)/shard_map/pallas_call | solution.py:46
  1214.5 41.8 %shard_map.104 = (bf16[3072,3456]{1,0:T(8,128)(2,1)}, bf16[3072,3456]{1,0:T(8,128)(2,1)}, bf16[3072,5120]{1,0:T(8,128)(2,1)}) custom-call(s32[1]{0:T(128)} %bitcast.i_ref.refs_0_, bf16[768,5120]{1,0:T(8,128)(2,1)} %pad_maximum_fusion.refs_1_, ...), custom_call_target="tpu_custom_call", output_to_operand_aliasing={{0}: (5, {}), {1}: (6, {}), {2}: (7, {})} | custom-call | flops 27179089920 | bytes 169869312 | tf_op jit(solution)/shard_map/pallas_call | solution.py:46
  1256.3 70.1 %shard_map.106 = f32[768,5120]{1,0:T(8,128)} custom-call(s32[1]{0:T(128)} %bitcast.i_ref.refs_0_, bf16[3072,3456]{1,0:T(8,128)(2,1)} %get-tuple-element.74.da_ref.d_ref, bf16[3072,3456]{1,0:T(8,128)(2,1)} %get-tuple-element.75.db_ref.d_ref, bf16[5120,3456]{1,0:T(8,128)(2,1)} %get-tuple-element.48.wg_ref, bf16[5120,3456]{1,0:T(8,128)(2,1)} %get-tuple-element.49.wu_ref), custom_call_target="tpu_custom_call" | custom-call | flops 54358179840 | bytes 113246208 | tf_op jit(solution)/shard_map/pallas_call | solution.py:46
  1329.1 12.6 collective-permute-done.7.rest_2_
  1341.8 664.8 %collective-permute-done.11.hr_ref = bf16[768,3456]{1,0:T(8,128)(2,1)} collective-permute-done((bf16[768,3456]{1,0:T(8,128)(2,1)}, bf16[768,3456]{1,0:T(8,128)(2,1)}, u32[]{:S(2)}, u32[]{:S(2)}) %collective-permute-start.11) | collective-permute-done | bytes 5308448 | tf_op jit(solution)/shard_map/ppermute | solution.py:415
  2007.1 71.4 %shard_map.97 = f32[768,5120]{1,0:T(8,128)} custom-call(s32[1]{0:T(128)} %bitcast.i_ref.refs_0_, bf16[768,3456]{1,0:T(8,128)(2,1)} %get-tuple-element.55.h_ref, bf16[3456,5120]{1,0:T(8,128)(2,1)} %get-tuple-element.47.w_ref.refs_2_, bf16[768,3456]{1,0:T(8,128)(2,1)} %collective-permute-done.11.hr_ref, bf16[1792,2560]{1,0:T(8,128)(2,1)} %collective-permute-done.5.rest_0_, ...), custom_call_target="tpu_custom_call" | custom-call | flops 54358179840 | bytes 81395712 | tf_op jit(solution)/shard_map/pallas_call | solution.py:46
  2078.8 70.2 %shard_map.105.u_ref = f32[768,5120]{1,0:T(8,128)} custom-call(s32[1]{0:T(128)} %bitcast.i_ref.refs_0_, bf16[3072,3456]{1,0:T(8,128)(2,1)} %get-tuple-element.74.da_ref.d_ref, bf16[3072,3456]{1,0:T(8,128)(2,1)} %get-tuple-element.75.db_ref.d_ref, bf16[5120,3456]{1,0:T(8,128)(2,1)} %get-tuple-element.48.wg_ref, bf16[5120,3456]{1,0:T(8,128)(2,1)} %get-tuple-element.49.wu_ref), custom_call_target="tpu_custom_call" | custom-call | flops 54358179840 | bytes 113246208 | tf_op jit(solution)/shard_map/pallas_call | solution.py:46
  2149.0 17.4 shard_map.107
  2168.5 124.6 %collective-permute-done.22.v_ref = f32[192,5120]{1,0:T(8,128)} collective-permute-done((f32[192,5120]{1,0:T(8,128)}, f32[192,5120]{1,0:T(8,128)}, u32[]{:S(2)}, u32[]{:S(2)}) %collective-permute-start.22) | collective-permute-done | bytes 3932192 | tf_op jit(solution)/shard_map/ppermute | solution.py:415
  2293.4 41.8 %collective-permute-done.21.v_ref = f32[192,5120]{1,0:T(8,128)} collective-permute-done((f32[192,5120]{1,0:T(8,128)}, f32[192,5120]{1,0:T(8,128)}, u32[]{:S(2)}, u32[]{:S(2)}) %collective-permute-start.21) | collective-permute-done | bytes 3932192 | tf_op jit(solution)/shard_map/ppermute | solution.py:415
  2335.5 41.8 %collective-permute-done.20.v_ref = f32[192,5120]{1,0:T(8,128)} collective-permute-done((f32[192,5120]{1,0:T(8,128)}, f32[192,5120]{1,0:T(8,128)}, u32[]{:S(2)}, u32[]{:S(2)}) %collective-permute-start.20) | collective-permute-done | bytes 3932192 | tf_op jit(solution)/shard_map/ppermute | solution.py:415
  2377.3 42.1 %collective-permute-done.19.v_ref = f32[192,5120]{1,0:T(8,128)} collective-permute-done((f32[192,5120]{1,0:T(8,128)}, f32[192,5120]{1,0:T(8,128)}, u32[]{:S(2)}, u32[]{:S(2)}) %collective-permute-start.19) | collective-permute-done | bytes 3932192 | tf_op jit(solution)/shard_map/ppermute | solution.py:415
  2419.5 17.4 shard_map.103.u_ref
  2457.9 72.3 %shard_map.98 = bf16[768,5120]{1,0:T(8,128)(2,1)} custom-call(s32[1]{0:T(128)} %bitcast.i_ref.refs_0_, bf16[768,3456]{1,0:T(8,128)(2,1)} %get-tuple-element.44.h_ref, bf16[3456,5120]{1,0:T(8,128)(2,1)} %get-tuple-element.47.w_ref.refs_2_, bf16[768,3456]{1,0:T(8,128)(2,1)} %collective-permute-done.4.hr_ref, ...), custom_call_target="tpu_custom_call" | custom-call | flops 54358179840 | bytes 104988672 | tf_op jit(solution)/shard_map/pallas_call | solution.py:46
  2530.3 136.9 %shard_map.113 = f32[2560,3456]{1,0:T(8,128)} custom-call(s32[1]{0:T(128)} %bitcast.i_ref.refs_0_, bf16[3072,5120]{1,0:T(8,128)(2,1)} %get-tuple-element.80.x_ref, bf16[3072,5120]{1,0:T(8,128)(2,1)} %collective-permute-done.23.xo_ref, bf16[3072,3456]{1,0:T(8,128)(2,1)} %get-tuple-element.75.db_ref.d_ref, bf16[3072,3456]{1,0:T(8,128)(2,1)} %collective-permute-done.25.do_ref), custom_call_target="tpu_custom_call" | custom-call | flops 108716359680 | bytes 105381888 | tf_op jit(solution)/shard_map/pallas_call | solution.py:46
  2667.2 136.9 %shard_map.112 = f32[2560,3456]{1,0:T(8,128)} custom-call(s32[1]{0:T(128)} %bitcast.i_ref.refs_0_, bf16[3072,5120]{1,0:T(8,128)(2,1)} %get-tuple-element.80.x_ref, bf16[3072,5120]{1,0:T(8,128)(2,1)} %collective-permute-done.23.xo_ref, bf16[3072,3456]{1,0:T(8,128)(2,1)} %get-tuple-element.74.da_ref.d_ref, bf16[3072,3456]{1,0:T(8,128)(2,1)} %collective-permute-done.24.do_ref), custom_call_target="tpu_custom_call" | custom-call | flops 108716359680 | bytes 105381888 | tf_op jit(solution)/shard_map/pallas_call | solution.py:46
  2804.1 127.7 %shard_map.114 = f32[3456,2560]{1,0:T(8,128)} custom-call(s32[1]{0:T(128)} %bitcast.i_ref.refs_0_, bf16[3072,3456]{1,0:T(8,128)(2,1)} %get-tuple-element.81.h_ref, bf16[3072,3456]{1,0:T(8,128)(2,1)} %collective-permute-done.26.ho_ref, bf16[3072,5120]{1,0:T(8,128)(2,1)} %get-tuple-element.82.d_ref, bf16[3072,5120]{1,0:T(8,128)(2,1)} %collective-permute-done.27.do_ref), custom_call_target="tpu_custom_call" | custom-call | flops 108716359680 | bytes 105381888 | tf_op jit(solution)/shard_map/pallas_call | solution.py:46
  (52 shorter events, 57.3 us)
Async XLA Ops:
  0.6 172.9 %collective-permute-start.14 = (bf16[768,5120]{1,0:T(8,128)(2,1)}, bf16[768,5120]{1,0:T(8,128)(2,1)}, u32[]{:S(2)}, u32[]{:S(2)}) collective-permute-start(bf16[768,5120]{1,0:T(8,128)(2,1)} %rest_0_.1), channel_id=1, source_target_pairs={{0,2},{1,3},{2,0},{3,1},{4,6},{5,7},{6,4},{7,5}} | collective-permute-start | bytes 23592968 | tf_op jit(solution)/shard_map/ppermute | solution.py:415
  4.0 174.0 %collective-permute-start.13 = (bf16[768,5120]{1,0:T(8,128)(2,1)}, bf16[768,5120]{1,0:T(8,128)(2,1)}, u32[]{:S(2)}, u32[]{:S(2)}) collective-permute-start(bf16[768,5120]{1,0:T(8,128)(2,1)} %rest_0_.1), channel_id=1, source_target_pairs={{0,4},{1,5},{2,6},{3,7},{4,0},{5,1},{6,2},{7,3}} | collective-permute-start | bytes 23592968 | tf_op jit(solution)/shard_map/ppermute | solution.py:415
  5.5 478.5 %collective-permute-start = (bf16[2560,3456]{1,0:T(8,128)(2,1)}, bf16[2560,3456]{1,0:T(8,128)(2,1)}, u32[]{:S(2)}, u32[]{:S(2)}) collective-permute-start(bf16[2560,3456]{1,0:T(8,128)(2,1)} %wg_ref.1), channel_id=1, source_target_pairs={{0,1},{1,0},{2,3},{3,2},{4,5},{5,4},{6,7},{7,6}} | collective-permute-start | bytes 53084168 | tf_op jit(solution)/shard_map/ppermute | solution.py:418
  5.5 480.6 %collective-permute-start.1 = (bf16[2560,3456]{1,0:T(8,128)(2,1)}, bf16[2560,3456]{1,0:T(8,128)(2,1)}, u32[]{:S(2)}, u32[]{:S(2)}) collective-permute-start(bf16[2560,3456]{1,0:T(8,128)(2,1)} %wu_ref.1), channel_id=1, source_target_pairs={{0,1},{1,0},{2,3},{3,2},{4,5},{5,4},{6,7},{7,6}} | collective-permute-start | bytes 53084168 | tf_op jit(solution)/shard_map/ppermute | solution.py:418
  6.0 730.7 %collective-permute-start.2 = (bf16[3456,2560]{1,0:T(8,128)(2,1)}, bf16[3456,2560]{1,0:T(8,128)(2,1)}, u32[]{:S(2)}, u32[]{:S(2)}) collective-permute-start(bf16[3456,2560]{1,0:T(8,128)(2,1)} %w_ref.1), channel_id=1, source_target_pairs={{0,1},{1,0},{2,3},{3,2},{4,5},{5,4},{6,7},{7,6}} | collective-permute-start | bytes 53084168 | tf_op jit(solution)/shard_map/ppermute | solution.py:418
  176.2 105.5 %collective-permute-start.17 = (bf16[464,5120]{1,0:T(8,128)(2,1)S(1)}, bf16[464,5120]{1,0:T(8,128)(2,1)}, u32[]{:S(2)}, u32[]{:S(2)}) collective-permute-start(bf16[464,5120]{1,0:T(8,128)(2,1)S(1)} %slice.22), channel_id=1, source_target_pairs={{0,4},{1,5},{2,6},{3,7},{4,0},{5,1},{6,2},{7,3}} | collective-permute-start | bytes 14254088 | tf_op jit(solution)/shard_map/ppermute | solution.py:415
  182.7 37.2 %collective-permute-start.16 = (bf16[304,5120]{1,0:T(8,128)(2,1)}, bf16[304,5120]{1,0:T(8,128)(2,1)}, u32[]{:S(2)}, u32[]{:S(2)}) collective-permute-start(bf16[304,5120]{1,0:T(8,128)(2,1)} %slice_select_fusion), channel_id=1, source_target_pairs={{0,2},{1,5},{2,0},{3,7},{4,6},{5,1},{6,4},{7,3}} | collective-permute-start | bytes 9338888 | tf_op jit(solution)/shard_map/ppermute | solution.py:415
  220.0 262.5 %collective-permute-start.6 = (bf16[1664,2560]{1,0:T(8,128)(2,1)}, bf16[1664,2560]{1,0:T(8,128)(2,1)}, u32[]{:S(2)}, u32[]{:S(2)}) collective-permute-start(bf16[1664,2560]{1,0:T(8,128)(2,1)} %slice.16), channel_id=1, source_target_pairs={{0,2},{1,3},{2,0},{3,1},{4,6},{5,7},{6,4},{7,5}} | collective-permute-start | bytes 25559048 | tf_op jit(solution)/shard_map/ppermute | solution.py:415
  281.7 200.8 %collective-permute-start.3 = (bf16[768,5120]{1,0:T(8,128)(2,1)}, bf16[768,5120]{1,0:T(8,128)(2,1)}, u32[]{:S(2)}, u32[]{:S(2)}) collective-permute-start(bf16[768,5120]{1,0:T(8,128)(2,1)} %rest_4_.1), channel_id=1, source_target_pairs={{0,2},{1,3},{2,0},{3,1},{4,6},{5,7},{6,4},{7,5}} | collective-permute-start | bytes 23592968 | tf_op jit(solution)/shard_map/ppermute | solution.py:415
  482.5 367.5 %collective-permute-start.9 = (bf16[768,5120]{1,0:T(8,128)(2,1)}, bf16[768,5120]{1,0:T(8,128)(2,1)}, u32[]{:S(2)}, u32[]{:S(2)}) collective-permute-start(bf16[768,5120]{1,0:T(8,128)(2,1)} %rest_4_.1), channel_id=1, source_target_pairs={{0,4},{1,5},{2,6},{3,7},{4,0},{5,1},{6,2},{7,3}} | collective-permute-start | bytes 23592968 | tf_op jit(solution)/shard_map/ppermute | solution.py:415
  482.5 844.5 %collective-permute-start.5 = (bf16[1792,2560]{1,0:T(8,128)(2,1)}, bf16[1792,2560]{1,0:T(8,128)(2,1)}, u32[]{:S(2)}, u32[]{:S(2)}) collective-permute-start(bf16[1792,2560]{1,0:T(8,128)(2,1)} %slice.15), channel_id=1, source_target_pairs={{0,2},{1,3},{2,0},{3,1},{4,6},{5,7},{6,4},{7,5}} | collective-permute-start | bytes 27525128 | tf_op jit(solution)/shard_map/ppermute | solution.py:415
  484.0 661.5 %collective-permute-start.10 = (bf16[768,5120]{1,0:T(8,128)(2,1)}, bf16[768,5120]{1,0:T(8,128)(2,1)}, u32[]{:S(2)}, u32[]{:S(2)}) collective-permute-start(bf16[768,5120]{1,0:T(8,128)(2,1)} %collective-permute-done.3.x_ref), channel_id=1, source_target_pairs={{0,4},{1,5},{2,6},{3,7},{4,0},{5,1},{6,2},{7,3}} | collective-permute-start | bytes 23592968 | tf_op jit(solution)/shard_map/ppermute | solution.py:415
  486.0 843.0 %collective-permute-start.8 = (bf16[1664,2560]{1,0:T(8,128)(2,1)}, bf16[1664,2560]{1,0:T(8,128)(2,1)}, u32[]{:S(2)}, u32[]{:S(2)}) collective-permute-start(bf16[1664,2560]{1,0:T(8,128)(2,1)} %collective-permute-done.6.rest_1_), channel_id=1, source_target_pairs={{0,1},{1,0},{2,3},{3,2},{4,5},{5,4},{6,7},{7,6}} | collective-permute-start | bytes 25559048 | tf_op jit(solution)/shard_map/ppermute | solution.py:418
  1326.5 752.1 %collective-permute-start.18 = (f32[768,5120]{1,0:T(8,128)}, f32[768,5120]{1,0:T(8,128)}, u32[]{:S(2)}, u32[]{:S(2)}) collective-permute-start(f32[768,5120]{1,0:T(8,128)} %shard_map.106), channel_id=1, source_target_pairs={{0,2},{1,5},{2,0},{3,7},{4,6},{5,1},{6,4},{7,3}} | collective-permute-start | bytes 47185928 | tf_op jit(solution)/shard_map/ppermute | solution.py:415
  1327.0 14.6 collective-permute-start.7
  1327.0 841.1 %collective-permute-start.15 = (f32[768,5120]{1,0:T(8,128)}, f32[768,5120]{1,0:T(8,128)}, u32[]{:S(2)}, u32[]{:S(2)}) collective-permute-start(f32[768,5120]{1,0:T(8,128)} %shard_map.102.refs_9_), channel_id=1, source_target_pairs={{0,2},{1,5},{2,0},{3,7},{4,6},{5,1},{6,4},{7,3}} | collective-permute-start | bytes 47185928 | tf_op jit(solution)/shard_map/ppermute | solution.py:415
  1328.5 678.1 %collective-permute-start.11 = (bf16[768,3456]{1,0:T(8,128)(2,1)}, bf16[768,3456]{1,0:T(8,128)(2,1)}, u32[]{:S(2)}, u32[]{:S(2)}) collective-permute-start(bf16[768,3456]{1,0:T(8,128)(2,1)} %get-tuple-element.58), channel_id=1, source_target_pairs={{0,2},{1,3},{2,0},{3,1},{4,6},{5,7},{6,4},{7,5}} | collective-permute-start | bytes 15925256 | tf_op jit(solution)/shard_map/ppermute | solution.py:415
  1329.1 1201.2 %collective-permute-start.23 = (bf16[3072,5120]{1,0:T(8,128)(2,1)}, bf16[3072,5120]{1,0:T(8,128)(2,1)}, u32[]{:S(2)}, u32[]{:S(2)}) collective-permute-start(bf16[3072,5120]{1,0:T(8,128)(2,1)} %get-tuple-element.80.x_ref), channel_id=1, source_target_pairs={{0,1},{1,0},{2,3},{3,2},{4,5},{5,4},{6,7},{7,6}} | collective-permute-start | bytes 94371848 | tf_op jit(solution)/shard_map/ppermute | solution.py:418
  1341.7 1188.6 %collective-permute-start.25 = (bf16[3072,3456]{1,0:T(8,128)(2,1)}, bf16[3072,3456]{1,0:T(8,128)(2,1)}, u32[]{:S(2)}, u32[]{:S(2)}) collective-permute-start(bf16[3072,3456]{1,0:T(8,128)(2,1)} %get-tuple-element.75.db_ref.d_ref), channel_id=1, source_target_pairs={{0,1},{1,0},{2,3},{3,2},{4,5},{5,4},{6,7},{7,6}} | collective-permute-start | bytes 63701000 | tf_op jit(solution)/shard_map/ppermute | solution.py:418
  2006.6 159.9 %collective-permute-start.4 = (bf16[768,3456]{1,0:T(8,128)(2,1)}, bf16[768,3456]{1,0:T(8,128)(2,1)}, u32[]{:S(2)}, u32[]{:S(2)}) collective-permute-start(bf16[768,3456]{1,0:T(8,128)(2,1)} %get-tuple-element.52), channel_id=1, source_target_pairs={{0,2},{1,3},{2,0},{3,1},{4,6},{5,7},{6,4},{7,5}} | collective-permute-start | bytes 15925256 | tf_op jit(solution)/shard_map/ppermute | solution.py:415
  2078.5 378.9 %collective-permute-start.12 = (f32[768,5120]{1,0:T(8,128)}, f32[768,5120]{1,0:T(8,128)}, u32[]{:S(2)}, u32[]{:S(2)}) collective-permute-start(f32[768,5120]{1,0:T(8,128)} %shard_map.97), channel_id=1, source_target_pairs={{0,4},{1,5},{2,6},{3,7},{4,0},{5,1},{6,2},{7,3}} | collective-permute-start | bytes 47185928 | tf_op jit(solution)/shard_map/ppermute | solution.py:415
  2166.4 126.6 %collective-permute-start.22 = (f32[192,5120]{1,0:T(8,128)}, f32[192,5120]{1,0:T(8,128)}, u32[]{:S(2)}, u32[]{:S(2)}) collective-permute-start(f32[192,5120]{1,0:T(8,128)} %get-tuple-element.79), channel_id=1, source_target_pairs={{0,4},{1,3},{2,6},{3,1},{4,0},{5,7},{6,2},{7,5}} | collective-permute-start | bytes 11796488 | tf_op jit(solution)/shard_map/ppermute | solution.py:415
  2168.2 167.0 %collective-permute-start.21 = (f32[192,5120]{1,0:T(8,128)}, f32[192,5120]{1,0:T(8,128)}, u32[]{:S(2)}, u32[]{:S(2)}) collective-permute-start(f32[192,5120]{1,0:T(8,128)} %get-tuple-element.78), channel_id=1, source_target_pairs={{0,4},{1,3},{2,6},{3,1},{4,0},{5,7},{6,2},{7,5}} | collective-permute-start | bytes 11796488 | tf_op jit(solution)/shard_map/ppermute | solution.py:415
  2293.1 84.3 %collective-permute-start.20 = (f32[192,5120]{1,0:T(8,128)}, f32[192,5120]{1,0:T(8,128)}, u32[]{:S(2)}, u32[]{:S(2)}) collective-permute-start(f32[192,5120]{1,0:T(8,128)} %get-tuple-element.77), channel_id=1, source_target_pairs={{0,4},{1,3},{2,6},{3,1},{4,0},{5,7},{6,2},{7,5}} | collective-permute-start | bytes 11796488 | tf_op jit(solution)/shard_map/ppermute | solution.py:415
  2335.2 84.3 %collective-permute-start.19 = (f32[192,5120]{1,0:T(8,128)}, f32[192,5120]{1,0:T(8,128)}, u32[]{:S(2)}, u32[]{:S(2)}) collective-permute-start(f32[192,5120]{1,0:T(8,128)} %get-tuple-element.76), channel_id=1, source_target_pairs={{0,4},{1,3},{2,6},{3,1},{4,0},{5,7},{6,2},{7,5}} | collective-permute-start | bytes 11796488 | tf_op jit(solution)/shard_map/ppermute | solution.py:415
  2377.3 426.7 %collective-permute-start.27 = (bf16[3072,5120]{1,0:T(8,128)(2,1)}, bf16[3072,5120]{1,0:T(8,128)(2,1)}, u32[]{:S(2)}, u32[]{:S(2)}) collective-permute-start(bf16[3072,5120]{1,0:T(8,128)(2,1)} %get-tuple-element.82.d_ref), channel_id=1, source_target_pairs={{0,1},{1,0},{2,3},{3,2},{4,5},{5,4},{6,7},{7,6}} | collective-permute-start | bytes 94371848 | tf_op jit(solution)/shard_map/ppermute | solution.py:418
  2419.5 247.7 %collective-permute-start.24 = (bf16[3072,3456]{1,0:T(8,128)(2,1)}, bf16[3072,3456]{1,0:T(8,128)(2,1)}, u32[]{:S(2)}, u32[]{:S(2)}) collective-permute-start(bf16[3072,3456]{1,0:T(8,128)(2,1)} %get-tuple-element.74.da_ref.d_ref), channel_id=1, source_target_pairs={{0,1},{1,0},{2,3},{3,2},{4,5},{5,4},{6,7},{7,6}} | collective-permute-start | bytes 63701000 | tf_op jit(solution)/shard_map/ppermute | solution.py:418
  2457.4 346.7 %collective-permute-start.26 = (bf16[3072,3456]{1,0:T(8,128)(2,1)}, bf16[3072,3456]{1,0:T(8,128)(2,1)}, u32[]{:S(2)}, u32[]{:S(2)}) collective-permute-start(bf16[3072,3456]{1,0:T(8,128)(2,1)} %get-tuple-element.81.h_ref), channel_id=1, source_target_pairs={{0,1},{1,0},{2,3},{3,2},{4,5},{5,4},{6,7},{7,6}} | collective-permute-start | bytes 63701000 | tf_op jit(solution)/shard_map/ppermute | solution.py:418

commit v3 on v2

--- a/solution.py
+++ b/solution.py
@@ -375,23 +375,25 @@
     )[0]
 
 
-def k_add(core, u, v, pieces=1, tn=512):
+def k_add(core, u, v, sizes=None, tn=512):
     r, d = u.shape
-    rp = r // pieces
+    sizes = sizes or (r,)
 
     def body(i_ref, u_ref, v_ref, *outs):
-        for p, o_ref in enumerate(outs):
-            m = slice(p * rp, (p + 1) * rp)
+        at = 0
+        for size, o_ref in zip(sizes, outs):
+            m = slice(at, at + size)
             o_ref[...] = u_ref[m, :] + v_ref[m, :]
+            at += size
 
     s = spec((r, tn), lambda n, i: (0, n))
-    o = spec((rp, tn), lambda n, i: (0, n))
-    return call(body, core, (d // tn,), [s, s], [(o, (rp, d), f32)] * pieces, (u, v), r * d)
-
-
-def k_fin(core, p, u, v, keep, tr=64):
+    outs = [(spec((size, tn), lambda n, i: (0, n)), (size, d), f32) for size in sizes]
+    return call(body, core, (d // tn,), [s, s], outs, (u, v), r * d)
+
+
+def k_fin(core, at, u, v, keep, tr):
     r, d = u.shape
-    n0 = p * v.shape[0] // tr
+    n0 = at // tr
 
     def body(i_ref, u_ref, v_ref, *rest):
         rest[-1][...] = (u_ref[...] + v_ref[...]).astype(bf)
@@ -420,7 +422,8 @@
     def layer(x, wg, wu, wd, dy):
         i = lax.axis_index("dp").astype(jnp.int32).reshape(1)
         ka = 1792
-        qa = 304
+        qa = 312
+        sizes = (448, 256, 64)
         xX, xY = hop(x, 1, 1), hop(x, 2, 2)
         dyX, dyY = hop(dy, 1, 1), hop(dy, 2, 2)
         wgo, wuo, wdo = swap(wg), swap(wu), swap(wd)
@@ -446,8 +449,8 @@
         z3 = k_dx(i, lambda c: 3, daall, dball, wgc, wuc)
         sa = hop(z3, 1, 2)
         z2 = k_dx(i, lambda c: 2 - c, daall, dball, wgc, wuc)
-        s2 = k_add(i, z2, sa, pieces=4)
-        s2 = [hop(s2[p], 2, 1) for p in range(4)]
+        s2 = k_add(i, z2, sa, sizes)
+        s2 = [hop(v, 2, 1) for v in s2]
 
         hDr, hXr = hop(h3, 1, 1), hop(h1, 1, 1)
         yYr = hop(k_y2(i, h2, wdc, hDr, wX), 2, 2)
@@ -461,8 +464,8 @@
 
         pre = k_add(i, z0, s1)[0]
         dx = ()
-        for p in range(4):
-            dx = (k_fin(i, p, pre, s2[p], dx),)
+        for p, v in enumerate(s2):
+            dx = (k_fin(i, sum(sizes[:p]), pre, v, dx, 64 if p < 2 else 32),)
         return y, dx[0], dwg, dwu, dwd
 
     return jax.shard_map(layer, mesh=mesh, in_specs=(rows, wsp, wsp, dsp, rows), out_specs=(rows, rows, wsp, wsp, dsp), check_vma=False)

time: 2930 us -> 2770 us (0.945)
  waiting for transfers between devices: 1370 us -> 1170 us
  starting transfers between devices: 202 us -> 238 us
    ppermute x18 -> x17, waiting for transfers between devices: 1360 us -> 1170 us  [hop(): return lax.ppermute(v, axes, pairs)]
    ppermute x10, starting transfers between devices: 181 us -> 215 us  [swap(): return lax.ppermute(v, 'dp', [(0, 1), (1, 0)])]
    pallas_call x23 -> x22, Pallas kernels: 1330 us -> 1330 us  [call(): pl.pallas_call(body, grid_spec=pltpu.PrefetchScalarGridSpec(num_scalar_pr...]
  transfers between devices with their start and end apart: 28 -> 27, of which waited for: 10 -> 8; matrix products, arithmetic and copies ran while one was open for 1% -> 1% of each run, Pallas kernels for 41% -> 43%
where the time goes in v3:
time: 2770 us
  Pallas kernels  1330 us (48%)
  waiting for transfers between devices  1170 us (42%)
  starting transfers between devices  238 us (9%)
    pallas_call x22, Pallas kernels, call(): pl.pallas_call(body, grid_spec=pltpu.PrefetchScalarGridSpec(num_scalar_pr...  1330 us
    ppermute x17, waiting for transfers between devices, hop(): return lax.ppermute(v, axes, pairs)  1170 us
    ppermute x10, starting transfers between devices, swap(): return lax.ppermute(v, 'dp', [(0, 1), (1, 0)])  215 us
  transfers between devices with their start and end apart: 27, of which 8 were waited for; matrix products, arithmetic and copies ran while one was open for 1% of the time, Pallas kernels for 43%

profile of v3, /device:TPU:0, one launch (start us, length us, event | category | flops | bytes accessed | tf_op | source)
XLA Modules:
  0.0 2770.3 jit_solution(6683465498656094897)
XLA Ops:
  6.5 167.8 %collective-permute-done.14.refs_1_ = bf16[768,5120]{1,0:T(8,128)(2,1)} collective-permute-done((bf16[768,5120]{1,0:T(8,128)(2,1)}, bf16[768,5120]{1,0:T(8,128)(2,1)}, u32[]{:S(2)}, u32[]{:S(2)}) %collective-permute-start.14) | collective-permute-done | bytes 7864352 | tf_op jit(solution)/shard_map/ppermute | solution.py:417
  184.4 157.6 %collective-permute-done.3.x_ref = bf16[768,5120]{1,0:T(8,128)(2,1)} collective-permute-done((bf16[768,5120]{1,0:T(8,128)(2,1)}, bf16[768,5120]{1,0:T(8,128)(2,1)}, u32[]{:S(2)}, u32[]{:S(2)}) %collective-permute-start.3) | collective-permute-done | bytes 7864352 | tf_op jit(solution)/shard_map/ppermute | solution.py:417
  343.8 7.9 slice.15
  351.6 28.3 %collective-permute-done.16 = bf16[312,5120]{1,0:T(8,128)(2,1)} collective-permute-done((bf16[312,5120]{1,0:T(8,128)(2,1)S(1)}, bf16[312,5120]{1,0:T(8,128)(2,1)}, u32[]{:S(2)}, u32[]{:S(2)}) %collective-permute-start.16) | collective-permute-done | bytes 3194912 | tf_op jit(solution)/shard_map/ppermute | solution.py:417
  381.7 7.4 slice.16
  389.4 7.1 pad_maximum_fusion.refs_1_
  396.4 364.0 %collective-permute-done.6.rest_1_ = bf16[1664,2560]{1,0:T(8,128)(2,1)} collective-permute-done((bf16[1664,2560]{1,0:T(8,128)(2,1)}, bf16[1664,2560]{1,0:T(8,128)(2,1)}, u32[]{:S(2)}, u32[]{:S(2)}) %collective-permute-start.6) | collective-permute-done | bytes 8519712 | tf_op jit(solution)/shard_map/ppermute | solution.py:417
  763.0 70.3 %shard_map.92 = (f32[768,3456]{1,0:T(8,128)}, f32[768,3456]{1,0:T(8,128)}, bf16[768,3456]{1,0:T(8,128)(2,1)}, bf16[3072,3456]{1,0:T(8,128)(2,1)}, bf16[3072,5120...) custom-call(s32[1]{0:T(128)} %bitcast.i_ref.refs_0_, bf16[768,5120]{1,0:T(8,128)(2,1)} %rest_4_.1, ...), custom_call_target="tpu_custom_call" | custom-call | flops 54358179840 | bytes 78643200 | tf_op jit(solution)/shard_map/pallas_call | solution.py:46
  833.3 44.3 %shard_map.93 = (bf16[3072,3456]{1,0:T(8,128)(2,1)}, bf16[3072,3456]{1,0:T(8,128)(2,1)}, bf16[3072,5120]{1,0:T(8,128)(2,1)}, bf16[3456,5120]{1,0:T(8,128)(2,1)}) custom-call(s32[1]{0:T(128)} %bitcast.i_ref.refs_0_, bf16[768,5120]{1,0:T(8,128)(2,1)} %rest_0_.1, bf16[3456,2560]{1,0:T(8,128)(2,1)} %w_ref.1, bf16[3456,2560]{1,0:T(8,128)(2,1)} %collective-permute-done.2.wo_ref, ...), custom_call_target="tpu_custom_call" | custom-call | flops 27179089920 | bytes 64487424 | tf_op jit(solution)/shard_map/pallas_call | solution.py:46
  877.6 68.9 %shard_map.94 = (f32[768,3456]{1,0:T(8,128)}, f32[768,3456]{1,0:T(8,128)}, bf16[768,3456]{1,0:T(8,128)(2,1)}, bf16[3072,3456]{1,0:T(8,128)(2,1)}, bf16[3072,5120]{1,0:T(8,128)(2,1)}) custom-call(s32[1]{0:T(128)} %bitcast.i_ref.refs_0_, bf16[768,5120]{1,0:T(8,128)(2,1)} %collective-permute-done.3.x_ref, ...), custom_call_target="tpu_custom_call", output_to_operand_aliasing={{3}: (4, {}), {4}: (5, {})} | custom-call | flops 54358179840 | bytes 131334144 | tf_op jit(solution)/shard_map/pallas_call | solution.py:46
  946.6 69.0 %shard_map.95 = (f32[768,3456]{1,0:T(8,128)}, f32[768,3456]{1,0:T(8,128)}, bf16[768,3456]{1,0:T(8,128)(2,1)}, bf16[3072,3456]{1,0:T(8,128)(2,1)}, bf16[3072,5120]{1,0:T(8,128)(2,1)}) custom-call(s32[1]{0:T(128)} %bitcast.i_ref.refs_0_, bf16[768,5120]{1,0:T(8,128)(2,1)} %collective-permute-done.9.x_ref, ...), custom_call_target="tpu_custom_call", output_to_operand_aliasing={{3}: (4, {}), {4}: (5, {})} | custom-call | flops 54358179840 | bytes 131334144 | tf_op jit(solution)/shard_map/pallas_call | solution.py:46
  1015.6 41.9 %shard_map.99 = (bf16[3072,3456]{1,0:T(8,128)(2,1)}, bf16[3072,3456]{1,0:T(8,128)(2,1)}, bf16[3072,5120]{1,0:T(8,128)(2,1)}) custom-call(s32[1]{0:T(128)} %bitcast.i_ref.refs_0_, bf16[768,5120]{1,0:T(8,128)(2,1)} %collective-permute-done.14.refs_1_, ...), custom_call_target="tpu_custom_call", output_to_operand_aliasing={{0}: (5, {}), {1}: (6, {}), {2}: (7, {})} | custom-call | flops 27179089920 | bytes 138412032 | tf_op jit(solution)/shard_map/pallas_call | solution.py:46
  1057.5 41.8 %shard_map.100 = (bf16[3072,3456]{1,0:T(8,128)(2,1)}, bf16[3072,3456]{1,0:T(8,128)(2,1)}, bf16[3072,5120]{1,0:T(8,128)(2,1)}) custom-call(s32[1]{0:T(128)} %bitcast.i_ref.refs_0_, bf16[768,5120]{1,0:T(8,128)(2,1)} %collective-permute-done.13.refs_1_, ...), custom_call_target="tpu_custom_call", output_to_operand_aliasing={{0}: (5, {}), {1}: (6, {}), {2}: (7, {})} | custom-call | flops 27179089920 | bytes 138412032 | tf_op jit(solution)/shard_map/pallas_call | solution.py:46
  1099.3 70.3 %shard_map.102.refs_9_ = f32[768,5120]{1,0:T(8,128)} custom-call(s32[1]{0:T(128)} %bitcast.i_ref.refs_0_, bf16[3072,3456]{1,0:T(8,128)(2,1)} %get-tuple-element.68.da_ref.refs_5_, bf16[3072,3456]{1,0:T(8,128)(2,1)} %get-tuple-element.69.db_ref.refs_6_, bf16[5120,3456]{1,0:T(8,128)(2,1)} %get-tuple-element.47.wg_ref, bf16[5120,3456]{1,0:T(8,128)(2,1)} %get-tuple-element.48.wu_ref), custom_call_target="tpu_custom_call" | custom-call | flops 54358179840 | bytes 113246208 | tf_op jit(solution)/shard_map/pallas_call | solution.py:46
  1169.6 72.9 %shard_map.101.u_ref.refs_8_ = f32[768,5120]{1,0:T(8,128)} custom-call(s32[1]{0:T(128)} %bitcast.i_ref.refs_0_, bf16[3072,3456]{1,0:T(8,128)(2,1)} %get-tuple-element.68.da_ref.refs_5_, bf16[3072,3456]{1,0:T(8,128)(2,1)} %get-tuple-element.69.db_ref.refs_6_, bf16[5120,3456]{1,0:T(8,128)(2,1)} %get-tuple-element.47.wg_ref, ...), custom_call_target="tpu_custom_call" | custom-call | flops 54358179840 | bytes 121110528 | tf_op jit(solution)/shard_map/pallas_call | solution.py:46
  1242.5 69.1 %shard_map.96 = (f32[768,3456]{1,0:T(8,128)}, f32[768,3456]{1,0:T(8,128)}, bf16[768,3456]{1,0:T(8,128)(2,1)}, bf16[3072,3456]{1,0:T(8,128)(2,1)}, bf16[3072,5120]{1,0:T(8,128)(2,1)}) custom-call(s32[1]{0:T(128)} %bitcast.i_ref.refs_0_, bf16[768,5120]{1,0:T(8,128)(2,1)} %collective-permute-done.10.x_ref, ...), custom_call_target="tpu_custom_call", output_to_operand_aliasing={{3}: (4, {}), {4}: (5, {})} | custom-call | flops 54358179840 | bytes 131334144 | tf_op jit(solution)/shard_map/pallas_call | solution.py:46
  1313.0 41.9 %shard_map.104 = (bf16[3072,3456]{1,0:T(8,128)(2,1)}, bf16[3072,3456]{1,0:T(8,128)(2,1)}, bf16[3072,5120]{1,0:T(8,128)(2,1)}) custom-call(s32[1]{0:T(128)} %bitcast.i_ref.refs_0_, bf16[768,5120]{1,0:T(8,128)(2,1)} %pad_maximum_fusion.refs_1_, ...), custom_call_target="tpu_custom_call", output_to_operand_aliasing={{0}: (5, {}), {1}: (6, {}), {2}: (7, {})} | custom-call | flops 27179089920 | bytes 169869312 | tf_op jit(solution)/shard_map/pallas_call | solution.py:46
  1354.9 70.2 %shard_map.106 = f32[768,5120]{1,0:T(8,128)} custom-call(s32[1]{0:T(128)} %bitcast.i_ref.refs_0_, bf16[3072,3456]{1,0:T(8,128)(2,1)} %get-tuple-element.73.da_ref.d_ref, bf16[3072,3456]{1,0:T(8,128)(2,1)} %get-tuple-element.74.db_ref.d_ref, bf16[5120,3456]{1,0:T(8,128)(2,1)} %get-tuple-element.47.wg_ref, bf16[5120,3456]{1,0:T(8,128)(2,1)} %get-tuple-element.48.wu_ref), custom_call_target="tpu_custom_call" | custom-call | flops 54358179840 | bytes 113246208 | tf_op jit(solution)/shard_map/pallas_call | solution.py:46
  1428.5 71.4 %shard_map.97 = f32[768,5120]{1,0:T(8,128)} custom-call(s32[1]{0:T(128)} %bitcast.i_ref.refs_0_, bf16[768,3456]{1,0:T(8,128)(2,1)} %get-tuple-element.54.h_ref, bf16[3456,5120]{1,0:T(8,128)(2,1)} %get-tuple-element.46.w_ref.refs_2_, bf16[768,3456]{1,0:T(8,128)(2,1)} %collective-permute-done.11.hr_ref, bf16[1792,2560]{1,0:T(8,128)(2,1)} %collective-permute-done.5.rest_0_, ...), custom_call_target="tpu_custom_call" | custom-call | flops 54358179840 | bytes 81395712 | tf_op jit(solution)/shard_map/pallas_call | solution.py:46
  1502.8 151.5 %collective-permute-done.18.v_ref = f32[768,5120]{1,0:T(8,128)} collective-permute-done((f32[768,5120]{1,0:T(8,128)}, f32[768,5120]{1,0:T(8,128)}, u32[]{:S(2)}, u32[]{:S(2)}) %collective-permute-start.18) | collective-permute-done | bytes 15728672 | tf_op jit(solution)/shard_map/ppermute | solution.py:417
  1654.4 35.0 %collective-permute-start.24 = (bf16[3072,3456]{1,0:T(8,128)(2,1)}, bf16[3072,3456]{1,0:T(8,128)(2,1)}, u32[]{:S(2)}, u32[]{:S(2)}) collective-permute-start(bf16[3072,3456]{1,0:T(8,128)(2,1)} %get-tuple-element.74.db_ref.d_ref), channel_id=1, source_target_pairs={{0,1},{1,0},{2,3},{3,2},{4,5},{5,4},{6,7},{7,6}} | collective-permute-start | bytes 63701000 | tf_op jit(solution)/shard_map/ppermute | solution.py:420
  1689.4 70.2 %shard_map.105.u_ref = f32[768,5120]{1,0:T(8,128)} custom-call(s32[1]{0:T(128)} %bitcast.i_ref.refs_0_, bf16[3072,3456]{1,0:T(8,128)(2,1)} %get-tuple-element.73.da_ref.d_ref, bf16[3072,3456]{1,0:T(8,128)(2,1)} %get-tuple-element.74.db_ref.d_ref, bf16[5120,3456]{1,0:T(8,128)(2,1)} %get-tuple-element.47.wg_ref, bf16[5120,3456]{1,0:T(8,128)(2,1)} %get-tuple-element.48.wu_ref), custom_call_target="tpu_custom_call" | custom-call | flops 54358179840 | bytes 113246208 | tf_op jit(solution)/shard_map/pallas_call | solution.py:46
  1759.6 17.4 shard_map.107
  1777.0 159.0 %collective-permute-done.4.hr_ref = bf16[768,3456]{1,0:T(8,128)(2,1)} collective-permute-done((bf16[768,3456]{1,0:T(8,128)(2,1)}, bf16[768,3456]{1,0:T(8,128)(2,1)}, u32[]{:S(2)}, u32[]{:S(2)}) %collective-permute-start.4) | collective-permute-done | bytes 5308448 | tf_op jit(solution)/shard_map/ppermute | solution.py:417
  1938.0 142.2 %collective-permute-done.19.v_ref = f32[64,5120]{1,0:T(8,128)S(1)} collective-permute-done((f32[64,5120]{1,0:T(8,128)}, f32[64,5120]{1,0:T(8,128)S(1)}, u32[]{:S(2)}, u32[]{:S(2)}) %collective-permute-start.19) | collective-permute-done | bytes 1310752 | tf_op jit(solution)/shard_map/ppermute | solution.py:417
  2081.7 179.0 %collective-permute-start.23 = (bf16[3072,3456]{1,0:T(8,128)(2,1)}, bf16[3072,3456]{1,0:T(8,128)(2,1)}, u32[]{:S(2)}, u32[]{:S(2)}) collective-permute-start(bf16[3072,3456]{1,0:T(8,128)(2,1)} %get-tuple-element.73.da_ref.d_ref), channel_id=1, source_target_pairs={{0,1},{1,0},{2,3},{3,2},{4,5},{5,4},{6,7},{7,6}} | collective-permute-start | bytes 63701000 | tf_op jit(solution)/shard_map/ppermute | solution.py:420
  2260.7 17.4 shard_map.103.u_ref
  2278.1 72.6 %shard_map.98 = bf16[768,5120]{1,0:T(8,128)(2,1)} custom-call(s32[1]{0:T(128)} %bitcast.i_ref.refs_0_, bf16[768,3456]{1,0:T(8,128)(2,1)} %get-tuple-element.43.h_ref, bf16[3456,5120]{1,0:T(8,128)(2,1)} %get-tuple-element.46.w_ref.refs_2_, bf16[768,3456]{1,0:T(8,128)(2,1)} %collective-permute-done.4.hr_ref, ...), custom_call_target="tpu_custom_call" | custom-call | flops 54358179840 | bytes 104988672 | tf_op jit(solution)/shard_map/pallas_call | solution.py:46
  2350.7 10.0 shard_map.108.rest_0_
  2369.0 136.7 %shard_map.112 = f32[2560,3456]{1,0:T(8,128)} custom-call(s32[1]{0:T(128)} %bitcast.i_ref.refs_0_, bf16[3072,5120]{1,0:T(8,128)(2,1)} %get-tuple-element.78.x_ref, bf16[3072,5120]{1,0:T(8,128)(2,1)} %collective-permute-done.22.xo_ref, bf16[3072,3456]{1,0:T(8,128)(2,1)} %get-tuple-element.74.db_ref.d_ref, bf16[3072,3456]{1,0:T(8,128)(2,1)} %collective-permute-done.24.do_ref), custom_call_target="tpu_custom_call" | custom-call | flops 108716359680 | bytes 105381888 | tf_op jit(solution)/shard_map/pallas_call | solution.py:46
  2505.8 136.8 %shard_map.111 = f32[2560,3456]{1,0:T(8,128)} custom-call(s32[1]{0:T(128)} %bitcast.i_ref.refs_0_, bf16[3072,5120]{1,0:T(8,128)(2,1)} %get-tuple-element.78.x_ref, bf16[3072,5120]{1,0:T(8,128)(2,1)} %collective-permute-done.22.xo_ref, bf16[3072,3456]{1,0:T(8,128)(2,1)} %get-tuple-element.73.da_ref.d_ref, bf16[3072,3456]{1,0:T(8,128)(2,1)} %collective-permute-done.23.do_ref), custom_call_target="tpu_custom_call" | custom-call | flops 108716359680 | bytes 105381888 | tf_op jit(solution)/shard_map/pallas_call | solution.py:46
  2642.6 127.6 %shard_map.113 = f32[3456,2560]{1,0:T(8,128)} custom-call(s32[1]{0:T(128)} %bitcast.i_ref.refs_0_, bf16[3072,3456]{1,0:T(8,128)(2,1)} %get-tuple-element.79.h_ref, bf16[3072,3456]{1,0:T(8,128)(2,1)} %collective-permute-done.25.ho_ref, bf16[3072,5120]{1,0:T(8,128)(2,1)} %get-tuple-element.80.d_ref, bf16[3072,5120]{1,0:T(8,128)(2,1)} %collective-permute-done.26.do_ref), custom_call_target="tpu_custom_call" | custom-call | flops 108716359680 | bytes 105381888 | tf_op jit(solution)/shard_map/pallas_call | solution.py:46
  (51 shorter events, 42.0 us)
Async XLA Ops:
  0.6 173.7 %collective-permute-start.14 = (bf16[768,5120]{1,0:T(8,128)(2,1)}, bf16[768,5120]{1,0:T(8,128)(2,1)}, u32[]{:S(2)}, u32[]{:S(2)}) collective-permute-start(bf16[768,5120]{1,0:T(8,128)(2,1)} %rest_0_.1), channel_id=1, source_target_pairs={{0,2},{1,3},{2,0},{3,1},{4,6},{5,7},{6,4},{7,5}} | collective-permute-start | bytes 23592968 | tf_op jit(solution)/shard_map/ppermute | solution.py:417
  4.0 175.2 %collective-permute-start.13 = (bf16[768,5120]{1,0:T(8,128)(2,1)}, bf16[768,5120]{1,0:T(8,128)(2,1)}, u32[]{:S(2)}, u32[]{:S(2)}) collective-permute-start(bf16[768,5120]{1,0:T(8,128)(2,1)} %rest_0_.1), channel_id=1, source_target_pairs={{0,4},{1,5},{2,6},{3,7},{4,0},{5,1},{6,2},{7,3}} | collective-permute-start | bytes 23592968 | tf_op jit(solution)/shard_map/ppermute | solution.py:417
  5.5 336.5 %collective-permute-start.3 = (bf16[768,5120]{1,0:T(8,128)(2,1)}, bf16[768,5120]{1,0:T(8,128)(2,1)}, u32[]{:S(2)}, u32[]{:S(2)}) collective-permute-start(bf16[768,5120]{1,0:T(8,128)(2,1)} %rest_4_.1), channel_id=1, source_target_pairs={{0,2},{1,3},{2,0},{3,1},{4,6},{5,7},{6,4},{7,5}} | collective-permute-start | bytes 23592968 | tf_op jit(solution)/shard_map/ppermute | solution.py:417
  6.0 756.5 %collective-permute-start = (bf16[2560,3456]{1,0:T(8,128)(2,1)}, bf16[2560,3456]{1,0:T(8,128)(2,1)}, u32[]{:S(2)}, u32[]{:S(2)}) collective-permute-start(bf16[2560,3456]{1,0:T(8,128)(2,1)} %wg_ref.1), channel_id=1, source_target_pairs={{0,1},{1,0},{2,3},{3,2},{4,5},{5,4},{6,7},{7,6}} | collective-permute-start | bytes 53084168 | tf_op jit(solution)/shard_map/ppermute | solution.py:420
  6.0 756.5 %collective-permute-start.1 = (bf16[2560,3456]{1,0:T(8,128)(2,1)}, bf16[2560,3456]{1,0:T(8,128)(2,1)}, u32[]{:S(2)}, u32[]{:S(2)}) collective-permute-start(bf16[2560,3456]{1,0:T(8,128)(2,1)} %wu_ref.1), channel_id=1, source_target_pairs={{0,1},{1,0},{2,3},{3,2},{4,5},{5,4},{6,7},{7,6}} | collective-permute-start | bytes 53084168 | tf_op jit(solution)/shard_map/ppermute | solution.py:420
  174.3 659.0 %collective-permute-start.2 = (bf16[3456,2560]{1,0:T(8,128)(2,1)}, bf16[3456,2560]{1,0:T(8,128)(2,1)}, u32[]{:S(2)}, u32[]{:S(2)}) collective-permute-start(bf16[3456,2560]{1,0:T(8,128)(2,1)} %w_ref.1), channel_id=1, source_target_pairs={{0,1},{1,0},{2,3},{3,2},{4,5},{5,4},{6,7},{7,6}} | collective-permute-start | bytes 53084168 | tf_op jit(solution)/shard_map/ppermute | solution.py:420
  179.1 209.9 %collective-permute-start.17 = (bf16[456,5120]{1,0:T(8,128)(2,1)}, bf16[456,5120]{1,0:T(8,128)(2,1)}, u32[]{:S(2)}, u32[]{:S(2)}) collective-permute-start(bf16[456,5120]{1,0:T(8,128)(2,1)} %slice.22), channel_id=1, source_target_pairs={{0,4},{1,5},{2,6},{3,7},{4,0},{5,1},{6,2},{7,3}} | collective-permute-start | bytes 14008328 | tf_op jit(solution)/shard_map/ppermute | solution.py:417
  342.0 37.9 %collective-permute-start.16 = (bf16[312,5120]{1,0:T(8,128)(2,1)S(1)}, bf16[312,5120]{1,0:T(8,128)(2,1)}, u32[]{:S(2)}, u32[]{:S(2)}) collective-permute-start(bf16[312,5120]{1,0:T(8,128)(2,1)S(1)} %slice_select_fusion), channel_id=1, source_target_pairs={{0,2},{1,5},{2,0},{3,7},{4,6},{5,1},{6,4},{7,3}} | collective-permute-start | bytes 9584648 | tf_op jit(solution)/shard_map/ppermute | solution.py:417
  379.9 382.0 %collective-permute-start.5 = (bf16[1792,2560]{1,0:T(8,128)(2,1)}, bf16[1792,2560]{1,0:T(8,128)(2,1)}, u32[]{:S(2)}, u32[]{:S(2)}) collective-permute-start(bf16[1792,2560]{1,0:T(8,128)(2,1)} %slice.15), channel_id=1, source_target_pairs={{0,2},{1,3},{2,0},{3,1},{4,6},{5,7},{6,4},{7,5}} | collective-permute-start | bytes 27525128 | tf_op jit(solution)/shard_map/ppermute | solution.py:417
  389.1 371.4 %collective-permute-start.6 = (bf16[1664,2560]{1,0:T(8,128)(2,1)}, bf16[1664,2560]{1,0:T(8,128)(2,1)}, u32[]{:S(2)}, u32[]{:S(2)}) collective-permute-start(bf16[1664,2560]{1,0:T(8,128)(2,1)} %slice.16), channel_id=1, source_target_pairs={{0,2},{1,3},{2,0},{3,1},{4,6},{5,7},{6,4},{7,5}} | collective-permute-start | bytes 25559048 | tf_op jit(solution)/shard_map/ppermute | solution.py:417
  760.4 186.1 %collective-permute-start.9 = (bf16[768,5120]{1,0:T(8,128)(2,1)}, bf16[768,5120]{1,0:T(8,128)(2,1)}, u32[]{:S(2)}, u32[]{:S(2)}) collective-permute-start(bf16[768,5120]{1,0:T(8,128)(2,1)} %rest_4_.1), channel_id=1, source_target_pairs={{0,4},{1,5},{2,6},{3,7},{4,0},{5,1},{6,2},{7,3}} | collective-permute-start | bytes 23592968 | tf_op jit(solution)/shard_map/ppermute | solution.py:417
  761.9 480.5 %collective-permute-start.10 = (bf16[768,5120]{1,0:T(8,128)(2,1)}, bf16[768,5120]{1,0:T(8,128)(2,1)}, u32[]{:S(2)}, u32[]{:S(2)}) collective-permute-start(bf16[768,5120]{1,0:T(8,128)(2,1)} %collective-permute-done.3.x_ref), channel_id=1, source_target_pairs={{0,4},{1,5},{2,6},{3,7},{4,0},{5,1},{6,2},{7,3}} | collective-permute-start | bytes 23592968 | tf_op jit(solution)/shard_map/ppermute | solution.py:417
  762.5 664.6 %collective-permute-start.8 = (bf16[1664,2560]{1,0:T(8,128)(2,1)}, bf16[1664,2560]{1,0:T(8,128)(2,1)}, u32[]{:S(2)}, u32[]{:S(2)}) collective-permute-start(bf16[1664,2560]{1,0:T(8,128)(2,1)} %collective-permute-done.6.rest_1_), channel_id=1, source_target_pairs={{0,1},{1,0},{2,3},{3,2},{4,5},{5,4},{6,7},{7,6}} | collective-permute-start | bytes 25559048 | tf_op jit(solution)/shard_map/ppermute | solution.py:420
  762.5 664.6 %collective-permute-start.7 = (bf16[1792,2560]{1,0:T(8,128)(2,1)}, bf16[1792,2560]{1,0:T(8,128)(2,1)}, u32[]{:S(2)}, u32[]{:S(2)}) collective-permute-start(bf16[1792,2560]{1,0:T(8,128)(2,1)} %collective-permute-done.5.rest_0_), channel_id=1, source_target_pairs={{0,1},{1,0},{2,3},{3,2},{4,5},{5,4},{6,7},{7,6}} | collective-permute-start | bytes 27525128 | tf_op jit(solution)/shard_map/ppermute | solution.py:420
  1311.5 116.9 %collective-permute-start.11 = (bf16[768,3456]{1,0:T(8,128)(2,1)}, bf16[768,3456]{1,0:T(8,128)(2,1)}, u32[]{:S(2)}, u32[]{:S(2)}) collective-permute-start(bf16[768,3456]{1,0:T(8,128)(2,1)} %get-tuple-element.57), channel_id=1, source_target_pairs={{0,2},{1,3},{2,0},{3,1},{4,6},{5,7},{6,4},{7,5}} | collective-permute-start | bytes 15925256 | tf_op jit(solution)/shard_map/ppermute | solution.py:417
  1425.1 229.3 %collective-permute-start.18 = (f32[768,5120]{1,0:T(8,128)}, f32[768,5120]{1,0:T(8,128)}, u32[]{:S(2)}, u32[]{:S(2)}) collective-permute-start(f32[768,5120]{1,0:T(8,128)} %shard_map.106), channel_id=1, source_target_pairs={{0,2},{1,5},{2,0},{3,7},{4,6},{5,1},{6,4},{7,3}} | collective-permute-start | bytes 47185928 | tf_op jit(solution)/shard_map/ppermute | solution.py:417
  1425.7 511.8 %collective-permute-start.15 = (f32[768,5120]{1,0:T(8,128)}, f32[768,5120]{1,0:T(8,128)}, u32[]{:S(2)}, u32[]{:S(2)}) collective-permute-start(f32[768,5120]{1,0:T(8,128)} %shard_map.102.refs_9_), channel_id=1, source_target_pairs={{0,2},{1,5},{2,0},{3,7},{4,6},{5,1},{6,4},{7,3}} | collective-permute-start | bytes 47185928 | tf_op jit(solution)/shard_map/ppermute | solution.py:417
  1427.1 941.9 %collective-permute-start.22 = (bf16[3072,5120]{1,0:T(8,128)(2,1)}, bf16[3072,5120]{1,0:T(8,128)(2,1)}, u32[]{:S(2)}, u32[]{:S(2)}) collective-permute-start(bf16[3072,5120]{1,0:T(8,128)(2,1)} %get-tuple-element.78.x_ref), channel_id=1, source_target_pairs={{0,1},{1,0},{2,3},{3,2},{4,5},{5,4},{6,7},{7,6}} | collective-permute-start | bytes 94371848 | tf_op jit(solution)/shard_map/ppermute | solution.py:420
  1499.9 581.9 %collective-permute-start.12 = (f32[768,5120]{1,0:T(8,128)}, f32[768,5120]{1,0:T(8,128)}, u32[]{:S(2)}, u32[]{:S(2)}) collective-permute-start(f32[768,5120]{1,0:T(8,128)} %shard_map.97), channel_id=1, source_target_pairs={{0,4},{1,5},{2,6},{3,7},{4,0},{5,1},{6,2},{7,3}} | collective-permute-start | bytes 47185928 | tf_op jit(solution)/shard_map/ppermute | solution.py:417
  1501.3 434.6 %collective-permute-start.4 = (bf16[768,3456]{1,0:T(8,128)(2,1)}, bf16[768,3456]{1,0:T(8,128)(2,1)}, u32[]{:S(2)}, u32[]{:S(2)}) collective-permute-start(bf16[768,3456]{1,0:T(8,128)(2,1)} %get-tuple-element.51), channel_id=1, source_target_pairs={{0,2},{1,3},{2,0},{3,1},{4,6},{5,7},{6,4},{7,5}} | collective-permute-start | bytes 15925256 | tf_op jit(solution)/shard_map/ppermute | solution.py:417
  1654.4 714.7 %collective-permute-start.24 = (bf16[3072,3456]{1,0:T(8,128)(2,1)}, bf16[3072,3456]{1,0:T(8,128)(2,1)}, u32[]{:S(2)}, u32[]{:S(2)}) collective-permute-start(bf16[3072,3456]{1,0:T(8,128)(2,1)} %get-tuple-element.74.db_ref.d_ref), channel_id=1, source_target_pairs={{0,1},{1,0},{2,3},{3,2},{4,5},{5,4},{6,7},{7,6}} | collective-permute-start | bytes 63701000 | tf_op jit(solution)/shard_map/ppermute | solution.py:420
  1936.0 145.7 %collective-permute-start.20 = (f32[256,5120]{1,0:T(8,128)}, f32[256,5120]{1,0:T(8,128)}, u32[]{:S(2)}, u32[]{:S(2)}) collective-permute-start(f32[256,5120]{1,0:T(8,128)} %get-tuple-element.76), channel_id=1, source_target_pairs={{0,4},{1,3},{2,6},{3,1},{4,0},{5,7},{6,2},{7,5}} | collective-permute-start | bytes 15728648 | tf_op jit(solution)/shard_map/ppermute | solution.py:417
  1937.5 142.7 %collective-permute-start.19 = (f32[64,5120]{1,0:T(8,128)}, f32[64,5120]{1,0:T(8,128)S(1)}, u32[]{:S(2)}, u32[]{:S(2)}) collective-permute-start(f32[64,5120]{1,0:T(8,128)} %get-tuple-element.75), channel_id=1, source_target_pairs={{0,4},{1,3},{2,6},{3,1},{4,0},{5,7},{6,2},{7,5}} | collective-permute-start | bytes 3932168 | tf_op jit(solution)/shard_map/ppermute | solution.py:417
  2080.2 197.9 %copy-start = (f32[64,5120]{1,0:T(8,128)}, f32[64,5120]{1,0:T(8,128)S(1)}, u32[]{:S(2)}) copy-start(f32[64,5120]{1,0:T(8,128)S(1)} %collective-permute-done.19.v_ref) | copy-start | bytes 3932164
  2080.2 197.9 %collective-permute-start.21 = (f32[448,5120]{1,0:T(8,128)}, f32[448,5120]{1,0:T(8,128)}, u32[]{:S(2)}, u32[]{:S(2)}) collective-permute-start(f32[448,5120]{1,0:T(8,128)} %get-tuple-element.77), channel_id=1, source_target_pairs={{0,4},{1,3},{2,6},{3,1},{4,0},{5,7},{6,2},{7,5}} | collective-permute-start | bytes 27525128 | tf_op jit(solution)/shard_map/ppermute | solution.py:417
  2081.7 560.9 %collective-permute-start.26 = (bf16[3072,5120]{1,0:T(8,128)(2,1)}, bf16[3072,5120]{1,0:T(8,128)(2,1)}, u32[]{:S(2)}, u32[]{:S(2)}) collective-permute-start(bf16[3072,5120]{1,0:T(8,128)(2,1)} %get-tuple-element.80.d_ref), channel_id=1, source_target_pairs={{0,1},{1,0},{2,3},{3,2},{4,5},{5,4},{6,7},{7,6}} | collective-permute-start | bytes 94371848 | tf_op jit(solution)/shard_map/ppermute | solution.py:420
  2081.7 424.1 %collective-permute-start.23 = (bf16[3072,3456]{1,0:T(8,128)(2,1)}, bf16[3072,3456]{1,0:T(8,128)(2,1)}, u32[]{:S(2)}, u32[]{:S(2)}) collective-permute-start(bf16[3072,3456]{1,0:T(8,128)(2,1)} %get-tuple-element.73.da_ref.d_ref), channel_id=1, source_target_pairs={{0,1},{1,0},{2,3},{3,2},{4,5},{5,4},{6,7},{7,6}} | collective-permute-start | bytes 63701000 | tf_op jit(solution)/shard_map/ppermute | solution.py:420
  2278.1 364.6 %collective-permute-start.25 = (bf16[3072,3456]{1,0:T(8,128)(2,1)}, bf16[3072,3456]{1,0:T(8,128)(2,1)}, u32[]{:S(2)}, u32[]{:S(2)}) collective-permute-start(bf16[3072,3456]{1,0:T(8,128)(2,1)} %get-tuple-element.79.h_ref), channel_id=1, source_target_pairs={{0,1},{1,0},{2,3},{3,2},{4,5},{5,4},{6,7},{7,6}} | collective-permute-start | bytes 63701000 | tf_op jit(solution)/shard_map/ppermute | solution.py:420

commit v4 on v3

--- a/solution.py
+++ b/solution.py
@@ -423,8 +423,9 @@
         i = lax.axis_index("dp").astype(jnp.int32).reshape(1)
         ka = 1792
         qa = 312
-        sizes = (448, 256, 64)
-        xX, xY = hop(x, 1, 1), hop(x, 2, 2)
+        sizes = (448, 256, 48, 16)
+        x1, x2 = hop(x, 1, 2), hop(x, 2, 1)
+        xX, xY = jnp.where(i[0] == 0, x1, x2), jnp.where(i[0] == 0, x2, x1)
         dyX, dyY = hop(dy, 1, 1), hop(dy, 2, 2)
         wgo, wuo, wdo = swap(wg), swap(wu), swap(wd)
         wXa, wXb = hop(wd[:ka], 1, 1), hop(wd[ka:], 1, 1)
@@ -465,7 +466,7 @@
         pre = k_add(i, z0, s1)[0]
         dx = ()
         for p, v in enumerate(s2):
-            dx = (k_fin(i, sum(sizes[:p]), pre, v, dx, 64 if p < 2 else 32),)
+            dx = (k_fin(i, sum(sizes[:p]), pre, v, dx, 64 if p < 2 else 16),)
         return y, dx[0], dwg, dwu, dwd
 
     return jax.shard_map(layer, mesh=mesh, in_specs=(rows, wsp, wsp, dsp, rows), out_specs=(rows, rows, wsp, wsp, dsp), check_vma=False)

time: 2770 us -> 2760 us (level)
    ppermute x17 -> x18, waiting for transfers between devices: 1170 us -> 1160 us  [hop(): return lax.ppermute(v, axes, pairs)]
    pallas_call x22 -> x23, Pallas kernels: 1330 us -> 1330 us  [call(): pl.pallas_call(body, grid_spec=pltpu.PrefetchScalarGridSpec(num_scalar_pr...]
  transfers between devices with their start and end apart: 27 -> 28, of which waited for: 8 -> 11; matrix products, arithmetic and copies ran while one was open for 1% -> 1% of each run, Pallas kernels for 43% -> 44%
where the time goes in v4:
time: 2760 us
  Pallas kernels  1330 us (48%)
  waiting for transfers between devices  1160 us (42%)
  starting transfers between devices  230 us (8%)
    pallas_call x23, Pallas kernels, call(): pl.pallas_call(body, grid_spec=pltpu.PrefetchScalarGridSpec(num_scalar_pr...  1330 us
    ppermute x18, waiting for transfers between devices, hop(): return lax.ppermute(v, axes, pairs)  1160 us
    ppermute x10, starting transfers between devices, swap(): return lax.ppermute(v, 'dp', [(0, 1), (1, 0)])  208 us
  transfers between devices with their start and end apart: 28, of which 11 were waited for; matrix products, arithmetic and copies ran while one was open for 1% of the time, Pallas kernels for 44%

profile of v4, /device:TPU:0, one launch (start us, length us, event | category | flops | bytes accessed | tf_op | source)
XLA Modules:
  0.0 2764.1 jit_solution(9914366662060696756)
XLA Ops:
  6.5 167.0 %collective-permute-done.14.refs_1_ = bf16[768,5120]{1,0:T(8,128)(2,1)} collective-permute-done((bf16[768,5120]{1,0:T(8,128)(2,1)}, bf16[768,5120]{1,0:T(8,128)(2,1)}, u32[]{:S(2)}, u32[]{:S(2)}) %collective-permute-start.14) | collective-permute-done | bytes 7864352 | tf_op jit(solution)/shard_map/ppermute | solution.py:417
  187.8 152.0 %collective-permute-done.3 = bf16[768,5120]{1,0:T(8,128)(2,1)} collective-permute-done((bf16[768,5120]{1,0:T(8,128)(2,1)}, bf16[768,5120]{1,0:T(8,128)(2,1)}, u32[]{:S(2)}, u32[]{:S(2)}) %collective-permute-start.3) | collective-permute-done | bytes 7864352 | tf_op jit(solution)/shard_map/ppermute | solution.py:417
  351.9 56.4 %collective-permute-done.16 = bf16[312,5120]{1,0:T(8,128)(2,1)} collective-permute-done((bf16[312,5120]{1,0:T(8,128)(2,1)S(1)}, bf16[312,5120]{1,0:T(8,128)(2,1)}, u32[]{:S(2)}, u32[]{:S(2)}) %collective-permute-start.16) | collective-permute-done | bytes 3194912 | tf_op jit(solution)/shard_map/ppermute | solution.py:417
  410.4 70.2 %collective-permute-done.17 = bf16[456,5120]{1,0:T(8,128)(2,1)} collective-permute-done((bf16[456,5120]{1,0:T(8,128)(2,1)S(1)}, bf16[456,5120]{1,0:T(8,128)(2,1)}, u32[]{:S(2)}, u32[]{:S(2)}) %collective-permute-start.17) | collective-permute-done | bytes 4669472 | tf_op jit(solution)/shard_map/ppermute | solution.py:417
  480.6 11.1 broadcast_select_fusion
  498.7 256.8 %collective-permute-done.7.rest_1_ = bf16[1664,2560]{1,0:T(8,128)(2,1)} collective-permute-done((bf16[1664,2560]{1,0:T(8,128)(2,1)}, bf16[1664,2560]{1,0:T(8,128)(2,1)}, u32[]{:S(2)}, u32[]{:S(2)}) %collective-permute-start.7) | collective-permute-done | bytes 8519712 | tf_op jit(solution)/shard_map/ppermute | solution.py:417
  757.7 70.3 %shard_map.92 = (f32[768,3456]{1,0:T(8,128)}, f32[768,3456]{1,0:T(8,128)}, bf16[768,3456]{1,0:T(8,128)(2,1)}, bf16[3072,3456]{1,0:T(8,128)(2,1)}, bf16[3072,5120...) custom-call(s32[1]{0:T(128)} %bitcast.i_ref.refs_0_, bf16[768,5120]{1,0:T(8,128)(2,1)} %rest_4_.1, ...), custom_call_target="tpu_custom_call" | custom-call | flops 54358179840 | bytes 78643200 | tf_op jit(solution)/shard_map/pallas_call | solution.py:46
  828.1 68.9 %shard_map.94 = (f32[768,3456]{1,0:T(8,128)}, f32[768,3456]{1,0:T(8,128)}, bf16[768,3456]{1,0:T(8,128)(2,1)}, bf16[3072,3456]{1,0:T(8,128)(2,1)}, bf16[3072,5120]{1,0:T(8,128)(2,1)}) custom-call(s32[1]{0:T(128)} %bitcast.i_ref.refs_0_, bf16[768,5120]{1,0:T(8,128)(2,1)} %get-tuple-element.84.x_ref, ...), custom_call_target="tpu_custom_call", output_to_operand_aliasing={{3}: (4, {}), {4}: (5, {})} | custom-call | flops 54358179840 | bytes 131334144 | tf_op jit(solution)/shard_map/pallas_call | solution.py:46
  897.0 68.9 %shard_map.95 = (f32[768,3456]{1,0:T(8,128)}, f32[768,3456]{1,0:T(8,128)}, bf16[768,3456]{1,0:T(8,128)(2,1)}, bf16[3072,3456]{1,0:T(8,128)(2,1)}, bf16[3072,5120]{1,0:T(8,128)(2,1)}) custom-call(s32[1]{0:T(128)} %bitcast.i_ref.refs_0_, bf16[768,5120]{1,0:T(8,128)(2,1)} %get-tuple-element.83.x_ref, ...), custom_call_target="tpu_custom_call", output_to_operand_aliasing={{3}: (4, {}), {4}: (5, {})} | custom-call | flops 54358179840 | bytes 131334144 | tf_op jit(solution)/shard_map/pallas_call | solution.py:46
  966.0 44.3 %shard_map.93 = (bf16[3072,3456]{1,0:T(8,128)(2,1)}, bf16[3072,3456]{1,0:T(8,128)(2,1)}, bf16[3072,5120]{1,0:T(8,128)(2,1)}, bf16[3456,5120]{1,0:T(8,128)(2,1)}) custom-call(s32[1]{0:T(128)} %bitcast.i_ref.refs_0_, bf16[768,5120]{1,0:T(8,128)(2,1)} %rest_0_.1, bf16[3456,2560]{1,0:T(8,128)(2,1)} %w_ref.1, bf16[3456,2560]{1,0:T(8,128)(2,1)} %collective-permute-done.2.wo_ref, ...), custom_call_target="tpu_custom_call" | custom-call | flops 27179089920 | bytes 64487424 | tf_op jit(solution)/shard_map/pallas_call | solution.py:46
  1010.3 41.9 %shard_map.99 = (bf16[3072,3456]{1,0:T(8,128)(2,1)}, bf16[3072,3456]{1,0:T(8,128)(2,1)}, bf16[3072,5120]{1,0:T(8,128)(2,1)}) custom-call(s32[1]{0:T(128)} %bitcast.i_ref.refs_0_, bf16[768,5120]{1,0:T(8,128)(2,1)} %collective-permute-done.14.refs_1_, ...), custom_call_target="tpu_custom_call", output_to_operand_aliasing={{0}: (5, {}), {1}: (6, {}), {2}: (7, {})} | custom-call | flops 27179089920 | bytes 138412032 | tf_op jit(solution)/shard_map/pallas_call | solution.py:46
  1052.2 41.9 %shard_map.100 = (bf16[3072,3456]{1,0:T(8,128)(2,1)}, bf16[3072,3456]{1,0:T(8,128)(2,1)}, bf16[3072,5120]{1,0:T(8,128)(2,1)}) custom-call(s32[1]{0:T(128)} %bitcast.i_ref.refs_0_, bf16[768,5120]{1,0:T(8,128)(2,1)} %collective-permute-done.13.refs_1_, ...), custom_call_target="tpu_custom_call", output_to_operand_aliasing={{0}: (5, {}), {1}: (6, {}), {2}: (7, {})} | custom-call | flops 27179089920 | bytes 138412032 | tf_op jit(solution)/shard_map/pallas_call | solution.py:46
  1094.1 70.4 %shard_map.102.refs_9_ = f32[768,5120]{1,0:T(8,128)} custom-call(s32[1]{0:T(128)} %bitcast.i_ref.refs_0_, bf16[3072,3456]{1,0:T(8,128)(2,1)} %get-tuple-element.69.da_ref.refs_5_, bf16[3072,3456]{1,0:T(8,128)(2,1)} %get-tuple-element.70.db_ref.refs_6_, bf16[5120,3456]{1,0:T(8,128)(2,1)} %get-tuple-element.48.wg_ref, bf16[5120,3456]{1,0:T(8,128)(2,1)} %get-tuple-element.49.wu_ref), custom_call_target="tpu_custom_call" | custom-call | flops 54358179840 | bytes 113246208 | tf_op jit(solution)/shard_map/pallas_call | solution.py:46
  1164.5 72.8 %shard_map.101.u_ref.refs_8_ = f32[768,5120]{1,0:T(8,128)} custom-call(s32[1]{0:T(128)} %bitcast.i_ref.refs_0_, bf16[3072,3456]{1,0:T(8,128)(2,1)} %get-tuple-element.69.da_ref.refs_5_, bf16[3072,3456]{1,0:T(8,128)(2,1)} %get-tuple-element.70.db_ref.refs_6_, bf16[5120,3456]{1,0:T(8,128)(2,1)} %get-tuple-element.48.wg_ref, ...), custom_call_target="tpu_custom_call" | custom-call | flops 54358179840 | bytes 121110528 | tf_op jit(solution)/shard_map/pallas_call | solution.py:46
  1237.3 69.0 %shard_map.96 = (f32[768,3456]{1,0:T(8,128)}, f32[768,3456]{1,0:T(8,128)}, bf16[768,3456]{1,0:T(8,128)(2,1)}, bf16[3072,3456]{1,0:T(8,128)(2,1)}, bf16[3072,5120]{1,0:T(8,128)(2,1)}) custom-call(s32[1]{0:T(128)} %bitcast.i_ref.refs_0_, bf16[768,5120]{1,0:T(8,128)(2,1)} %collective-permute-done.10.x_ref, ...), custom_call_target="tpu_custom_call", output_to_operand_aliasing={{3}: (4, {}), {4}: (5, {})} | custom-call | flops 54358179840 | bytes 131334144 | tf_op jit(solution)/shard_map/pallas_call | solution.py:46
  1307.9 41.8 %shard_map.104 = (bf16[3072,3456]{1,0:T(8,128)(2,1)}, bf16[3072,3456]{1,0:T(8,128)(2,1)}, bf16[3072,5120]{1,0:T(8,128)(2,1)}) custom-call(s32[1]{0:T(128)} %bitcast.i_ref.refs_0_, bf16[768,5120]{1,0:T(8,128)(2,1)} %pad_maximum_fusion.refs_1_, ...), custom_call_target="tpu_custom_call", output_to_operand_aliasing={{0}: (5, {}), {1}: (6, {}), {2}: (7, {})} | custom-call | flops 27179089920 | bytes 169869312 | tf_op jit(solution)/shard_map/pallas_call | solution.py:46
  1349.7 70.2 %shard_map.106 = f32[768,5120]{1,0:T(8,128)} custom-call(s32[1]{0:T(128)} %bitcast.i_ref.refs_0_, bf16[3072,3456]{1,0:T(8,128)(2,1)} %get-tuple-element.74.da_ref.d_ref, bf16[3072,3456]{1,0:T(8,128)(2,1)} %get-tuple-element.75.db_ref.d_ref, bf16[5120,3456]{1,0:T(8,128)(2,1)} %get-tuple-element.48.wg_ref, bf16[5120,3456]{1,0:T(8,128)(2,1)} %get-tuple-element.49.wu_ref), custom_call_target="tpu_custom_call" | custom-call | flops 54358179840 | bytes 113246208 | tf_op jit(solution)/shard_map/pallas_call | solution.py:46
  1423.3 71.5 %shard_map.97 = f32[768,5120]{1,0:T(8,128)} custom-call(s32[1]{0:T(128)} %bitcast.i_ref.refs_0_, bf16[768,3456]{1,0:T(8,128)(2,1)} %get-tuple-element.55.h_ref, bf16[3456,5120]{1,0:T(8,128)(2,1)} %get-tuple-element.47.w_ref.refs_2_, bf16[768,3456]{1,0:T(8,128)(2,1)} %collective-permute-done.11.hr_ref, bf16[1792,2560]{1,0:T(8,128)(2,1)} %collective-permute-done.6.rest_0_, ...), custom_call_target="tpu_custom_call" | custom-call | flops 54358179840 | bytes 81395712 | tf_op jit(solution)/shard_map/pallas_call | solution.py:46
  1496.8 152.3 %collective-permute-done.18.v_ref = f32[768,5120]{1,0:T(8,128)} collective-permute-done((f32[768,5120]{1,0:T(8,128)}, f32[768,5120]{1,0:T(8,128)}, u32[]{:S(2)}, u32[]{:S(2)}) %collective-permute-start.18) | collective-permute-done | bytes 15728672 | tf_op jit(solution)/shard_map/ppermute | solution.py:417
  1649.2 34.8 %collective-permute-start.25 = (bf16[3072,3456]{1,0:T(8,128)(2,1)}, bf16[3072,3456]{1,0:T(8,128)(2,1)}, u32[]{:S(2)}, u32[]{:S(2)}) collective-permute-start(bf16[3072,3456]{1,0:T(8,128)(2,1)} %get-tuple-element.75.db_ref.d_ref), channel_id=1, source_target_pairs={{0,1},{1,0},{2,3},{3,2},{4,5},{5,4},{6,7},{7,6}} | collective-permute-start | bytes 63701000 | tf_op jit(solution)/shard_map/ppermute | solution.py:420
  1684.0 70.5 %shard_map.105.u_ref = f32[768,5120]{1,0:T(8,128)} custom-call(s32[1]{0:T(128)} %bitcast.i_ref.refs_0_, bf16[3072,3456]{1,0:T(8,128)(2,1)} %get-tuple-element.74.da_ref.d_ref, bf16[3072,3456]{1,0:T(8,128)(2,1)} %get-tuple-element.75.db_ref.d_ref, bf16[5120,3456]{1,0:T(8,128)(2,1)} %get-tuple-element.48.wg_ref, bf16[5120,3456]{1,0:T(8,128)(2,1)} %get-tuple-element.49.wu_ref), custom_call_target="tpu_custom_call" | custom-call | flops 54358179840 | bytes 113246208 | tf_op jit(solution)/shard_map/pallas_call | solution.py:46
  1754.5 17.4 shard_map.107
  1771.9 158.9 %collective-permute-done.5.hr_ref = bf16[768,3456]{1,0:T(8,128)(2,1)} collective-permute-done((bf16[768,3456]{1,0:T(8,128)(2,1)}, bf16[768,3456]{1,0:T(8,128)(2,1)}, u32[]{:S(2)}, u32[]{:S(2)}) %collective-permute-start.5) | collective-permute-done | bytes 5308448 | tf_op jit(solution)/shard_map/ppermute | solution.py:417
  1932.8 121.1 %collective-permute-done.19.v_ref = f32[16,5120]{1,0:T(8,128)S(1)} collective-permute-done((f32[16,5120]{1,0:T(8,128)}, f32[16,5120]{1,0:T(8,128)S(1)}, u32[]{:S(2)}, u32[]{:S(2)}) %collective-permute-start.19) | collective-permute-done | bytes 327712 | tf_op jit(solution)/shard_map/ppermute | solution.py:417
  2054.4 24.3 collective-permute-done.20.v_ref
  2079.3 172.5 %collective-permute-start.24 = (bf16[3072,3456]{1,0:T(8,128)(2,1)}, bf16[3072,3456]{1,0:T(8,128)(2,1)}, u32[]{:S(2)}, u32[]{:S(2)}) collective-permute-start(bf16[3072,3456]{1,0:T(8,128)(2,1)} %get-tuple-element.74.da_ref.d_ref), channel_id=1, source_target_pairs={{0,1},{1,0},{2,3},{3,2},{4,5},{5,4},{6,7},{7,6}} | collective-permute-start | bytes 63701000 | tf_op jit(solution)/shard_map/ppermute | solution.py:420
  2251.7 17.4 shard_map.103.u_ref
  2269.2 72.4 %shard_map.98 = bf16[768,5120]{1,0:T(8,128)(2,1)} custom-call(s32[1]{0:T(128)} %bitcast.i_ref.refs_0_, bf16[768,3456]{1,0:T(8,128)(2,1)} %get-tuple-element.44.h_ref, bf16[3456,5120]{1,0:T(8,128)(2,1)} %get-tuple-element.47.w_ref.refs_2_, bf16[768,3456]{1,0:T(8,128)(2,1)} %collective-permute-done.5.hr_ref, ...), custom_call_target="tpu_custom_call" | custom-call | flops 54358179840 | bytes 104988672 | tf_op jit(solution)/shard_map/pallas_call | solution.py:46
  2341.5 10.0 shard_map.108.rest_0_
  2362.2 137.1 %shard_map.113 = f32[2560,3456]{1,0:T(8,128)} custom-call(s32[1]{0:T(128)} %bitcast.i_ref.refs_0_, bf16[3072,5120]{1,0:T(8,128)(2,1)} %get-tuple-element.80.x_ref, bf16[3072,5120]{1,0:T(8,128)(2,1)} %collective-permute-done.23.xo_ref, bf16[3072,3456]{1,0:T(8,128)(2,1)} %get-tuple-element.75.db_ref.d_ref, bf16[3072,3456]{1,0:T(8,128)(2,1)} %collective-permute-done.25.do_ref), custom_call_target="tpu_custom_call" | custom-call | flops 108716359680 | bytes 105381888 | tf_op jit(solution)/shard_map/pallas_call | solution.py:46
  2499.3 137.0 %shard_map.112 = f32[2560,3456]{1,0:T(8,128)} custom-call(s32[1]{0:T(128)} %bitcast.i_ref.refs_0_, bf16[3072,5120]{1,0:T(8,128)(2,1)} %get-tuple-element.80.x_ref, bf16[3072,5120]{1,0:T(8,128)(2,1)} %collective-permute-done.23.xo_ref, bf16[3072,3456]{1,0:T(8,128)(2,1)} %get-tuple-element.74.da_ref.d_ref, bf16[3072,3456]{1,0:T(8,128)(2,1)} %collective-permute-done.24.do_ref), custom_call_target="tpu_custom_call" | custom-call | flops 108716359680 | bytes 105381888 | tf_op jit(solution)/shard_map/pallas_call | solution.py:46
  2636.3 127.8 %shard_map.114 = f32[3456,2560]{1,0:T(8,128)} custom-call(s32[1]{0:T(128)} %bitcast.i_ref.refs_0_, bf16[3072,3456]{1,0:T(8,128)(2,1)} %get-tuple-element.81.h_ref, bf16[3072,3456]{1,0:T(8,128)(2,1)} %collective-permute-done.26.ho_ref, bf16[3072,5120]{1,0:T(8,128)(2,1)} %get-tuple-element.82.d_ref, bf16[3072,5120]{1,0:T(8,128)(2,1)} %collective-permute-done.27.do_ref), custom_call_target="tpu_custom_call" | custom-call | flops 108716359680 | bytes 105381888 | tf_op jit(solution)/shard_map/pallas_call | solution.py:46
  (57 shorter events, 64.3 us)
Async XLA Ops:
  0.6 172.9 %collective-permute-start.14 = (bf16[768,5120]{1,0:T(8,128)(2,1)}, bf16[768,5120]{1,0:T(8,128)(2,1)}, u32[]{:S(2)}, u32[]{:S(2)}) collective-permute-start(bf16[768,5120]{1,0:T(8,128)(2,1)} %rest_0_.1), channel_id=1, source_target_pairs={{0,2},{1,3},{2,0},{3,1},{4,6},{5,7},{6,4},{7,5}} | collective-permute-start | bytes 23592968 | tf_op jit(solution)/shard_map/ppermute | solution.py:417
  4.0 172.4 %collective-permute-start.13 = (bf16[768,5120]{1,0:T(8,128)(2,1)}, bf16[768,5120]{1,0:T(8,128)(2,1)}, u32[]{:S(2)}, u32[]{:S(2)}) collective-permute-start(bf16[768,5120]{1,0:T(8,128)(2,1)} %rest_0_.1), channel_id=1, source_target_pairs={{0,4},{1,5},{2,6},{3,7},{4,0},{5,1},{6,2},{7,3}} | collective-permute-start | bytes 23592968 | tf_op jit(solution)/shard_map/ppermute | solution.py:417
  5.5 751.8 %collective-permute-start = (bf16[2560,3456]{1,0:T(8,128)(2,1)}, bf16[2560,3456]{1,0:T(8,128)(2,1)}, u32[]{:S(2)}, u32[]{:S(2)}) collective-permute-start(bf16[2560,3456]{1,0:T(8,128)(2,1)} %wg_ref.1), channel_id=1, source_target_pairs={{0,1},{1,0},{2,3},{3,2},{4,5},{5,4},{6,7},{7,6}} | collective-permute-start | bytes 53084168 | tf_op jit(solution)/shard_map/ppermute | solution.py:420
  5.5 752.3 %collective-permute-start.1 = (bf16[2560,3456]{1,0:T(8,128)(2,1)}, bf16[2560,3456]{1,0:T(8,128)(2,1)}, u32[]{:S(2)}, u32[]{:S(2)}) collective-permute-start(bf16[2560,3456]{1,0:T(8,128)(2,1)} %wu_ref.1), channel_id=1, source_target_pairs={{0,1},{1,0},{2,3},{3,2},{4,5},{5,4},{6,7},{7,6}} | collective-permute-start | bytes 53084168 | tf_op jit(solution)/shard_map/ppermute | solution.py:420
  6.0 333.9 %collective-permute-start.3 = (bf16[768,5120]{1,0:T(8,128)(2,1)}, bf16[768,5120]{1,0:T(8,128)(2,1)}, u32[]{:S(2)}, u32[]{:S(2)}) collective-permute-start(bf16[768,5120]{1,0:T(8,128)(2,1)} %rest_4_.1), channel_id=1, source_target_pairs={{0,2},{1,5},{2,0},{3,7},{4,6},{5,1},{6,4},{7,3}} | collective-permute-start | bytes 23592968 | tf_op jit(solution)/shard_map/ppermute | solution.py:417
  173.5 175.8 %collective-permute-start.4 = (bf16[768,5120]{1,0:T(8,128)(2,1)}, bf16[768,5120]{1,0:T(8,128)(2,1)}, u32[]{:S(2)}, u32[]{:S(2)}) collective-permute-start(bf16[768,5120]{1,0:T(8,128)(2,1)} %rest_4_.1), channel_id=1, source_target_pairs={{0,4},{1,3},{2,6},{3,1},{4,0},{5,7},{6,2},{7,5}} | collective-permute-start | bytes 23592968 | tf_op jit(solution)/shard_map/ppermute | solution.py:417
  179.6 228.7 %collective-permute-start.16 = (bf16[312,5120]{1,0:T(8,128)(2,1)S(1)}, bf16[312,5120]{1,0:T(8,128)(2,1)}, u32[]{:S(2)}, u32[]{:S(2)}) collective-permute-start(bf16[312,5120]{1,0:T(8,128)(2,1)S(1)} %slice_select_fusion), channel_id=1, source_target_pairs={{0,2},{1,5},{2,0},{3,7},{4,6},{5,1},{6,4},{7,3}} | collective-permute-start | bytes 9584648 | tf_op jit(solution)/shard_map/ppermute | solution.py:417
  339.9 417.4 %collective-permute-start.6 = (bf16[1792,2560]{1,0:T(8,128)(2,1)}, bf16[1792,2560]{1,0:T(8,128)(2,1)}, u32[]{:S(2)}, u32[]{:S(2)}) collective-permute-start(bf16[1792,2560]{1,0:T(8,128)(2,1)} %slice.15), channel_id=1, source_target_pairs={{0,2},{1,3},{2,0},{3,1},{4,6},{5,7},{6,4},{7,5}} | collective-permute-start | bytes 27525128 | tf_op jit(solution)/shard_map/ppermute | solution.py:417
  349.3 406.2 %collective-permute-start.7 = (bf16[1664,2560]{1,0:T(8,128)(2,1)}, bf16[1664,2560]{1,0:T(8,128)(2,1)}, u32[]{:S(2)}, u32[]{:S(2)}) collective-permute-start(bf16[1664,2560]{1,0:T(8,128)(2,1)} %slice.16), channel_id=1, source_target_pairs={{0,2},{1,3},{2,0},{3,1},{4,6},{5,7},{6,4},{7,5}} | collective-permute-start | bytes 25559048 | tf_op jit(solution)/shard_map/ppermute | solution.py:417
  408.3 72.3 %collective-permute-start.17 = (bf16[456,5120]{1,0:T(8,128)(2,1)S(1)}, bf16[456,5120]{1,0:T(8,128)(2,1)}, u32[]{:S(2)}, u32[]{:S(2)}) collective-permute-start(bf16[456,5120]{1,0:T(8,128)(2,1)S(1)} %slice.22), channel_id=1, source_target_pairs={{0,4},{1,5},{2,6},{3,7},{4,0},{5,1},{6,2},{7,3}} | collective-permute-start | bytes 14008328 | tf_op jit(solution)/shard_map/ppermute | solution.py:417
  480.6 485.4 %collective-permute-start.2 = (bf16[3456,2560]{1,0:T(8,128)(2,1)}, bf16[3456,2560]{1,0:T(8,128)(2,1)}, u32[]{:S(2)}, u32[]{:S(2)}) collective-permute-start(bf16[3456,2560]{1,0:T(8,128)(2,1)} %w_ref.1), channel_id=1, source_target_pairs={{0,1},{1,0},{2,3},{3,2},{4,5},{5,4},{6,7},{7,6}} | collective-permute-start | bytes 53084168 | tf_op jit(solution)/shard_map/ppermute | solution.py:420
  755.5 481.9 %collective-permute-start.10 = (bf16[768,5120]{1,0:T(8,128)(2,1)}, bf16[768,5120]{1,0:T(8,128)(2,1)}, u32[]{:S(2)}, u32[]{:S(2)}) collective-permute-start(bf16[768,5120]{1,0:T(8,128)(2,1)} %get-tuple-element.84.x_ref), channel_id=1, source_target_pairs={{0,4},{1,5},{2,6},{3,7},{4,0},{5,1},{6,2},{7,3}} | collective-permute-start | bytes 23592968 | tf_op jit(solution)/shard_map/ppermute | solution.py:417
  757.2 664.7 %collective-permute-start.9 = (bf16[1664,2560]{1,0:T(8,128)(2,1)}, bf16[1664,2560]{1,0:T(8,128)(2,1)}, u32[]{:S(2)}, u32[]{:S(2)}) collective-permute-start(bf16[1664,2560]{1,0:T(8,128)(2,1)} %collective-permute-done.7.rest_1_), channel_id=1, source_target_pairs={{0,1},{1,0},{2,3},{3,2},{4,5},{5,4},{6,7},{7,6}} | collective-permute-start | bytes 25559048 | tf_op jit(solution)/shard_map/ppermute | solution.py:420
  757.2 664.7 %collective-permute-start.8 = (bf16[1792,2560]{1,0:T(8,128)(2,1)}, bf16[1792,2560]{1,0:T(8,128)(2,1)}, u32[]{:S(2)}, u32[]{:S(2)}) collective-permute-start(bf16[1792,2560]{1,0:T(8,128)(2,1)} %collective-permute-done.6.rest_0_), channel_id=1, source_target_pairs={{0,1},{1,0},{2,3},{3,2},{4,5},{5,4},{6,7},{7,6}} | collective-permute-start | bytes 27525128 | tf_op jit(solution)/shard_map/ppermute | solution.py:420
  1306.4 117.0 %collective-permute-start.11 = (bf16[768,3456]{1,0:T(8,128)(2,1)}, bf16[768,3456]{1,0:T(8,128)(2,1)}, u32[]{:S(2)}, u32[]{:S(2)}) collective-permute-start(bf16[768,3456]{1,0:T(8,128)(2,1)} %get-tuple-element.58), channel_id=1, source_target_pairs={{0,2},{1,3},{2,0},{3,1},{4,6},{5,7},{6,4},{7,5}} | collective-permute-start | bytes 15925256 | tf_op jit(solution)/shard_map/ppermute | solution.py:417
  1419.9 229.3 %collective-permute-start.18 = (f32[768,5120]{1,0:T(8,128)}, f32[768,5120]{1,0:T(8,128)}, u32[]{:S(2)}, u32[]{:S(2)}) collective-permute-start(f32[768,5120]{1,0:T(8,128)} %shard_map.106), channel_id=1, source_target_pairs={{0,2},{1,5},{2,0},{3,7},{4,6},{5,1},{6,4},{7,3}} | collective-permute-start | bytes 47185928 | tf_op jit(solution)/shard_map/ppermute | solution.py:417
  1420.4 510.9 %collective-permute-start.15 = (f32[768,5120]{1,0:T(8,128)}, f32[768,5120]{1,0:T(8,128)}, u32[]{:S(2)}, u32[]{:S(2)}) collective-permute-start(f32[768,5120]{1,0:T(8,128)} %shard_map.102.refs_9_), channel_id=1, source_target_pairs={{0,2},{1,5},{2,0},{3,7},{4,6},{5,1},{6,4},{7,3}} | collective-permute-start | bytes 47185928 | tf_op jit(solution)/shard_map/ppermute | solution.py:417
  1421.9 940.3 %collective-permute-start.23 = (bf16[3072,5120]{1,0:T(8,128)(2,1)}, bf16[3072,5120]{1,0:T(8,128)(2,1)}, u32[]{:S(2)}, u32[]{:S(2)}) collective-permute-start(bf16[3072,5120]{1,0:T(8,128)(2,1)} %get-tuple-element.80.x_ref), channel_id=1, source_target_pairs={{0,1},{1,0},{2,3},{3,2},{4,5},{5,4},{6,7},{7,6}} | collective-permute-start | bytes 94371848 | tf_op jit(solution)/shard_map/ppermute | solution.py:420
  1494.8 584.4 %collective-permute-start.12 = (f32[768,5120]{1,0:T(8,128)}, f32[768,5120]{1,0:T(8,128)}, u32[]{:S(2)}, u32[]{:S(2)}) collective-permute-start(f32[768,5120]{1,0:T(8,128)} %shard_map.97), channel_id=1, source_target_pairs={{0,4},{1,5},{2,6},{3,7},{4,0},{5,1},{6,2},{7,3}} | collective-permute-start | bytes 47185928 | tf_op jit(solution)/shard_map/ppermute | solution.py:417
  1495.1 435.7 %collective-permute-start.5 = (bf16[768,3456]{1,0:T(8,128)(2,1)}, bf16[768,3456]{1,0:T(8,128)(2,1)}, u32[]{:S(2)}, u32[]{:S(2)}) collective-permute-start(bf16[768,3456]{1,0:T(8,128)(2,1)} %get-tuple-element.52), channel_id=1, source_target_pairs={{0,2},{1,3},{2,0},{3,1},{4,6},{5,7},{6,4},{7,5}} | collective-permute-start | bytes 15925256 | tf_op jit(solution)/shard_map/ppermute | solution.py:417
  1649.2 713.1 %collective-permute-start.25 = (bf16[3072,3456]{1,0:T(8,128)(2,1)}, bf16[3072,3456]{1,0:T(8,128)(2,1)}, u32[]{:S(2)}, u32[]{:S(2)}) collective-permute-start(bf16[3072,3456]{1,0:T(8,128)(2,1)} %get-tuple-element.75.db_ref.d_ref), channel_id=1, source_target_pairs={{0,1},{1,0},{2,3},{3,2},{4,5},{5,4},{6,7},{7,6}} | collective-permute-start | bytes 63701000 | tf_op jit(solution)/shard_map/ppermute | solution.py:420
  1930.8 148.5 %collective-permute-start.21 = (f32[256,5120]{1,0:T(8,128)}, f32[256,5120]{1,0:T(8,128)}, u32[]{:S(2)}, u32[]{:S(2)}) collective-permute-start(f32[256,5120]{1,0:T(8,128)} %get-tuple-element.78), channel_id=1, source_target_pairs={{0,4},{1,3},{2,6},{3,1},{4,0},{5,7},{6,2},{7,5}} | collective-permute-start | bytes 15728648 | tf_op jit(solution)/shard_map/ppermute | solution.py:417
  1931.3 122.6 %collective-permute-start.19 = (f32[16,5120]{1,0:T(8,128)}, f32[16,5120]{1,0:T(8,128)S(1)}, u32[]{:S(2)}, u32[]{:S(2)}) collective-permute-start(f32[16,5120]{1,0:T(8,128)} %get-tuple-element.76), channel_id=1, source_target_pairs={{0,4},{1,3},{2,6},{3,1},{4,0},{5,7},{6,2},{7,5}} | collective-permute-start | bytes 983048 | tf_op jit(solution)/shard_map/ppermute | solution.py:417
  2053.9 215.2 %copy-start.1 = (f32[16,5120]{1,0:T(8,128)}, f32[16,5120]{1,0:T(8,128)S(1)}, u32[]{:S(2)}) copy-start(f32[16,5120]{1,0:T(8,128)S(1)} %collective-permute-done.19.v_ref) | copy-start | bytes 983044
  2053.9 24.8 collective-permute-start.20
  2078.7 190.4 %copy-start = (f32[48,5120]{1,0:T(8,128)}, f32[48,5120]{1,0:T(8,128)S(1)}, u32[]{:S(2)}) copy-start(f32[48,5120]{1,0:T(8,128)S(1)} %collective-permute-done.20.v_ref) | copy-start | bytes 2949124
  2078.8 190.4 %collective-permute-start.22 = (f32[448,5120]{1,0:T(8,128)}, f32[448,5120]{1,0:T(8,128)}, u32[]{:S(2)}, u32[]{:S(2)}) collective-permute-start(f32[448,5120]{1,0:T(8,128)} %get-tuple-element.79), channel_id=1, source_target_pairs={{0,4},{1,3},{2,6},{3,1},{4,0},{5,7},{6,2},{7,5}} | collective-permute-start | bytes 27525128 | tf_op jit(solution)/shard_map/ppermute | solution.py:417
  2079.3 557.0 %collective-permute-start.27 = (bf16[3072,5120]{1,0:T(8,128)(2,1)}, bf16[3072,5120]{1,0:T(8,128)(2,1)}, u32[]{:S(2)}, u32[]{:S(2)}) collective-permute-start(bf16[3072,5120]{1,0:T(8,128)(2,1)} %get-tuple-element.82.d_ref), channel_id=1, source_target_pairs={{0,1},{1,0},{2,3},{3,2},{4,5},{5,4},{6,7},{7,6}} | collective-permute-start | bytes 94371848 | tf_op jit(solution)/shard_map/ppermute | solution.py:420
  2079.3 420.1 %collective-permute-start.24 = (bf16[3072,3456]{1,0:T(8,128)(2,1)}, bf16[3072,3456]{1,0:T(8,128)(2,1)}, u32[]{:S(2)}, u32[]{:S(2)}) collective-permute-start(bf16[3072,3456]{1,0:T(8,128)(2,1)} %get-tuple-element.74.da_ref.d_ref), channel_id=1, source_target_pairs={{0,1},{1,0},{2,3},{3,2},{4,5},{5,4},{6,7},{7,6}} | collective-permute-start | bytes 63701000 | tf_op jit(solution)/shard_map/ppermute | solution.py:420
  2269.1 367.2 %collective-permute-start.26 = (bf16[3072,3456]{1,0:T(8,128)(2,1)}, bf16[3072,3456]{1,0:T(8,128)(2,1)}, u32[]{:S(2)}, u32[]{:S(2)}) collective-permute-start(bf16[3072,3456]{1,0:T(8,128)(2,1)} %get-tuple-element.81.h_ref), channel_id=1, source_target_pairs={{0,1},{1,0},{2,3},{3,2},{4,5},{5,4},{6,7},{7,6}} | collective-permute-start | bytes 63701000 | tf_op jit(solution)/shard_map/ppermute | solution.py:420

commit v5 on v4

--- a/solution.py
+++ b/solution.py
@@ -422,17 +422,22 @@
     def layer(x, wg, wu, wd, dy):
         i = lax.axis_index("dp").astype(jnp.int32).reshape(1)
         ka = 1792
-        qa = 312
-        sizes = (448, 256, 48, 16)
+        qa = 304
+        sizes = (432, 288, 32, 16)
         x1, x2 = hop(x, 1, 2), hop(x, 2, 1)
         xX, xY = jnp.where(i[0] == 0, x1, x2), jnp.where(i[0] == 0, x2, x1)
         dyX, dyY = hop(dy, 1, 1), hop(dy, 2, 2)
         wgo, wuo, wdo = swap(wg), swap(wu), swap(wd)
         wXa, wXb = hop(wd[:ka], 1, 1), hop(wd[ka:], 1, 1)
         xD = hop(xX, 2, 2)
-        dyDa = hop(jnp.where(i[0] == 0, dyY[:qa], dyX[:qa]), 1, 2)
-        dyDb = hop(dyX[qa:], 2, 2)
-        dyD = jnp.concatenate([dyDa, dyDb], axis=0)
+        qb = qa + 8
+        hd = wg.shape[0]
+        part = jnp.where(i[0] == 0, dyY[:qb], dyX[:qb])
+        dyDa = hop(part[:qa], 1, 2)
+        dyDc = hop(part[qa:, :hd], 1, 2)
+        dyDe = hop(dyX[qa:qb, hd:], 2, 2)
+        dyDb = hop(dyX[qb:], 2, 2)
+        dyD = jnp.concatenate([dyDa, jnp.concatenate([dyDc, dyDe], axis=1), dyDb], axis=0)
         wX = (wXa, wXb, swap(wXa), swap(wXb))
 
         a0, b0, h0, hall, xall, wgc, wuc = k_fwd0(i, x, wg, wgo, wu, wuo)
@@ -466,7 +471,7 @@
         pre = k_add(i, z0, s1)[0]
         dx = ()
         for p, v in enumerate(s2):
-            dx = (k_fin(i, sum(sizes[:p]), pre, v, dx, 64 if p < 2 else 16),)
+            dx = (k_fin(i, sum(sizes[:p]), pre, v, dx, 48 if p < 2 else 16),)
         return y, dx[0], dwg, dwu, dwd
 
     return jax.shard_map(layer, mesh=mesh, in_specs=(rows, wsp, wsp, dsp, rows), out_specs=(rows, rows, wsp, wsp, dsp), check_vma=False)

time: 2760 us -> 2770 us (level)
  starting transfers between devices: 230 us -> 27.8 us
  waiting for transfers between devices: 1160 us -> 1360 us
    ppermute x10, starting transfers between devices: 208 us -> 1.54 us  [swap(): return lax.ppermute(v, 'dp', [(0, 1), (1, 0)])]
    ppermute x18 -> x20, waiting for transfers between devices: 1160 us -> 1360 us  [hop(): return lax.ppermute(v, axes, pairs)]
  transfers between devices with their start and end apart: 28 -> 30, of which waited for: 11 -> 12; matrix products, arithmetic and copies ran while one was open for 1% -> 1% of each run, Pallas kernels for 44% -> 44%
where the time goes in v5:
time: 2770 us
  waiting for transfers between devices  1360 us (49%)
  Pallas kernels  1330 us (48%)
  starting transfers between devices  27.8 us (1%)
    ppermute x20, waiting for transfers between devices, hop(): return lax.ppermute(v, axes, pairs)  1360 us
    pallas_call x23, Pallas kernels, call(): pl.pallas_call(body, grid_spec=pltpu.PrefetchScalarGridSpec(num_scalar_pr...  1330 us
  transfers between devices with their start and end apart: 30, of which 12 were waited for; matrix products, arithmetic and copies ran while one was open for 1% of the time, Pallas kernels for 44%

profile of v5, /device:TPU:0, one launch (start us, length us, event | category | flops | bytes accessed | tf_op | source)
XLA Modules:
  0.0 2767.0 jit_solution(14278416758205939792)
XLA Ops:
  6.5 167.0 %collective-permute-done.14.refs_1_ = bf16[768,5120]{1,0:T(8,128)(2,1)} collective-permute-done((bf16[768,5120]{1,0:T(8,128)(2,1)}, bf16[768,5120]{1,0:T(8,128)(2,1)}, u32[]{:S(2)}, u32[]{:S(2)}) %collective-permute-start.14) | collective-permute-done | bytes 7864352 | tf_op jit(solution)/shard_map/ppermute | solution.py:417
  181.8 7.8 slice.24
  189.7 150.2 %collective-permute-done.3 = bf16[768,5120]{1,0:T(8,128)(2,1)} collective-permute-done((bf16[768,5120]{1,0:T(8,128)(2,1)}, bf16[768,5120]{1,0:T(8,128)(2,1)}, u32[]{:S(2)}, u32[]{:S(2)}) %collective-permute-start.3) | collective-permute-done | bytes 7864352 | tf_op jit(solution)/shard_map/ppermute | solution.py:417
  348.4 255.5 %collective-permute-done.17 = bf16[8,2560]{1,0:T(8,128)(2,1)S(1)} collective-permute-done((bf16[8,2560]{1,0:T(8,128)(2,1)S(1)}, bf16[8,2560]{1,0:T(8,128)(2,1)S(1)}, u32[]{:S(2)}, u32[]{:S(2)}) %collective-permute-start.17) | collective-permute-done | bytes 40992 | tf_op jit(solution)/shard_map/ppermute | solution.py:417
  618.1 53.1 %collective-permute-done.19 = bf16[456,5120]{1,0:T(8,128)(2,1)S(1)} collective-permute-done((bf16[456,5120]{1,0:T(8,128)(2,1)S(1)}, bf16[456,5120]{1,0:T(8,128)(2,1)S(1)}, u32[]{:S(2)}, u32[]{:S(2)}) %collective-permute-start.19) | collective-permute-done | bytes 4669472 | tf_op jit(solution)/shard_map/ppermute | solution.py:417
  671.2 11.1 broadcast_select_fusion
  688.1 66.9 %collective-permute-done.7.rest_1_ = bf16[1664,2560]{1,0:T(8,128)(2,1)} collective-permute-done((bf16[1664,2560]{1,0:T(8,128)(2,1)}, bf16[1664,2560]{1,0:T(8,128)(2,1)}, u32[]{:S(2)}, u32[]{:S(2)}) %collective-permute-start.7) | collective-permute-done | bytes 8519712 | tf_op jit(solution)/shard_map/ppermute | solution.py:417
  757.3 70.5 %shard_map.92 = (f32[768,3456]{1,0:T(8,128)}, f32[768,3456]{1,0:T(8,128)}, bf16[768,3456]{1,0:T(8,128)(2,1)}, bf16[3072,3456]{1,0:T(8,128)(2,1)}, bf16[3072,5120...) custom-call(s32[1]{0:T(128)} %bitcast.i_ref.refs_0_, bf16[768,5120]{1,0:T(8,128)(2,1)} %rest_4_.1, ...), custom_call_target="tpu_custom_call" | custom-call | flops 54358179840 | bytes 78643200 | tf_op jit(solution)/shard_map/pallas_call | solution.py:46
  827.8 69.0 %shard_map.94 = (f32[768,3456]{1,0:T(8,128)}, f32[768,3456]{1,0:T(8,128)}, bf16[768,3456]{1,0:T(8,128)(2,1)}, bf16[3072,3456]{1,0:T(8,128)(2,1)}, bf16[3072,5120]{1,0:T(8,128)(2,1)}) custom-call(s32[1]{0:T(128)} %bitcast.i_ref.refs_0_, bf16[768,5120]{1,0:T(8,128)(2,1)} %get-tuple-element.84.x_ref, ...), custom_call_target="tpu_custom_call", output_to_operand_aliasing={{3}: (4, {}), {4}: (5, {})} | custom-call | flops 54358179840 | bytes 131334144 | tf_op jit(solution)/shard_map/pallas_call | solution.py:46
  896.8 69.0 %shard_map.95 = (f32[768,3456]{1,0:T(8,128)}, f32[768,3456]{1,0:T(8,128)}, bf16[768,3456]{1,0:T(8,128)(2,1)}, bf16[3072,3456]{1,0:T(8,128)(2,1)}, bf16[3072,5120]{1,0:T(8,128)(2,1)}) custom-call(s32[1]{0:T(128)} %bitcast.i_ref.refs_0_, bf16[768,5120]{1,0:T(8,128)(2,1)} %get-tuple-element.83.x_ref, ...), custom_call_target="tpu_custom_call", output_to_operand_aliasing={{3}: (4, {}), {4}: (5, {})} | custom-call | flops 54358179840 | bytes 131334144 | tf_op jit(solution)/shard_map/pallas_call | solution.py:46
  965.8 44.3 %shard_map.93 = (bf16[3072,3456]{1,0:T(8,128)(2,1)}, bf16[3072,3456]{1,0:T(8,128)(2,1)}, bf16[3072,5120]{1,0:T(8,128)(2,1)}, bf16[3456,5120]{1,0:T(8,128)(2,1)}) custom-call(s32[1]{0:T(128)} %bitcast.i_ref.refs_0_, bf16[768,5120]{1,0:T(8,128)(2,1)} %rest_0_.1, bf16[3456,2560]{1,0:T(8,128)(2,1)} %w_ref.1, bf16[3456,2560]{1,0:T(8,128)(2,1)} %collective-permute-done.2.wo_ref, ...), custom_call_target="tpu_custom_call" | custom-call | flops 27179089920 | bytes 64487424 | tf_op jit(solution)/shard_map/pallas_call | solution.py:46
  1010.1 41.9 %shard_map.99 = (bf16[3072,3456]{1,0:T(8,128)(2,1)}, bf16[3072,3456]{1,0:T(8,128)(2,1)}, bf16[3072,5120]{1,0:T(8,128)(2,1)}) custom-call(s32[1]{0:T(128)} %bitcast.i_ref.refs_0_, bf16[768,5120]{1,0:T(8,128)(2,1)} %collective-permute-done.14.refs_1_, ...), custom_call_target="tpu_custom_call", output_to_operand_aliasing={{0}: (5, {}), {1}: (6, {}), {2}: (7, {})} | custom-call | flops 27179089920 | bytes 138412032 | tf_op jit(solution)/shard_map/pallas_call | solution.py:46
  1052.0 41.8 %shard_map.100 = (bf16[3072,3456]{1,0:T(8,128)(2,1)}, bf16[3072,3456]{1,0:T(8,128)(2,1)}, bf16[3072,5120]{1,0:T(8,128)(2,1)}) custom-call(s32[1]{0:T(128)} %bitcast.i_ref.refs_0_, bf16[768,5120]{1,0:T(8,128)(2,1)} %collective-permute-done.13.refs_1_, ...), custom_call_target="tpu_custom_call", output_to_operand_aliasing={{0}: (5, {}), {1}: (6, {}), {2}: (7, {})} | custom-call | flops 27179089920 | bytes 138412032 | tf_op jit(solution)/shard_map/pallas_call | solution.py:46
  1093.8 70.6 %shard_map.102.refs_9_ = f32[768,5120]{1,0:T(8,128)} custom-call(s32[1]{0:T(128)} %bitcast.i_ref.refs_0_, bf16[3072,3456]{1,0:T(8,128)(2,1)} %get-tuple-element.69.da_ref.refs_5_, bf16[3072,3456]{1,0:T(8,128)(2,1)} %get-tuple-element.70.db_ref.refs_6_, bf16[5120,3456]{1,0:T(8,128)(2,1)} %get-tuple-element.48.wg_ref, bf16[5120,3456]{1,0:T(8,128)(2,1)} %get-tuple-element.49.wu_ref), custom_call_target="tpu_custom_call" | custom-call | flops 54358179840 | bytes 113246208 | tf_op jit(solution)/shard_map/pallas_call | solution.py:46
  1164.3 72.8 %shard_map.101.u_ref.refs_8_ = f32[768,5120]{1,0:T(8,128)} custom-call(s32[1]{0:T(128)} %bitcast.i_ref.refs_0_, bf16[3072,3456]{1,0:T(8,128)(2,1)} %get-tuple-element.69.da_ref.refs_5_, bf16[3072,3456]{1,0:T(8,128)(2,1)} %get-tuple-element.70.db_ref.refs_6_, bf16[5120,3456]{1,0:T(8,128)(2,1)} %get-tuple-element.48.wg_ref, ...), custom_call_target="tpu_custom_call" | custom-call | flops 54358179840 | bytes 121110528 | tf_op jit(solution)/shard_map/pallas_call | solution.py:46
  1237.1 69.0 %shard_map.96 = (f32[768,3456]{1,0:T(8,128)}, f32[768,3456]{1,0:T(8,128)}, bf16[768,3456]{1,0:T(8,128)(2,1)}, bf16[3072,3456]{1,0:T(8,128)(2,1)}, bf16[3072,5120]{1,0:T(8,128)(2,1)}) custom-call(s32[1]{0:T(128)} %bitcast.i_ref.refs_0_, bf16[768,5120]{1,0:T(8,128)(2,1)} %collective-permute-done.10.x_ref, ...), custom_call_target="tpu_custom_call", output_to_operand_aliasing={{3}: (4, {}), {4}: (5, {})} | custom-call | flops 54358179840 | bytes 131334144 | tf_op jit(solution)/shard_map/pallas_call | solution.py:46
  1306.1 41.9 %shard_map.104 = (bf16[3072,3456]{1,0:T(8,128)(2,1)}, bf16[3072,3456]{1,0:T(8,128)(2,1)}, bf16[3072,5120]{1,0:T(8,128)(2,1)}) custom-call(s32[1]{0:T(128)} %bitcast.i_ref.refs_0_, bf16[768,5120]{1,0:T(8,128)(2,1)} %pad_maximum_fusion.refs_1_, ...), custom_call_target="tpu_custom_call", output_to_operand_aliasing={{0}: (5, {}), {1}: (6, {}), {2}: (7, {})} | custom-call | flops 27179089920 | bytes 169869312 | tf_op jit(solution)/shard_map/pallas_call | solution.py:46
  1348.0 70.1 %shard_map.106 = f32[768,5120]{1,0:T(8,128)} custom-call(s32[1]{0:T(128)} %bitcast.i_ref.refs_0_, bf16[3072,3456]{1,0:T(8,128)(2,1)} %get-tuple-element.74.da_ref.d_ref, bf16[3072,3456]{1,0:T(8,128)(2,1)} %get-tuple-element.75.db_ref.d_ref, bf16[5120,3456]{1,0:T(8,128)(2,1)} %get-tuple-element.48.wg_ref, bf16[5120,3456]{1,0:T(8,128)(2,1)} %get-tuple-element.49.wu_ref), custom_call_target="tpu_custom_call" | custom-call | flops 54358179840 | bytes 113246208 | tf_op jit(solution)/shard_map/pallas_call | solution.py:46
  1421.6 338.5 %collective-permute-done.11.hr_ref = bf16[768,3456]{1,0:T(8,128)(2,1)} collective-permute-done((bf16[768,3456]{1,0:T(8,128)(2,1)}, bf16[768,3456]{1,0:T(8,128)(2,1)}, u32[]{:S(2)}, u32[]{:S(2)}) %collective-permute-start.11) | collective-permute-done | bytes 5308448 | tf_op jit(solution)/shard_map/ppermute | solution.py:417
  1760.2 71.4 %shard_map.97 = f32[768,5120]{1,0:T(8,128)} custom-call(s32[1]{0:T(128)} %bitcast.i_ref.refs_0_, bf16[768,3456]{1,0:T(8,128)(2,1)} %get-tuple-element.55.h_ref, bf16[3456,5120]{1,0:T(8,128)(2,1)} %get-tuple-element.47.w_ref.refs_2_, bf16[768,3456]{1,0:T(8,128)(2,1)} %collective-permute-done.11.hr_ref, bf16[1792,2560]{1,0:T(8,128)(2,1)} %collective-permute-done.6.rest_0_, ...), custom_call_target="tpu_custom_call" | custom-call | flops 54358179840 | bytes 81395712 | tf_op jit(solution)/shard_map/pallas_call | solution.py:46
  1834.6 70.2 %shard_map.105.u_ref = f32[768,5120]{1,0:T(8,128)} custom-call(s32[1]{0:T(128)} %bitcast.i_ref.refs_0_, bf16[3072,3456]{1,0:T(8,128)(2,1)} %get-tuple-element.74.da_ref.d_ref, bf16[3072,3456]{1,0:T(8,128)(2,1)} %get-tuple-element.75.db_ref.d_ref, bf16[5120,3456]{1,0:T(8,128)(2,1)} %get-tuple-element.48.wg_ref, bf16[5120,3456]{1,0:T(8,128)(2,1)} %get-tuple-element.49.wu_ref), custom_call_target="tpu_custom_call" | custom-call | flops 54358179840 | bytes 113246208 | tf_op jit(solution)/shard_map/pallas_call | solution.py:46
  1904.8 17.4 shard_map.107
  1922.2 124.0 %collective-permute-done.5.hr_ref = bf16[768,3456]{1,0:T(8,128)(2,1)} collective-permute-done((bf16[768,3456]{1,0:T(8,128)(2,1)}, bf16[768,3456]{1,0:T(8,128)(2,1)}, u32[]{:S(2)}, u32[]{:S(2)}) %collective-permute-start.5) | collective-permute-done | bytes 5308448 | tf_op jit(solution)/shard_map/ppermute | solution.py:417
  2048.2 113.5 %collective-permute-done.21.v_ref = f32[16,5120]{1,0:T(8,128)S(1)} collective-permute-done((f32[16,5120]{1,0:T(8,128)}, f32[16,5120]{1,0:T(8,128)S(1)}, u32[]{:S(2)}, u32[]{:S(2)}) %collective-permute-start.21) | collective-permute-done | bytes 327712 | tf_op jit(solution)/shard_map/ppermute | solution.py:417
  2162.0 10.5 collective-permute-done.22.v_ref
  2173.3 17.4 shard_map.103.u_ref
  2190.7 80.5 %collective-permute-done.24.v_ref = f32[432,5120]{1,0:T(8,128)} collective-permute-done((f32[432,5120]{1,0:T(8,128)}, f32[432,5120]{1,0:T(8,128)}, u32[]{:S(2)}, u32[]{:S(2)}) %collective-permute-start.24) | collective-permute-done | bytes 8847392 | tf_op jit(solution)/shard_map/ppermute | solution.py:417
  2271.2 72.3 %shard_map.98 = bf16[768,5120]{1,0:T(8,128)(2,1)} custom-call(s32[1]{0:T(128)} %bitcast.i_ref.refs_0_, bf16[768,3456]{1,0:T(8,128)(2,1)} %get-tuple-element.44.h_ref, bf16[3456,5120]{1,0:T(8,128)(2,1)} %get-tuple-element.47.w_ref.refs_2_, bf16[768,3456]{1,0:T(8,128)(2,1)} %collective-permute-done.5.hr_ref, ...), custom_call_target="tpu_custom_call" | custom-call | flops 54358179840 | bytes 104988672 | tf_op jit(solution)/shard_map/pallas_call | solution.py:46
  2343.5 10.6 shard_map.108.rest_0_
  2364.9 137.0 %shard_map.113 = f32[2560,3456]{1,0:T(8,128)} custom-call(s32[1]{0:T(128)} %bitcast.i_ref.refs_0_, bf16[3072,5120]{1,0:T(8,128)(2,1)} %get-tuple-element.80.x_ref, bf16[3072,5120]{1,0:T(8,128)(2,1)} %collective-permute-done.25.xo_ref, bf16[3072,3456]{1,0:T(8,128)(2,1)} %get-tuple-element.75.db_ref.d_ref, bf16[3072,3456]{1,0:T(8,128)(2,1)} %collective-permute-done.27.do_ref), custom_call_target="tpu_custom_call" | custom-call | flops 108716359680 | bytes 105381888 | tf_op jit(solution)/shard_map/pallas_call | solution.py:46
  2501.9 137.3 %shard_map.112 = f32[2560,3456]{1,0:T(8,128)} custom-call(s32[1]{0:T(128)} %bitcast.i_ref.refs_0_, bf16[3072,5120]{1,0:T(8,128)(2,1)} %get-tuple-element.80.x_ref, bf16[3072,5120]{1,0:T(8,128)(2,1)} %collective-permute-done.25.xo_ref, bf16[3072,3456]{1,0:T(8,128)(2,1)} %get-tuple-element.74.da_ref.d_ref, bf16[3072,3456]{1,0:T(8,128)(2,1)} %collective-permute-done.26.do_ref), custom_call_target="tpu_custom_call" | custom-call | flops 108716359680 | bytes 105381888 | tf_op jit(solution)/shard_map/pallas_call | solution.py:46
  2639.1 127.8 %shard_map.114 = f32[3456,2560]{1,0:T(8,128)} custom-call(s32[1]{0:T(128)} %bitcast.i_ref.refs_0_, bf16[3072,3456]{1,0:T(8,128)(2,1)} %get-tuple-element.81.h_ref, bf16[3072,3456]{1,0:T(8,128)(2,1)} %collective-permute-done.28.ho_ref, bf16[3072,5120]{1,0:T(8,128)(2,1)} %get-tuple-element.82.d_ref, bf16[3072,5120]{1,0:T(8,128)(2,1)} %collective-permute-done.29.do_ref), custom_call_target="tpu_custom_call" | custom-call | flops 108716359680 | bytes 105381888 | tf_op jit(solution)/shard_map/pallas_call | solution.py:46
  (64 shorter events, 65.5 us)
Async XLA Ops:
  0.6 172.9 %collective-permute-start.14 = (bf16[768,5120]{1,0:T(8,128)(2,1)}, bf16[768,5120]{1,0:T(8,128)(2,1)}, u32[]{:S(2)}, u32[]{:S(2)}) collective-permute-start(bf16[768,5120]{1,0:T(8,128)(2,1)} %rest_0_.1), channel_id=1, source_target_pairs={{0,2},{1,3},{2,0},{3,1},{4,6},{5,7},{6,4},{7,5}} | collective-permute-start | bytes 23592968 | tf_op jit(solution)/shard_map/ppermute | solution.py:417
  4.0 172.4 %collective-permute-start.13 = (bf16[768,5120]{1,0:T(8,128)(2,1)}, bf16[768,5120]{1,0:T(8,128)(2,1)}, u32[]{:S(2)}, u32[]{:S(2)}) collective-permute-start(bf16[768,5120]{1,0:T(8,128)(2,1)} %rest_0_.1), channel_id=1, source_target_pairs={{0,4},{1,5},{2,6},{3,7},{4,0},{5,1},{6,2},{7,3}} | collective-permute-start | bytes 23592968 | tf_op jit(solution)/shard_map/ppermute | solution.py:417
  5.5 751.3 %collective-permute-start = (bf16[2560,3456]{1,0:T(8,128)(2,1)}, bf16[2560,3456]{1,0:T(8,128)(2,1)}, u32[]{:S(2)}, u32[]{:S(2)}) collective-permute-start(bf16[2560,3456]{1,0:T(8,128)(2,1)} %wg_ref.1), channel_id=1, source_target_pairs={{0,1},{1,0},{2,3},{3,2},{4,5},{5,4},{6,7},{7,6}} | collective-permute-start | bytes 53084168 | tf_op jit(solution)/shard_map/ppermute | solution.py:420
  5.5 751.8 %collective-permute-start.1 = (bf16[2560,3456]{1,0:T(8,128)(2,1)}, bf16[2560,3456]{1,0:T(8,128)(2,1)}, u32[]{:S(2)}, u32[]{:S(2)}) collective-permute-start(bf16[2560,3456]{1,0:T(8,128)(2,1)} %wu_ref.1), channel_id=1, source_target_pairs={{0,1},{1,0},{2,3},{3,2},{4,5},{5,4},{6,7},{7,6}} | collective-permute-start | bytes 53084168 | tf_op jit(solution)/shard_map/ppermute | solution.py:420
  6.0 333.9 %collective-permute-start.3 = (bf16[768,5120]{1,0:T(8,128)(2,1)}, bf16[768,5120]{1,0:T(8,128)(2,1)}, u32[]{:S(2)}, u32[]{:S(2)}) collective-permute-start(bf16[768,5120]{1,0:T(8,128)(2,1)} %rest_4_.1), channel_id=1, source_target_pairs={{0,2},{1,5},{2,0},{3,7},{4,6},{5,1},{6,4},{7,3}} | collective-permute-start | bytes 23592968 | tf_op jit(solution)/shard_map/ppermute | solution.py:417
  173.5 172.4 %collective-permute-start.4 = (bf16[768,5120]{1,0:T(8,128)(2,1)}, bf16[768,5120]{1,0:T(8,128)(2,1)}, u32[]{:S(2)}, u32[]{:S(2)}) collective-permute-start(bf16[768,5120]{1,0:T(8,128)(2,1)} %rest_4_.1), channel_id=1, source_target_pairs={{0,4},{1,3},{2,6},{3,1},{4,0},{5,7},{6,2},{7,5}} | collective-permute-start | bytes 23592968 | tf_op jit(solution)/shard_map/ppermute | solution.py:417
  181.4 436.1 %collective-permute-start.16 = (bf16[304,5120]{1,0:T(8,128)(2,1)}, bf16[304,5120]{1,0:T(8,128)(2,1)}, u32[]{:S(2)}, u32[]{:S(2)}) collective-permute-start(bf16[304,5120]{1,0:T(8,128)(2,1)} %slice.34), channel_id=1, source_target_pairs={{0,2},{1,5},{2,0},{3,7},{4,6},{5,1},{6,4},{7,3}} | collective-permute-start | bytes 9338888 | tf_op jit(solution)/shard_map/ppermute | solution.py:417
  339.9 416.9 %collective-permute-start.6 = (bf16[1792,2560]{1,0:T(8,128)(2,1)}, bf16[1792,2560]{1,0:T(8,128)(2,1)}, u32[]{:S(2)}, u32[]{:S(2)}) collective-permute-start(bf16[1792,2560]{1,0:T(8,128)(2,1)} %slice.24), channel_id=1, source_target_pairs={{0,2},{1,3},{2,0},{3,1},{4,6},{5,7},{6,4},{7,5}} | collective-permute-start | bytes 27525128 | tf_op jit(solution)/shard_map/ppermute | solution.py:417
  345.9 258.1 %collective-permute-start.17 = (bf16[8,2560]{1,0:T(8,128)(2,1)S(1)}, bf16[8,2560]{1,0:T(8,128)(2,1)S(1)}, u32[]{:S(2)}, u32[]{:S(2)}) collective-permute-start(bf16[8,2560]{1,0:T(8,128)(2,1)S(1)} %slice.35), channel_id=1, source_target_pairs={{0,2},{1,5},{2,0},{3,7},{4,6},{5,1},{6,4},{7,3}} | collective-permute-start | bytes 122888 | tf_op jit(solution)/shard_map/ppermute | solution.py:417
  604.0 9.5 collective-permute-start.18
  613.4 141.6 %collective-permute-start.7 = (bf16[1664,2560]{1,0:T(8,128)(2,1)}, bf16[1664,2560]{1,0:T(8,128)(2,1)}, u32[]{:S(2)}, u32[]{:S(2)}) collective-permute-start(bf16[1664,2560]{1,0:T(8,128)(2,1)} %slice.25), channel_id=1, source_target_pairs={{0,2},{1,3},{2,0},{3,1},{4,6},{5,7},{6,4},{7,5}} | collective-permute-start | bytes 25559048 | tf_op jit(solution)/shard_map/ppermute | solution.py:417
  617.5 53.6 %collective-permute-start.19 = (bf16[456,5120]{1,0:T(8,128)(2,1)S(1)}, bf16[456,5120]{1,0:T(8,128)(2,1)S(1)}, u32[]{:S(2)}, u32[]{:S(2)}) collective-permute-start(bf16[456,5120]{1,0:T(8,128)(2,1)S(1)} %slice.37), channel_id=1, source_target_pairs={{0,4},{1,5},{2,6},{3,7},{4,0},{5,1},{6,2},{7,3}} | collective-permute-start | bytes 14008328 | tf_op jit(solution)/shard_map/ppermute | solution.py:417
  671.2 294.6 %collective-permute-start.2 = (bf16[3456,2560]{1,0:T(8,128)(2,1)}, bf16[3456,2560]{1,0:T(8,128)(2,1)}, u32[]{:S(2)}, u32[]{:S(2)}) collective-permute-start(bf16[3456,2560]{1,0:T(8,128)(2,1)} %w_ref.1), channel_id=1, source_target_pairs={{0,1},{1,0},{2,3},{3,2},{4,5},{5,4},{6,7},{7,6}} | collective-permute-start | bytes 53084168 | tf_op jit(solution)/shard_map/ppermute | solution.py:420
  755.0 482.1 %collective-permute-start.10 = (bf16[768,5120]{1,0:T(8,128)(2,1)}, bf16[768,5120]{1,0:T(8,128)(2,1)}, u32[]{:S(2)}, u32[]{:S(2)}) collective-permute-start(bf16[768,5120]{1,0:T(8,128)(2,1)} %get-tuple-element.84.x_ref), channel_id=1, source_target_pairs={{0,4},{1,5},{2,6},{3,7},{4,0},{5,1},{6,2},{7,3}} | collective-permute-start | bytes 23592968 | tf_op jit(solution)/shard_map/ppermute | solution.py:417
  756.8 664.8 %collective-permute-start.9 = (bf16[1664,2560]{1,0:T(8,128)(2,1)}, bf16[1664,2560]{1,0:T(8,128)(2,1)}, u32[]{:S(2)}, u32[]{:S(2)}) collective-permute-start(bf16[1664,2560]{1,0:T(8,128)(2,1)} %collective-permute-done.7.rest_1_), channel_id=1, source_target_pairs={{0,1},{1,0},{2,3},{3,2},{4,5},{5,4},{6,7},{7,6}} | collective-permute-start | bytes 25559048 | tf_op jit(solution)/shard_map/ppermute | solution.py:420
  756.8 664.8 %collective-permute-start.8 = (bf16[1792,2560]{1,0:T(8,128)(2,1)}, bf16[1792,2560]{1,0:T(8,128)(2,1)}, u32[]{:S(2)}, u32[]{:S(2)}) collective-permute-start(bf16[1792,2560]{1,0:T(8,128)(2,1)} %collective-permute-done.6.rest_0_), channel_id=1, source_target_pairs={{0,1},{1,0},{2,3},{3,2},{4,5},{5,4},{6,7},{7,6}} | collective-permute-start | bytes 27525128 | tf_op jit(solution)/shard_map/ppermute | solution.py:420
  1418.1 416.5 %collective-permute-start.20 = (f32[768,5120]{1,0:T(8,128)}, f32[768,5120]{1,0:T(8,128)}, u32[]{:S(2)}, u32[]{:S(2)}) collective-permute-start(f32[768,5120]{1,0:T(8,128)} %shard_map.106), channel_id=1, source_target_pairs={{0,2},{1,5},{2,0},{3,7},{4,6},{5,1},{6,4},{7,3}} | collective-permute-start | bytes 47185928 | tf_op jit(solution)/shard_map/ppermute | solution.py:417
  1419.6 340.6 %collective-permute-start.11 = (bf16[768,3456]{1,0:T(8,128)(2,1)}, bf16[768,3456]{1,0:T(8,128)(2,1)}, u32[]{:S(2)}, u32[]{:S(2)}) collective-permute-start(bf16[768,3456]{1,0:T(8,128)(2,1)} %get-tuple-element.58), channel_id=1, source_target_pairs={{0,2},{1,3},{2,0},{3,1},{4,6},{5,7},{6,4},{7,5}} | collective-permute-start | bytes 15925256 | tf_op jit(solution)/shard_map/ppermute | solution.py:417
  1420.1 627.8 %collective-permute-start.15 = (f32[768,5120]{1,0:T(8,128)}, f32[768,5120]{1,0:T(8,128)}, u32[]{:S(2)}, u32[]{:S(2)}) collective-permute-start(f32[768,5120]{1,0:T(8,128)} %shard_map.102.refs_9_), channel_id=1, source_target_pairs={{0,2},{1,5},{2,0},{3,7},{4,6},{5,1},{6,4},{7,3}} | collective-permute-start | bytes 47185928 | tf_op jit(solution)/shard_map/ppermute | solution.py:417
  1421.6 943.3 %collective-permute-start.25 = (bf16[3072,5120]{1,0:T(8,128)(2,1)}, bf16[3072,5120]{1,0:T(8,128)(2,1)}, u32[]{:S(2)}, u32[]{:S(2)}) collective-permute-start(bf16[3072,5120]{1,0:T(8,128)(2,1)} %get-tuple-element.80.x_ref), channel_id=1, source_target_pairs={{0,1},{1,0},{2,3},{3,2},{4,5},{5,4},{6,7},{7,6}} | collective-permute-start | bytes 94371848 | tf_op jit(solution)/shard_map/ppermute | solution.py:420
  1831.6 341.2 %collective-permute-start.12 = (f32[768,5120]{1,0:T(8,128)}, f32[768,5120]{1,0:T(8,128)}, u32[]{:S(2)}, u32[]{:S(2)}) collective-permute-start(f32[768,5120]{1,0:T(8,128)} %shard_map.97), channel_id=1, source_target_pairs={{0,4},{1,5},{2,6},{3,7},{4,0},{5,1},{6,2},{7,3}} | collective-permute-start | bytes 47185928 | tf_op jit(solution)/shard_map/ppermute | solution.py:417
  1832.8 213.3 %collective-permute-start.5 = (bf16[768,3456]{1,0:T(8,128)(2,1)}, bf16[768,3456]{1,0:T(8,128)(2,1)}, u32[]{:S(2)}, u32[]{:S(2)}) collective-permute-start(bf16[768,3456]{1,0:T(8,128)(2,1)} %get-tuple-element.52), channel_id=1, source_target_pairs={{0,2},{1,3},{2,0},{3,1},{4,6},{5,7},{6,4},{7,5}} | collective-permute-start | bytes 15925256 | tf_op jit(solution)/shard_map/ppermute | solution.py:417
  1834.6 530.3 %collective-permute-start.27 = (bf16[3072,3456]{1,0:T(8,128)(2,1)}, bf16[3072,3456]{1,0:T(8,128)(2,1)}, u32[]{:S(2)}, u32[]{:S(2)}) collective-permute-start(bf16[3072,3456]{1,0:T(8,128)(2,1)} %get-tuple-element.75.db_ref.d_ref), channel_id=1, source_target_pairs={{0,1},{1,0},{2,3},{3,2},{4,5},{5,4},{6,7},{7,6}} | collective-permute-start | bytes 63701000 | tf_op jit(solution)/shard_map/ppermute | solution.py:420
  2046.1 126.7 %collective-permute-start.23 = (f32[288,5120]{1,0:T(8,128)}, f32[288,5120]{1,0:T(8,128)}, u32[]{:S(2)}, u32[]{:S(2)}) collective-permute-start(f32[288,5120]{1,0:T(8,128)} %get-tuple-element.78), channel_id=1, source_target_pairs={{0,4},{1,3},{2,6},{3,1},{4,0},{5,7},{6,2},{7,5}} | collective-permute-start | bytes 17694728 | tf_op jit(solution)/shard_map/ppermute | solution.py:417
  2047.9 113.8 %collective-permute-start.21 = (f32[16,5120]{1,0:T(8,128)}, f32[16,5120]{1,0:T(8,128)S(1)}, u32[]{:S(2)}, u32[]{:S(2)}) collective-permute-start(f32[16,5120]{1,0:T(8,128)} %get-tuple-element.76), channel_id=1, source_target_pairs={{0,4},{1,3},{2,6},{3,1},{4,0},{5,7},{6,2},{7,5}} | collective-permute-start | bytes 983048 | tf_op jit(solution)/shard_map/ppermute | solution.py:417
  2161.7 29.0 %copy-start.1 = (f32[16,5120]{1,0:T(8,128)}, f32[16,5120]{1,0:T(8,128)S(1)}, u32[]{:S(2)}) copy-start(f32[16,5120]{1,0:T(8,128)S(1)} %collective-permute-done.21.v_ref) | copy-start | bytes 983044
  2161.7 10.8 collective-permute-start.22
  2172.5 18.2 copy-start
  2172.5 98.7 %collective-permute-start.24 = (f32[432,5120]{1,0:T(8,128)}, f32[432,5120]{1,0:T(8,128)}, u32[]{:S(2)}, u32[]{:S(2)}) collective-permute-start(f32[432,5120]{1,0:T(8,128)} %get-tuple-element.79), channel_id=1, source_target_pairs={{0,4},{1,3},{2,6},{3,1},{4,0},{5,7},{6,2},{7,5}} | collective-permute-start | bytes 26542088 | tf_op jit(solution)/shard_map/ppermute | solution.py:417
  2172.8 466.3 %collective-permute-start.29 = (bf16[3072,5120]{1,0:T(8,128)(2,1)}, bf16[3072,5120]{1,0:T(8,128)(2,1)}, u32[]{:S(2)}, u32[]{:S(2)}) collective-permute-start(bf16[3072,5120]{1,0:T(8,128)(2,1)} %get-tuple-element.82.d_ref), channel_id=1, source_target_pairs={{0,1},{1,0},{2,3},{3,2},{4,5},{5,4},{6,7},{7,6}} | collective-permute-start | bytes 94371848 | tf_op jit(solution)/shard_map/ppermute | solution.py:420
  2172.8 329.1 %collective-permute-start.26 = (bf16[3072,3456]{1,0:T(8,128)(2,1)}, bf16[3072,3456]{1,0:T(8,128)(2,1)}, u32[]{:S(2)}, u32[]{:S(2)}) collective-permute-start(bf16[3072,3456]{1,0:T(8,128)(2,1)} %get-tuple-element.74.da_ref.d_ref), channel_id=1, source_target_pairs={{0,1},{1,0},{2,3},{3,2},{4,5},{5,4},{6,7},{7,6}} | collective-permute-start | bytes 63701000 | tf_op jit(solution)/shard_map/ppermute | solution.py:420
  2271.2 367.9 %collective-permute-start.28 = (bf16[3072,3456]{1,0:T(8,128)(2,1)}, bf16[3072,3456]{1,0:T(8,128)(2,1)}, u32[]{:S(2)}, u32[]{:S(2)}) collective-permute-start(bf16[3072,3456]{1,0:T(8,128)(2,1)} %get-tuple-element.81.h_ref), channel_id=1, source_target_pairs={{0,1},{1,0},{2,3},{3,2},{4,5},{5,4},{6,7},{7,6}} | collective-permute-start | bytes 63701000 | tf_op jit(solution)/shard_map/ppermute | solution.py:420

commit v6 on v5

--- a/solution.py
+++ b/solution.py
@@ -423,7 +423,7 @@
         i = lax.axis_index("dp").astype(jnp.int32).reshape(1)
         ka = 1792
         qa = 304
-        sizes = (432, 288, 32, 16)
+        sizes = (448, 256, 48, 16)
         x1, x2 = hop(x, 1, 2), hop(x, 2, 1)
         xX, xY = jnp.where(i[0] == 0, x1, x2), jnp.where(i[0] == 0, x2, x1)
         dyX, dyY = hop(dy, 1, 1), hop(dy, 2, 2)
@@ -470,8 +470,9 @@
 
         pre = k_add(i, z0, s1)[0]
         dx = ()
-        for p, v in enumerate(s2):
-            dx = (k_fin(i, sum(sizes[:p]), pre, v, dx, 48 if p < 2 else 16),)
-        return y, dx[0], dwg, dwu, dwd
+        for p, v in enumerate(s2[:3]):
+            dx = (k_fin(i, sum(sizes[:p]), pre, v, dx, 64 if p < 2 else 16),)
+        dx = lax.dynamic_update_slice(dx[0], (pre[752:] + s2[3]).astype(bf), (752, 0))
+        return y, dx, dwg, dwu, dwd
 
     return jax.shard_map(layer, mesh=mesh, in_specs=(rows, wsp, wsp, dsp, rows), out_specs=(rows, rows, wsp, wsp, dsp), check_vma=False)

time: 2770 us -> 2760 us (level)
    pallas_call x23 -> x22, Pallas kernels: 1330 us -> 1330 us  [call(): pl.pallas_call(body, grid_spec=pltpu.PrefetchScalarGridSpec(num_scalar_pr...]
  transfers between devices with their start and end apart: 30 -> 30, of which waited for: 12 -> 12; matrix products, arithmetic and copies ran while one was open for 1% -> 2% of each run, Pallas kernels for 44% -> 44%
where the time goes in v6:
time: 2760 us
  waiting for transfers between devices  1350 us (49%)
  Pallas kernels  1330 us (48%)
    ppermute x20, waiting for transfers between devices, hop(): return lax.ppermute(v, axes, pairs)  1350 us
    pallas_call x22, Pallas kernels, call(): pl.pallas_call(body, grid_spec=pltpu.PrefetchScalarGridSpec(num_scalar_pr...  1330 us
  transfers between devices with their start and end apart: 30, of which 12 were waited for; matrix products, arithmetic and copies ran while one was open for 2% of the time, Pallas kernels for 44%

profile of v6, /device:TPU:0, one launch (start us, length us, event | category | flops | bytes accessed | tf_op | source)
XLA Modules:
  0.0 2755.5 jit_solution(8895932135625023909)
XLA Ops:
  6.5 167.0 %collective-permute-done.14.refs_1_ = bf16[768,5120]{1,0:T(8,128)(2,1)} collective-permute-done((bf16[768,5120]{1,0:T(8,128)(2,1)}, bf16[768,5120]{1,0:T(8,128)(2,1)}, u32[]{:S(2)}, u32[]{:S(2)}) %collective-permute-start.14) | collective-permute-done | bytes 7864352 | tf_op jit(solution)/shard_map/ppermute | solution.py:417
  181.8 7.8 slice.27
  189.7 150.2 %collective-permute-done.3 = bf16[768,5120]{1,0:T(8,128)(2,1)} collective-permute-done((bf16[768,5120]{1,0:T(8,128)(2,1)}, bf16[768,5120]{1,0:T(8,128)(2,1)}, u32[]{:S(2)}, u32[]{:S(2)}) %collective-permute-start.3) | collective-permute-done | bytes 7864352 | tf_op jit(solution)/shard_map/ppermute | solution.py:417
  348.4 255.5 %collective-permute-done.17 = bf16[8,2560]{1,0:T(8,128)(2,1)S(1)} collective-permute-done((bf16[8,2560]{1,0:T(8,128)(2,1)S(1)}, bf16[8,2560]{1,0:T(8,128)(2,1)S(1)}, u32[]{:S(2)}, u32[]{:S(2)}) %collective-permute-start.17) | collective-permute-done | bytes 40992 | tf_op jit(solution)/shard_map/ppermute | solution.py:417
  618.1 53.1 %collective-permute-done.19 = bf16[456,5120]{1,0:T(8,128)(2,1)S(1)} collective-permute-done((bf16[456,5120]{1,0:T(8,128)(2,1)S(1)}, bf16[456,5120]{1,0:T(8,128)(2,1)S(1)}, u32[]{:S(2)}, u32[]{:S(2)}) %collective-permute-start.19) | collective-permute-done | bytes 4669472 | tf_op jit(solution)/shard_map/ppermute | solution.py:417
  671.2 11.1 broadcast_select_fusion
  688.1 67.0 %collective-permute-done.7.rest_1_ = bf16[1664,2560]{1,0:T(8,128)(2,1)} collective-permute-done((bf16[1664,2560]{1,0:T(8,128)(2,1)}, bf16[1664,2560]{1,0:T(8,128)(2,1)}, u32[]{:S(2)}, u32[]{:S(2)}) %collective-permute-start.7) | collective-permute-done | bytes 8519712 | tf_op jit(solution)/shard_map/ppermute | solution.py:417
  757.3 70.5 %shard_map.92 = (f32[768,3456]{1,0:T(8,128)}, f32[768,3456]{1,0:T(8,128)}, bf16[768,3456]{1,0:T(8,128)(2,1)}, bf16[3072,3456]{1,0:T(8,128)(2,1)}, bf16[3072,5120...) custom-call(s32[1]{0:T(128)} %bitcast.i_ref.refs_0_, bf16[768,5120]{1,0:T(8,128)(2,1)} %rest_4_.1, ...), custom_call_target="tpu_custom_call" | custom-call | flops 54358179840 | bytes 78643200 | tf_op jit(solution)/shard_map/pallas_call | solution.py:46
  827.8 69.0 %shard_map.94 = (f32[768,3456]{1,0:T(8,128)}, f32[768,3456]{1,0:T(8,128)}, bf16[768,3456]{1,0:T(8,128)(2,1)}, bf16[3072,3456]{1,0:T(8,128)(2,1)}, bf16[3072,5120]{1,0:T(8,128)(2,1)}) custom-call(s32[1]{0:T(128)} %bitcast.i_ref.refs_0_, bf16[768,5120]{1,0:T(8,128)(2,1)} %get-tuple-element.84.x_ref, ...), custom_call_target="tpu_custom_call", output_to_operand_aliasing={{3}: (4, {}), {4}: (5, {})} | custom-call | flops 54358179840 | bytes 131334144 | tf_op jit(solution)/shard_map/pallas_call | solution.py:46
  896.8 69.0 %shard_map.95 = (f32[768,3456]{1,0:T(8,128)}, f32[768,3456]{1,0:T(8,128)}, bf16[768,3456]{1,0:T(8,128)(2,1)}, bf16[3072,3456]{1,0:T(8,128)(2,1)}, bf16[3072,5120]{1,0:T(8,128)(2,1)}) custom-call(s32[1]{0:T(128)} %bitcast.i_ref.refs_0_, bf16[768,5120]{1,0:T(8,128)(2,1)} %get-tuple-element.83.x_ref, ...), custom_call_target="tpu_custom_call", output_to_operand_aliasing={{3}: (4, {}), {4}: (5, {})} | custom-call | flops 54358179840 | bytes 131334144 | tf_op jit(solution)/shard_map/pallas_call | solution.py:46
  965.8 44.3 %shard_map.93 = (bf16[3072,3456]{1,0:T(8,128)(2,1)}, bf16[3072,3456]{1,0:T(8,128)(2,1)}, bf16[3072,5120]{1,0:T(8,128)(2,1)}, bf16[3456,5120]{1,0:T(8,128)(2,1)}) custom-call(s32[1]{0:T(128)} %bitcast.i_ref.refs_0_, bf16[768,5120]{1,0:T(8,128)(2,1)} %rest_0_.1, bf16[3456,2560]{1,0:T(8,128)(2,1)} %w_ref.1, bf16[3456,2560]{1,0:T(8,128)(2,1)} %collective-permute-done.2.wo_ref, ...), custom_call_target="tpu_custom_call" | custom-call | flops 27179089920 | bytes 64487424 | tf_op jit(solution)/shard_map/pallas_call | solution.py:46
  1010.2 41.8 %shard_map.99 = (bf16[3072,3456]{1,0:T(8,128)(2,1)}, bf16[3072,3456]{1,0:T(8,128)(2,1)}, bf16[3072,5120]{1,0:T(8,128)(2,1)}) custom-call(s32[1]{0:T(128)} %bitcast.i_ref.refs_0_, bf16[768,5120]{1,0:T(8,128)(2,1)} %collective-permute-done.14.refs_1_, ...), custom_call_target="tpu_custom_call", output_to_operand_aliasing={{0}: (5, {}), {1}: (6, {}), {2}: (7, {})} | custom-call | flops 27179089920 | bytes 138412032 | tf_op jit(solution)/shard_map/pallas_call | solution.py:46
  1052.0 41.8 %shard_map.100 = (bf16[3072,3456]{1,0:T(8,128)(2,1)}, bf16[3072,3456]{1,0:T(8,128)(2,1)}, bf16[3072,5120]{1,0:T(8,128)(2,1)}) custom-call(s32[1]{0:T(128)} %bitcast.i_ref.refs_0_, bf16[768,5120]{1,0:T(8,128)(2,1)} %collective-permute-done.13.refs_1_, ...), custom_call_target="tpu_custom_call", output_to_operand_aliasing={{0}: (5, {}), {1}: (6, {}), {2}: (7, {})} | custom-call | flops 27179089920 | bytes 138412032 | tf_op jit(solution)/shard_map/pallas_call | solution.py:46
  1093.9 70.5 %shard_map.102.refs_9_ = f32[768,5120]{1,0:T(8,128)} custom-call(s32[1]{0:T(128)} %bitcast.i_ref.refs_0_, bf16[3072,3456]{1,0:T(8,128)(2,1)} %get-tuple-element.69.da_ref.refs_5_, bf16[3072,3456]{1,0:T(8,128)(2,1)} %get-tuple-element.70.db_ref.refs_6_, bf16[5120,3456]{1,0:T(8,128)(2,1)} %get-tuple-element.48.wg_ref, bf16[5120,3456]{1,0:T(8,128)(2,1)} %get-tuple-element.49.wu_ref), custom_call_target="tpu_custom_call" | custom-call | flops 54358179840 | bytes 113246208 | tf_op jit(solution)/shard_map/pallas_call | solution.py:46
  1164.4 72.8 %shard_map.101.u_ref.refs_8_ = f32[768,5120]{1,0:T(8,128)} custom-call(s32[1]{0:T(128)} %bitcast.i_ref.refs_0_, bf16[3072,3456]{1,0:T(8,128)(2,1)} %get-tuple-element.69.da_ref.refs_5_, bf16[3072,3456]{1,0:T(8,128)(2,1)} %get-tuple-element.70.db_ref.refs_6_, bf16[5120,3456]{1,0:T(8,128)(2,1)} %get-tuple-element.48.wg_ref, ...), custom_call_target="tpu_custom_call" | custom-call | flops 54358179840 | bytes 121110528 | tf_op jit(solution)/shard_map/pallas_call | solution.py:46
  1237.2 69.1 %shard_map.96 = (f32[768,3456]{1,0:T(8,128)}, f32[768,3456]{1,0:T(8,128)}, bf16[768,3456]{1,0:T(8,128)(2,1)}, bf16[3072,3456]{1,0:T(8,128)(2,1)}, bf16[3072,5120]{1,0:T(8,128)(2,1)}) custom-call(s32[1]{0:T(128)} %bitcast.i_ref.refs_0_, bf16[768,5120]{1,0:T(8,128)(2,1)} %collective-permute-done.10.x_ref, ...), custom_call_target="tpu_custom_call", output_to_operand_aliasing={{3}: (4, {}), {4}: (5, {})} | custom-call | flops 54358179840 | bytes 131334144 | tf_op jit(solution)/shard_map/pallas_call | solution.py:46
  1306.3 41.9 %shard_map.104 = (bf16[3072,3456]{1,0:T(8,128)(2,1)}, bf16[3072,3456]{1,0:T(8,128)(2,1)}, bf16[3072,5120]{1,0:T(8,128)(2,1)}) custom-call(s32[1]{0:T(128)} %bitcast.i_ref.refs_0_, bf16[768,5120]{1,0:T(8,128)(2,1)} %pad_maximum_fusion.refs_1_, ...), custom_call_target="tpu_custom_call", output_to_operand_aliasing={{0}: (5, {}), {1}: (6, {}), {2}: (7, {})} | custom-call | flops 27179089920 | bytes 169869312 | tf_op jit(solution)/shard_map/pallas_call | solution.py:46
  1348.1 70.1 %shard_map.106 = f32[768,5120]{1,0:T(8,128)} custom-call(s32[1]{0:T(128)} %bitcast.i_ref.refs_0_, bf16[3072,3456]{1,0:T(8,128)(2,1)} %get-tuple-element.74.da_ref.d_ref, bf16[3072,3456]{1,0:T(8,128)(2,1)} %get-tuple-element.75.db_ref.d_ref, bf16[5120,3456]{1,0:T(8,128)(2,1)} %get-tuple-element.48.wg_ref, bf16[5120,3456]{1,0:T(8,128)(2,1)} %get-tuple-element.49.wu_ref), custom_call_target="tpu_custom_call" | custom-call | flops 54358179840 | bytes 113246208 | tf_op jit(solution)/shard_map/pallas_call | solution.py:46
  1421.8 338.8 %collective-permute-done.11.hr_ref = bf16[768,3456]{1,0:T(8,128)(2,1)} collective-permute-done((bf16[768,3456]{1,0:T(8,128)(2,1)}, bf16[768,3456]{1,0:T(8,128)(2,1)}, u32[]{:S(2)}, u32[]{:S(2)}) %collective-permute-start.11) | collective-permute-done | bytes 5308448 | tf_op jit(solution)/shard_map/ppermute | solution.py:417
  1760.6 71.6 %shard_map.97 = f32[768,5120]{1,0:T(8,128)} custom-call(s32[1]{0:T(128)} %bitcast.i_ref.refs_0_, bf16[768,3456]{1,0:T(8,128)(2,1)} %get-tuple-element.55.h_ref, bf16[3456,5120]{1,0:T(8,128)(2,1)} %get-tuple-element.47.w_ref.refs_2_, bf16[768,3456]{1,0:T(8,128)(2,1)} %collective-permute-done.11.hr_ref, bf16[1792,2560]{1,0:T(8,128)(2,1)} %collective-permute-done.6.rest_0_, ...), custom_call_target="tpu_custom_call" | custom-call | flops 54358179840 | bytes 81395712 | tf_op jit(solution)/shard_map/pallas_call | solution.py:46
  1834.9 70.4 %shard_map.105.u_ref = f32[768,5120]{1,0:T(8,128)} custom-call(s32[1]{0:T(128)} %bitcast.i_ref.refs_0_, bf16[3072,3456]{1,0:T(8,128)(2,1)} %get-tuple-element.74.da_ref.d_ref, bf16[3072,3456]{1,0:T(8,128)(2,1)} %get-tuple-element.75.db_ref.d_ref, bf16[5120,3456]{1,0:T(8,128)(2,1)} %get-tuple-element.48.wg_ref, bf16[5120,3456]{1,0:T(8,128)(2,1)} %get-tuple-element.49.wu_ref), custom_call_target="tpu_custom_call" | custom-call | flops 54358179840 | bytes 113246208 | tf_op jit(solution)/shard_map/pallas_call | solution.py:46
  1905.3 17.4 shard_map.107
  1922.7 124.1 %collective-permute-done.5.hr_ref = bf16[768,3456]{1,0:T(8,128)(2,1)} collective-permute-done((bf16[768,3456]{1,0:T(8,128)(2,1)}, bf16[768,3456]{1,0:T(8,128)(2,1)}, u32[]{:S(2)}, u32[]{:S(2)}) %collective-permute-start.5) | collective-permute-done | bytes 5308448 | tf_op jit(solution)/shard_map/ppermute | solution.py:417
  2048.8 57.2 %collective-permute-done.21.v_ref = f32[48,5120]{1,0:T(8,128)S(1)} collective-permute-done((f32[48,5120]{1,0:T(8,128)}, f32[48,5120]{1,0:T(8,128)S(1)}, u32[]{:S(2)}, u32[]{:S(2)}) %collective-permute-start.21) | collective-permute-done | bytes 983072 | tf_op jit(solution)/shard_map/ppermute | solution.py:417
  2106.2 56.0 %collective-permute-done.22.v_ref = f32[256,5120]{1,0:T(8,128)} collective-permute-done((f32[256,5120]{1,0:T(8,128)}, f32[256,5120]{1,0:T(8,128)}, u32[]{:S(2)}, u32[]{:S(2)}) %collective-permute-start.22) | collective-permute-done | bytes 5242912 | tf_op jit(solution)/shard_map/ppermute | solution.py:417
  2162.8 17.4 shard_map.103.u_ref
  2180.2 80.4 %collective-permute-done.23.v_ref = f32[448,5120]{1,0:T(8,128)} collective-permute-done((f32[448,5120]{1,0:T(8,128)}, f32[448,5120]{1,0:T(8,128)}, u32[]{:S(2)}, u32[]{:S(2)}) %collective-permute-start.23) | collective-permute-done | bytes 9175072 | tf_op jit(solution)/shard_map/ppermute | solution.py:417
  2260.8 72.4 %shard_map.98 = bf16[768,5120]{1,0:T(8,128)(2,1)} custom-call(s32[1]{0:T(128)} %bitcast.i_ref.refs_0_, bf16[768,3456]{1,0:T(8,128)(2,1)} %get-tuple-element.44.h_ref, bf16[3456,5120]{1,0:T(8,128)(2,1)} %get-tuple-element.47.w_ref.refs_2_, bf16[768,3456]{1,0:T(8,128)(2,1)} %collective-permute-done.5.hr_ref, ...), custom_call_target="tpu_custom_call" | custom-call | flops 54358179840 | bytes 104988672 | tf_op jit(solution)/shard_map/pallas_call | solution.py:46
  2333.2 10.0 shard_map.108.rest_0_
  2353.9 136.9 %shard_map.112 = f32[2560,3456]{1,0:T(8,128)} custom-call(s32[1]{0:T(128)} %bitcast.i_ref.refs_0_, bf16[3072,5120]{1,0:T(8,128)(2,1)} %get-tuple-element.80.x_ref, bf16[3072,5120]{1,0:T(8,128)(2,1)} %collective-permute-done.25.xo_ref, bf16[3072,3456]{1,0:T(8,128)(2,1)} %get-tuple-element.75.db_ref.d_ref, bf16[3072,3456]{1,0:T(8,128)(2,1)} %collective-permute-done.27.do_ref), custom_call_target="tpu_custom_call" | custom-call | flops 108716359680 | bytes 105381888 | tf_op jit(solution)/shard_map/pallas_call | solution.py:46
  2490.8 136.9 %shard_map.111 = f32[2560,3456]{1,0:T(8,128)} custom-call(s32[1]{0:T(128)} %bitcast.i_ref.refs_0_, bf16[3072,5120]{1,0:T(8,128)(2,1)} %get-tuple-element.80.x_ref, bf16[3072,5120]{1,0:T(8,128)(2,1)} %collective-permute-done.25.xo_ref, bf16[3072,3456]{1,0:T(8,128)(2,1)} %get-tuple-element.74.da_ref.d_ref, bf16[3072,3456]{1,0:T(8,128)(2,1)} %collective-permute-done.26.do_ref), custom_call_target="tpu_custom_call" | custom-call | flops 108716359680 | bytes 105381888 | tf_op jit(solution)/shard_map/pallas_call | solution.py:46
  2627.7 127.9 %shard_map.113 = f32[3456,2560]{1,0:T(8,128)} custom-call(s32[1]{0:T(128)} %bitcast.i_ref.refs_0_, bf16[3072,3456]{1,0:T(8,128)(2,1)} %get-tuple-element.81.h_ref, bf16[3072,3456]{1,0:T(8,128)(2,1)} %collective-permute-done.28.ho_ref, bf16[3072,5120]{1,0:T(8,128)(2,1)} %get-tuple-element.82.d_ref, bf16[3072,5120]{1,0:T(8,128)(2,1)} %collective-permute-done.29.do_ref), custom_call_target="tpu_custom_call" | custom-call | flops 108716359680 | bytes 105381888 | tf_op jit(solution)/shard_map/pallas_call | solution.py:46
  (64 shorter events, 64.9 us)
Async XLA Ops:
  0.6 172.9 %collective-permute-start.14 = (bf16[768,5120]{1,0:T(8,128)(2,1)}, bf16[768,5120]{1,0:T(8,128)(2,1)}, u32[]{:S(2)}, u32[]{:S(2)}) collective-permute-start(bf16[768,5120]{1,0:T(8,128)(2,1)} %rest_0_.1), channel_id=1, source_target_pairs={{0,2},{1,3},{2,0},{3,1},{4,6},{5,7},{6,4},{7,5}} | collective-permute-start | bytes 23592968 | tf_op jit(solution)/shard_map/ppermute | solution.py:417
  4.0 172.4 %collective-permute-start.13 = (bf16[768,5120]{1,0:T(8,128)(2,1)}, bf16[768,5120]{1,0:T(8,128)(2,1)}, u32[]{:S(2)}, u32[]{:S(2)}) collective-permute-start(bf16[768,5120]{1,0:T(8,128)(2,1)} %rest_0_.1), channel_id=1, source_target_pairs={{0,4},{1,5},{2,6},{3,7},{4,0},{5,1},{6,2},{7,3}} | collective-permute-start | bytes 23592968 | tf_op jit(solution)/shard_map/ppermute | solution.py:417
  5.5 751.3 %collective-permute-start = (bf16[2560,3456]{1,0:T(8,128)(2,1)}, bf16[2560,3456]{1,0:T(8,128)(2,1)}, u32[]{:S(2)}, u32[]{:S(2)}) collective-permute-start(bf16[2560,3456]{1,0:T(8,128)(2,1)} %wg_ref.1), channel_id=1, source_target_pairs={{0,1},{1,0},{2,3},{3,2},{4,5},{5,4},{6,7},{7,6}} | collective-permute-start | bytes 53084168 | tf_op jit(solution)/shard_map/ppermute | solution.py:420
  5.5 751.8 %collective-permute-start.1 = (bf16[2560,3456]{1,0:T(8,128)(2,1)}, bf16[2560,3456]{1,0:T(8,128)(2,1)}, u32[]{:S(2)}, u32[]{:S(2)}) collective-permute-start(bf16[2560,3456]{1,0:T(8,128)(2,1)} %wu_ref.1), channel_id=1, source_target_pairs={{0,1},{1,0},{2,3},{3,2},{4,5},{5,4},{6,7},{7,6}} | collective-permute-start | bytes 53084168 | tf_op jit(solution)/shard_map/ppermute | solution.py:420
  6.0 333.9 %collective-permute-start.3 = (bf16[768,5120]{1,0:T(8,128)(2,1)}, bf16[768,5120]{1,0:T(8,128)(2,1)}, u32[]{:S(2)}, u32[]{:S(2)}) collective-permute-start(bf16[768,5120]{1,0:T(8,128)(2,1)} %rest_4_.1), channel_id=1, source_target_pairs={{0,2},{1,5},{2,0},{3,7},{4,6},{5,1},{6,4},{7,3}} | collective-permute-start | bytes 23592968 | tf_op jit(solution)/shard_map/ppermute | solution.py:417
  173.5 172.4 %collective-permute-start.4 = (bf16[768,5120]{1,0:T(8,128)(2,1)}, bf16[768,5120]{1,0:T(8,128)(2,1)}, u32[]{:S(2)}, u32[]{:S(2)}) collective-permute-start(bf16[768,5120]{1,0:T(8,128)(2,1)} %rest_4_.1), channel_id=1, source_target_pairs={{0,4},{1,3},{2,6},{3,1},{4,0},{5,7},{6,2},{7,5}} | collective-permute-start | bytes 23592968 | tf_op jit(solution)/shard_map/ppermute | solution.py:417
  181.4 436.1 %collective-permute-start.16 = (bf16[304,5120]{1,0:T(8,128)(2,1)}, bf16[304,5120]{1,0:T(8,128)(2,1)}, u32[]{:S(2)}, u32[]{:S(2)}) collective-permute-start(bf16[304,5120]{1,0:T(8,128)(2,1)} %slice.38), channel_id=1, source_target_pairs={{0,2},{1,5},{2,0},{3,7},{4,6},{5,1},{6,4},{7,3}} | collective-permute-start | bytes 9338888 | tf_op jit(solution)/shard_map/ppermute | solution.py:417
  339.9 416.9 %collective-permute-start.6 = (bf16[1792,2560]{1,0:T(8,128)(2,1)}, bf16[1792,2560]{1,0:T(8,128)(2,1)}, u32[]{:S(2)}, u32[]{:S(2)}) collective-permute-start(bf16[1792,2560]{1,0:T(8,128)(2,1)} %slice.27), channel_id=1, source_target_pairs={{0,2},{1,3},{2,0},{3,1},{4,6},{5,7},{6,4},{7,5}} | collective-permute-start | bytes 27525128 | tf_op jit(solution)/shard_map/ppermute | solution.py:417
  345.9 258.1 %collective-permute-start.17 = (bf16[8,2560]{1,0:T(8,128)(2,1)S(1)}, bf16[8,2560]{1,0:T(8,128)(2,1)S(1)}, u32[]{:S(2)}, u32[]{:S(2)}) collective-permute-start(bf16[8,2560]{1,0:T(8,128)(2,1)S(1)} %slice.39), channel_id=1, source_target_pairs={{0,2},{1,5},{2,0},{3,7},{4,6},{5,1},{6,4},{7,3}} | collective-permute-start | bytes 122888 | tf_op jit(solution)/shard_map/ppermute | solution.py:417
  604.0 9.5 collective-permute-start.18
  613.4 141.6 %collective-permute-start.7 = (bf16[1664,2560]{1,0:T(8,128)(2,1)}, bf16[1664,2560]{1,0:T(8,128)(2,1)}, u32[]{:S(2)}, u32[]{:S(2)}) collective-permute-start(bf16[1664,2560]{1,0:T(8,128)(2,1)} %slice.28), channel_id=1, source_target_pairs={{0,2},{1,3},{2,0},{3,1},{4,6},{5,7},{6,4},{7,5}} | collective-permute-start | bytes 25559048 | tf_op jit(solution)/shard_map/ppermute | solution.py:417
  617.5 53.6 %collective-permute-start.19 = (bf16[456,5120]{1,0:T(8,128)(2,1)S(1)}, bf16[456,5120]{1,0:T(8,128)(2,1)S(1)}, u32[]{:S(2)}, u32[]{:S(2)}) collective-permute-start(bf16[456,5120]{1,0:T(8,128)(2,1)S(1)} %slice.41), channel_id=1, source_target_pairs={{0,4},{1,5},{2,6},{3,7},{4,0},{5,1},{6,2},{7,3}} | collective-permute-start | bytes 14008328 | tf_op jit(solution)/shard_map/ppermute | solution.py:417
  671.2 294.7 %collective-permute-start.2 = (bf16[3456,2560]{1,0:T(8,128)(2,1)}, bf16[3456,2560]{1,0:T(8,128)(2,1)}, u32[]{:S(2)}, u32[]{:S(2)}) collective-permute-start(bf16[3456,2560]{1,0:T(8,128)(2,1)} %w_ref.1), channel_id=1, source_target_pairs={{0,1},{1,0},{2,3},{3,2},{4,5},{5,4},{6,7},{7,6}} | collective-permute-start | bytes 53084168 | tf_op jit(solution)/shard_map/ppermute | solution.py:420
  755.0 482.1 %collective-permute-start.10 = (bf16[768,5120]{1,0:T(8,128)(2,1)}, bf16[768,5120]{1,0:T(8,128)(2,1)}, u32[]{:S(2)}, u32[]{:S(2)}) collective-permute-start(bf16[768,5120]{1,0:T(8,128)(2,1)} %get-tuple-element.84.x_ref), channel_id=1, source_target_pairs={{0,4},{1,5},{2,6},{3,7},{4,0},{5,1},{6,2},{7,3}} | collective-permute-start | bytes 23592968 | tf_op jit(solution)/shard_map/ppermute | solution.py:417
  756.8 665.0 %collective-permute-start.9 = (bf16[1664,2560]{1,0:T(8,128)(2,1)}, bf16[1664,2560]{1,0:T(8,128)(2,1)}, u32[]{:S(2)}, u32[]{:S(2)}) collective-permute-start(bf16[1664,2560]{1,0:T(8,128)(2,1)} %collective-permute-done.7.rest_1_), channel_id=1, source_target_pairs={{0,1},{1,0},{2,3},{3,2},{4,5},{5,4},{6,7},{7,6}} | collective-permute-start | bytes 25559048 | tf_op jit(solution)/shard_map/ppermute | solution.py:420
  756.8 665.0 %collective-permute-start.8 = (bf16[1792,2560]{1,0:T(8,128)(2,1)}, bf16[1792,2560]{1,0:T(8,128)(2,1)}, u32[]{:S(2)}, u32[]{:S(2)}) collective-permute-start(bf16[1792,2560]{1,0:T(8,128)(2,1)} %collective-permute-done.6.rest_0_), channel_id=1, source_target_pairs={{0,1},{1,0},{2,3},{3,2},{4,5},{5,4},{6,7},{7,6}} | collective-permute-start | bytes 27525128 | tf_op jit(solution)/shard_map/ppermute | solution.py:420
  1418.3 416.6 %collective-permute-start.20 = (f32[768,5120]{1,0:T(8,128)}, f32[768,5120]{1,0:T(8,128)}, u32[]{:S(2)}, u32[]{:S(2)}) collective-permute-start(f32[768,5120]{1,0:T(8,128)} %shard_map.106), channel_id=1, source_target_pairs={{0,2},{1,5},{2,0},{3,7},{4,6},{5,1},{6,4},{7,3}} | collective-permute-start | bytes 47185928 | tf_op jit(solution)/shard_map/ppermute | solution.py:417
  1419.7 340.8 %collective-permute-start.11 = (bf16[768,3456]{1,0:T(8,128)(2,1)}, bf16[768,3456]{1,0:T(8,128)(2,1)}, u32[]{:S(2)}, u32[]{:S(2)}) collective-permute-start(bf16[768,3456]{1,0:T(8,128)(2,1)} %get-tuple-element.58), channel_id=1, source_target_pairs={{0,2},{1,3},{2,0},{3,1},{4,6},{5,7},{6,4},{7,5}} | collective-permute-start | bytes 15925256 | tf_op jit(solution)/shard_map/ppermute | solution.py:417
  1420.3 627.4 %collective-permute-start.15 = (f32[768,5120]{1,0:T(8,128)}, f32[768,5120]{1,0:T(8,128)}, u32[]{:S(2)}, u32[]{:S(2)}) collective-permute-start(f32[768,5120]{1,0:T(8,128)} %shard_map.102.refs_9_), channel_id=1, source_target_pairs={{0,2},{1,5},{2,0},{3,7},{4,6},{5,1},{6,4},{7,3}} | collective-permute-start | bytes 47185928 | tf_op jit(solution)/shard_map/ppermute | solution.py:417
  1421.8 932.1 %collective-permute-start.25 = (bf16[3072,5120]{1,0:T(8,128)(2,1)}, bf16[3072,5120]{1,0:T(8,128)(2,1)}, u32[]{:S(2)}, u32[]{:S(2)}) collective-permute-start(bf16[3072,5120]{1,0:T(8,128)(2,1)} %get-tuple-element.80.x_ref), channel_id=1, source_target_pairs={{0,1},{1,0},{2,3},{3,2},{4,5},{5,4},{6,7},{7,6}} | collective-permute-start | bytes 94371848 | tf_op jit(solution)/shard_map/ppermute | solution.py:420
  1832.1 330.1 %collective-permute-start.12 = (f32[768,5120]{1,0:T(8,128)}, f32[768,5120]{1,0:T(8,128)}, u32[]{:S(2)}, u32[]{:S(2)}) collective-permute-start(f32[768,5120]{1,0:T(8,128)} %shard_map.97), channel_id=1, source_target_pairs={{0,4},{1,5},{2,6},{3,7},{4,0},{5,1},{6,2},{7,3}} | collective-permute-start | bytes 47185928 | tf_op jit(solution)/shard_map/ppermute | solution.py:417
  1833.1 213.7 %collective-permute-start.5 = (bf16[768,3456]{1,0:T(8,128)(2,1)}, bf16[768,3456]{1,0:T(8,128)(2,1)}, u32[]{:S(2)}, u32[]{:S(2)}) collective-permute-start(bf16[768,3456]{1,0:T(8,128)(2,1)} %get-tuple-element.52), channel_id=1, source_target_pairs={{0,2},{1,3},{2,0},{3,1},{4,6},{5,7},{6,4},{7,5}} | collective-permute-start | bytes 15925256 | tf_op jit(solution)/shard_map/ppermute | solution.py:417
  1834.9 519.0 %collective-permute-start.27 = (bf16[3072,3456]{1,0:T(8,128)(2,1)}, bf16[3072,3456]{1,0:T(8,128)(2,1)}, u32[]{:S(2)}, u32[]{:S(2)}) collective-permute-start(bf16[3072,3456]{1,0:T(8,128)(2,1)} %get-tuple-element.75.db_ref.d_ref), channel_id=1, source_target_pairs={{0,1},{1,0},{2,3},{3,2},{4,5},{5,4},{6,7},{7,6}} | collective-permute-start | bytes 63701000 | tf_op jit(solution)/shard_map/ppermute | solution.py:420
  2046.8 59.2 %collective-permute-start.21 = (f32[48,5120]{1,0:T(8,128)}, f32[48,5120]{1,0:T(8,128)S(1)}, u32[]{:S(2)}, u32[]{:S(2)}) collective-permute-start(f32[48,5120]{1,0:T(8,128)} %get-tuple-element.76), channel_id=1, source_target_pairs={{0,4},{1,3},{2,6},{3,1},{4,0},{5,7},{6,2},{7,5}} | collective-permute-start | bytes 2949128 | tf_op jit(solution)/shard_map/ppermute | solution.py:417
  2047.7 114.5 %collective-permute-start.22 = (f32[256,5120]{1,0:T(8,128)}, f32[256,5120]{1,0:T(8,128)}, u32[]{:S(2)}, u32[]{:S(2)}) collective-permute-start(f32[256,5120]{1,0:T(8,128)} %get-tuple-element.77), channel_id=1, source_target_pairs={{0,4},{1,3},{2,6},{3,1},{4,0},{5,7},{6,2},{7,5}} | collective-permute-start | bytes 15728648 | tf_op jit(solution)/shard_map/ppermute | solution.py:417
  2106.0 74.2 %copy-start = (f32[48,5120]{1,0:T(8,128)}, f32[48,5120]{1,0:T(8,128)S(1)}, u32[]{:S(2)}) copy-start(f32[48,5120]{1,0:T(8,128)S(1)} %collective-permute-done.21.v_ref) | copy-start | bytes 2949124
  2106.0 154.6 %collective-permute-start.23 = (f32[448,5120]{1,0:T(8,128)}, f32[448,5120]{1,0:T(8,128)}, u32[]{:S(2)}, u32[]{:S(2)}) collective-permute-start(f32[448,5120]{1,0:T(8,128)} %get-tuple-element.78), channel_id=1, source_target_pairs={{0,4},{1,3},{2,6},{3,1},{4,0},{5,7},{6,2},{7,5}} | collective-permute-start | bytes 27525128 | tf_op jit(solution)/shard_map/ppermute | solution.py:417
  2162.2 98.3 %copy-start.1 = (f32[16,5120]{1,0:T(8,128)S(1)}, f32[16,5120]{1,0:T(8,128)}, u32[]{:S(2)}) copy-start(f32[16,5120]{1,0:T(8,128)} %get-tuple-element.79) | copy-start | bytes 983044
  2162.2 465.4 %collective-permute-start.29 = (bf16[3072,5120]{1,0:T(8,128)(2,1)}, bf16[3072,5120]{1,0:T(8,128)(2,1)}, u32[]{:S(2)}, u32[]{:S(2)}) collective-permute-start(bf16[3072,5120]{1,0:T(8,128)(2,1)} %get-tuple-element.82.d_ref), channel_id=1, source_target_pairs={{0,1},{1,0},{2,3},{3,2},{4,5},{5,4},{6,7},{7,6}} | collective-permute-start | bytes 94371848 | tf_op jit(solution)/shard_map/ppermute | solution.py:420
  2162.3 328.5 %collective-permute-start.26 = (bf16[3072,3456]{1,0:T(8,128)(2,1)}, bf16[3072,3456]{1,0:T(8,128)(2,1)}, u32[]{:S(2)}, u32[]{:S(2)}) collective-permute-start(bf16[3072,3456]{1,0:T(8,128)(2,1)} %get-tuple-element.74.da_ref.d_ref), channel_id=1, source_target_pairs={{0,1},{1,0},{2,3},{3,2},{4,5},{5,4},{6,7},{7,6}} | collective-permute-start | bytes 63701000 | tf_op jit(solution)/shard_map/ppermute | solution.py:420
  2260.6 91.6 %collective-permute-start.24 = (f32[16,5120]{1,0:T(8,128)S(1)}, f32[16,5120]{1,0:T(8,128)S(1)}, u32[]{:S(2)}, u32[]{:S(2)}) collective-permute-start(f32[16,5120]{1,0:T(8,128)S(1)} %copy-done.1), channel_id=1, source_target_pairs={{0,4},{1,3},{2,6},{3,1},{4,0},{5,7},{6,2},{7,5}} | collective-permute-start | bytes 983048 | tf_op jit(solution)/shard_map/ppermute | solution.py:417
  2352.2 275.5 %collective-permute-start.28 = (bf16[3072,3456]{1,0:T(8,128)(2,1)}, bf16[3072,3456]{1,0:T(8,128)(2,1)}, u32[]{:S(2)}, u32[]{:S(2)}) collective-permute-start(bf16[3072,3456]{1,0:T(8,128)(2,1)} %get-tuple-element.81.h_ref), channel_id=1, source_target_pairs={{0,1},{1,0},{2,3},{3,2},{4,5},{5,4},{6,7},{7,6}} | collective-permute-start | bytes 63701000 | tf_op jit(solution)/shard_map/ppermute | solution.py:420
